TPU v7x, 128 devices: a whole 4x4x4 slice. The times are simulated.
128 devices in a mesh: box: 4 (over z), leaf: 32 (over y, x, core).
Axes of the slice: x: 4, y: 4, z: 4, core: 2. Of those that a mesh axis runs over, the one named last changes fastest.
Arguments:
- probes: bfloat16 [64, 524288], P(None, ('box', 'leaf')), may hold values from -6 to 6
- near_index: int32 [8192, 8], P(('box', 'leaf')), may hold values from 0 to 8191, as said below
- far_index: int32 [8192, 8], P(('box', 'leaf')), may hold values from 0 to 8191, as said below
- inner_near: bfloat16 [8, 64, 524288], P(None, None, ('box', 'leaf')), may hold values from -0.25 to 0.25
- inner_basis: bfloat16 [64, 524288], P(None, ('box', 'leaf')), may hold values from -0.75 to 0.75
- inner_far: bfloat16 [8, 64, 524288], P(None, None, ('box', 'leaf')), may hold values from -0.25 to 0.25
- inner_transfer: bfloat16 [64, 524288], P(None, ('box', 'leaf')), may hold values from -0.09375 to 0.09375
- inner_tree: bfloat16 [2, 2, 64, 8192], P(None, None, None, ('box', 'leaf')), as said below
- inner_links: bfloat16 [3, 3, 64, 8192], P(None, None, None, ('box', 'leaf')), as said below
- outer_near: bfloat16 [8, 64, 524288], P(None, None, ('box', 'leaf')), may hold values from -0.25 to 0.25
- outer_basis: bfloat16 [64, 524288], P(None, ('box', 'leaf')), may hold values from -0.75 to 0.75
- outer_far: bfloat16 [8, 64, 524288], P(None, None, ('box', 'leaf')), may hold values from -0.25 to 0.25
- outer_transfer: bfloat16 [64, 524288], P(None, ('box', 'leaf')), may hold values from -0.09375 to 0.09375
- outer_tree: bfloat16 [2, 2, 64, 8192], P(None, None, None, ('box', 'leaf')), as said below
- outer_links: bfloat16 [3, 3, 64, 8192], P(None, None, None, ('box', 'leaf')), as said below
Outputs:
- pair_basis: float32 [64, 524288], P(None, ('box', 'leaf'))
- group_basis: float32 [64, 262144], P(None, ('box', 'leaf'))
Inputs may be any that keep to these rules, and one draw needn't show every extreme that they name: near_index[i, 0] = i; every other entry differs from i by 1 to 64. `far_index`: every entry differs from i by 1 to 64. inner_tree[c, j] holds equal blocks on all nodes of one cluster of level c + 1. inner_links[c, s] holds equal blocks on all nodes of one cluster of level c. outer_tree[c, j] holds equal blocks on all nodes of one cluster of level c + 1. outer_links[c, s] holds equal blocks on all nodes of one cluster of level c.
All inputs are finite; a program needn't handle non-finite values.
Results may differ from a plain program's by a relative error of at most 0.0078.
Values may be sent and summed in bfloat16 or wider, within the bound.
No kernel may reach another device: no remote copies, remote signals or barrier semaphores. Data moves between devices by JAX's collectives and lax.ppermute only.
A program may use at most 192 MiB of HBM per device.

v0:
```python
import jax
import jax.numpy as jnp
from jax import lax
from jax.sharding import PartitionSpec as P

CLEVELS = 3


highest = lax.Precision.HIGHEST


def partner_2(block, axis, stride):
    count = lax.axis_size(axis)
    route = []
    for low in range(count):
        high = low | 1 << stride
        if high != low and high < count:
            route += [(low, high), (high, low)]
    return lax.ppermute(block, axis, route)


def shifted(x, axis, by):
    devices = lax.axis_size(axis)
    pairs = [(i, i + by) for i in range(devices) if 0 <= i + by < devices]
    return lax.ppermute(x, axis, pairs)


def extended(x, sides, width):
    edges = {}
    for axis, dim in sides:
        devices, length = (lax.axis_size(axis), x.shape[dim])
        up = [(i, (i + 1) % devices) for i in range(devices - 1)]
        last = lax.slice_in_dim(x, length - width, length, axis=dim)
        initial = lax.slice_in_dim(x, 0, width, axis=dim)
        edges[dim] = (
            lax.ppermute(last, axis, up),
            lax.ppermute(initial, axis, [(b, a) for a, b in up]),
        )
    done = []
    for _, dim in sides:
        low, high = edges[dim]
        around = [(width, width) if d in done else (0, 0) for d in range(x.ndim)]
        x = jnp.concatenate([jnp.pad(low, around), x, jnp.pad(high, around)], axis=dim)
        done.append(dim)
    return x


def from_everyone(x, axis):
    devices = lax.axis_size(axis)
    return lax.all_to_all(jnp.broadcast_to(x[None], (devices, *x.shape)), axis, 0, 0, tiled=True)


def over_copies(x, axis):
    return from_everyone(x, axis).sum(axis=0)


def exact_product(matrix, factor):
    return jnp.dot(matrix, factor, precision=highest, preferred_element_type=jnp.float32)


def descend_chain(coupled, parities, tree_shard):
    descent = coupled[CLEVELS - 1]
    for height in range(CLEVELS - 2, -1, -1):
        tree = tree_shard[height].astype(jnp.float32)
        owned = jnp.where(parities[height], tree[0], tree[1])
        descent = coupled[height] + exact_product(descent, owned.T)
    return descent


def coarse_levels(node_coords, tree_shard, links_shard):
    leaf_place = lax.axis_index("leaf")
    current = node_coords
    parities = []
    coupled = []
    for height in range(CLEVELS):
        partner = partner_2(current, "leaf", height)
        is_even = jnp.right_shift(leaf_place, height) % 2 == 0
        low_coords = jnp.where(is_even, current, partner)
        high_coords = jnp.where(is_even, partner, current)
        reach = 2 ** (height + 1)
        left_low, left_high = shifted((low_coords, high_coords), ("box", "leaf"), reach)
        right_low, right_high = shifted((low_coords, high_coords), ("box", "leaf"), -reach)
        middle = jnp.where(is_even, right_low, left_high)
        links = links_shard[height].astype(jnp.float32)
        summed = exact_product(left_low, links[0])
        summed = summed + exact_product(middle, links[1])
        summed = summed + exact_product(right_high, links[2])
        coupled.append(summed)
        parities.append(is_even)
        if height + 1 < CLEVELS:
            tree = tree_shard[height].astype(jnp.float32)
            current = exact_product(low_coords, tree[0]) + exact_product(high_coords, tree[1])
    return descend_chain(coupled, parities, tree_shard)


def leaf_coords(samples, basis3):
    probe = samples.shape[0]
    leaves = basis3.shape[1]
    coords = jnp.einsum(
        "pim,kim->pik",
        samples.reshape(probe, leaves, basis3.shape[2]),
        basis3,
        preferred_element_type=jnp.float32,
    )
    return coords.astype(jnp.bfloat16).reshape(probe, leaves * basis3.shape[0])


def apply_matrix(
    samples,
    near_index,
    far_index,
    near_blocks,
    basis,
    far_blocks,
    transfer,
    tree_shard,
    links_shard,
):
    probe = samples.shape[0]
    leaves = near_index.shape[0]
    rank = basis.shape[0]
    leaf_size = basis.shape[1] // leaves
    basis3 = basis.reshape(rank, leaves, leaf_size)
    transfer3 = transfer.reshape(rank, leaves, rank)
    offset = (lax.axis_index(("box", "leaf")) - 1) * leaves
    padded_rows = extended(samples, ((("box", "leaf"), 1),), samples.shape[1])
    coords = leaf_coords(samples, basis3)
    padded_coords = extended(coords, ((("box", "leaf"), 1),), coords.shape[1])
    node_coords = jnp.einsum(
        "pik,kil->pl",
        coords.reshape(probe, leaves, rank),
        transfer3,
        preferred_element_type=jnp.float32,
    )
    descent = coarse_levels(node_coords, tree_shard, links_shard).astype(jnp.bfloat16)
    near_rows = jnp.take(
        padded_rows.reshape(probe, 3 * leaves, leaf_size), near_index - offset, axis=1
    )
    near_local = near_blocks.reshape(near_blocks.shape[0], leaf_size, leaves, leaf_size)
    near_part = jnp.einsum(
        "pisa,saib->pib", near_rows, near_local, preferred_element_type=jnp.float32
    )
    far_rows = jnp.take(padded_coords.reshape(probe, 3 * leaves, rank), far_index - offset, axis=1)
    far_local = far_blocks.reshape(far_blocks.shape[0], rank, leaves, rank)
    far_part = jnp.einsum("pisk,skil->pil", far_rows, far_local, preferred_element_type=jnp.float32)
    down_part = jnp.einsum("pl,kil->pik", descent, transfer3, preferred_element_type=jnp.float32)
    leaf_coeffs = (far_part + down_part).astype(jnp.bfloat16)
    result = near_part + jnp.einsum(
        "pik,kim->pim", leaf_coeffs, basis3, preferred_element_type=jnp.float32
    )
    return result.reshape(probe, leaves * leaf_size)


def local(
    probes,
    near_index,
    far_index,
    inner_near,
    inner_basis,
    inner_far,
    inner_transfer,
    inner_tree,
    inner_links,
    outer_near,
    outer_basis,
    outer_far,
    outer_transfer,
    outer_tree,
    outer_links,
):
    middle = apply_matrix(
        probes,
        near_index,
        far_index,
        inner_near,
        inner_basis,
        inner_far,
        inner_transfer,
        inner_tree,
        inner_links,
    ).astype(jnp.bfloat16)
    samples = apply_matrix(
        middle,
        near_index,
        far_index,
        outer_near,
        outer_basis,
        outer_far,
        outer_transfer,
        outer_tree,
        outer_links,
    )
    probe = samples.shape[0]
    pair_rows = 2 * (samples.shape[1] // near_index.shape[0])
    count = samples.shape[1] // pair_rows
    blocks = jnp.transpose(samples.reshape(probe, count, pair_rows), (1, 0, 2))
    gram = (
        jnp.einsum(
            "rpm,rqm->rpq", blocks, blocks, precision=highest, preferred_element_type=jnp.float32
        )
        / pair_rows
    )
    lower = jnp.linalg.cholesky(gram)
    local_gram = jnp.sum(gram, axis=0)
    group_gram = over_copies(local_gram, "leaf") / (count * lax.axis_size("leaf"))
    pair_q = jax.scipy.linalg.solve_triangular(lower, blocks, lower=True)
    group_lower = jnp.linalg.cholesky(group_gram)
    group_q = jax.scipy.linalg.solve_triangular(
        jnp.broadcast_to(group_lower, lower.shape), lower, lower=True
    )
    pair_basis = jnp.transpose(pair_q, (1, 0, 2)).reshape(probe, count * pair_rows)
    group_basis = jnp.transpose(group_q, (1, 0, 2)).reshape(probe, count * probe)
    return (pair_basis, group_basis)


def solution(mesh):
    return jax.shard_map(
        local,
        mesh=mesh,
        in_specs=(
            P(None, ("box", "leaf")),
            P(("box", "leaf"), None),
            P(("box", "leaf"), None),
            P(None, None, ("box", "leaf")),
            P(None, ("box", "leaf")),
            P(None, None, ("box", "leaf")),
            P(None, ("box", "leaf")),
            P(None, None, None, ("box", "leaf")),
            P(None, None, None, ("box", "leaf")),
            P(None, None, ("box", "leaf")),
            P(None, ("box", "leaf")),
            P(None, None, ("box", "leaf")),
            P(None, ("box", "leaf")),
            P(None, None, None, ("box", "leaf")),
            P(None, None, None, ("box", "leaf")),
        ),
        out_specs=(P(None, ("box", "leaf")), P(None, ("box", "leaf"))),
        check_vma=False,
    )
```

profile of v0, /device:TPU:0, one launch (start us, length us, event | category | flops | bytes accessed | tf_op | source)
XLA Modules:
  0.0 796.7 jit_solution(8775494422986557527)
XLA Ops:
  21.4 12.6 %reshape.182 = bf16[8,64,64,64]{3,2,1,0:T(8,128)(2,1)} reshape(bf16[8,64,4096]{2,1,0:T(8,128)(2,1)} %param.22) | data formatting | bytes 8388608 | tf_op jit(solution)/shard_map/reshape | solution.py:144
  34.1 12.7 %reshape.178 = bf16[8,64,64,64]{3,2,1,0:T(8,128)(2,1)} reshape(bf16[8,64,4096]{2,1,0:T(8,128)(2,1)} %param.20) | data formatting | bytes 8388608 | tf_op jit(solution)/shard_map/reshape | solution.py:139
  52.4 4.5 collective-permute-start.7
  69.4 5.4 collective-permute-start.12
  82.2 5.9 collective-permute-start.17
  96.2 6.5 collective-permute-start.15
  104.2 8.4 %collective-permute-start.10 = (f32[64,64]{1,0:T(8,128)S(1)}, f32[64,64]{1,0:T(8,128)S(1)}, u32[]{:S(2)}, u32[]{:S(2)}) collective-permute-start(f32[64,64]{1,0:T(8,128)S(1)} %get-tuple-element.21), channel_id=1, source_target_pairs={{0,4},{1,5},{2,6},{3,7},{4,8},{5,9},{6,10},{7,11},{8,12},{9,13},{1... | collective-permute-start | bytes 49160 | tf_op jit(solution)/shard_map/ppermute | solution.py:25
  128.1 13.5 %gather_fusion.1 = bf16[512,64,64]{1,2,0:T(8,128)(2,1)} fusion(bf16[64,192,64]{0,2,1:T(8,128)(2,1)S(1)} %pad_maximum_fusion, s32[1024]{0:T(1024)S(1)} %pad_clamp_fusion), kind=kCustom, calls=%fused_computation.1.clone | custom fusion | bytes 8390656 | tf_op jit(solution)/shard_map/jit(_take)/gather | solution.py:143
  141.6 12.0 %copy.139 = bf16[64,8,64,64]{3,2,1,0:T(8,128)(2,1)} copy(bf16[64,8,64,64]{2,3,1,0:T(8,128)(2,1)} %bitcast.231) | data formatting | bytes 8388608 | tf_op jit(solution)/shard_map/jit(_take)/gather | solution.py:143
  155.0 4.4 reshape.177
  163.3 13.7 %gather_fusion = bf16[512,64,64]{2,1,0:T(8,128)(2,1)} fusion(bf16[64,192,64]{2,0,1:T(8,128)(2,1)S(1)} %copy.129, s32[1024]{0:T(1024)S(1)} %pad_clamp_fusion.1), kind=kCustom, calls=%fused_computation.clone | custom fusion | bytes 8390656 | tf_op jit(solution)/shard_map/jit(_take)/gather | solution.py:136
  177.0 14.7 %fusion.46 = f32[64,64,64]{2,1,0:T(8,128)S(1)} fusion(f32[64,64,64]{1,0,2:T(8,128)} %fusion.83, bf16[8,64,64,64]{3,2,1,0:T(8,128)(2,1)} %reshape.182, bf16[64,8,64,64]{3,2,1,0:T(8,128)(2,1)} %copy.139, pred[64,8]{1,0:T(8,128)(4,1)S(1)} %copy.131, bf16[64,64,64]{2,1,0:T(8,128)(2,1)} %copy-done.5), kind=kOutput, calls=%fused_computation.45 | convolution fusion | flops 304611328 | bytes 11010560 | tf_op jit(solution)/shard_map/pik,kim->pim/dot_general | solution.py:148
  191.7 18.0 %fusion.55 = bf16[64,64,64]{2,0,1:T(8,128)(2,1)S(1)} fusion(f32[64,64,64]{2,1,0:T(8,128)S(1)} %fusion.46, bf16[8,64,64,64]{3,2,1,0:T(8,128)(2,1)} %reshape.178, bf16[64,8,64,64]{3,2,1,0:T(8,128)(2,1)} %bitcast.238, pred[64,8]{1,0:T(8,128)(4,1)S(1)} %copy.126), kind=kOutput, calls=%fused_computation.51 | convolution fusion | flops 271056896 | bytes 9961984 | tf_op jit(solution)/shard_map/pisa,saib->pib/dot_general | solution.py:140
  216.9 12.7 %reshape.188 = bf16[8,64,64,64]{3,2,1,0:T(8,128)(2,1)} reshape(bf16[8,64,4096]{2,1,0:T(8,128)(2,1)} %param.28) | data formatting | bytes 8388608 | tf_op jit(solution)/shard_map/reshape | solution.py:144
  229.7 12.6 %reshape.185 = bf16[8,64,64,64]{3,2,1,0:T(8,128)(2,1)} reshape(bf16[8,64,4096]{2,1,0:T(8,128)(2,1)} %param.26) | data formatting | bytes 8388608 | tf_op jit(solution)/shard_map/reshape | solution.py:139
  256.6 5.1 collective-permute-start.26
  272.0 6.6 collective-permute-start.33
  280.4 5.7 collective-permute-start.31
  293.5 6.0 collective-permute-start.36
  304.6 8.5 %collective-permute-done.37 = f32[64,64]{1,0:T(8,128)S(1)} collective-permute-done((f32[64,64]{1,0:T(8,128)S(1)}, f32[64,64]{1,0:T(8,128)S(1)}, u32[]{:S(2)}, u32[]{:S(2)}) %collective-permute-start.37) | collective-permute-done | bytes 16416 | tf_op jit(solution)/shard_map/ppermute | solution.py:25
  313.1 8.5 %collective-permute-start.34 = (f32[64,64]{1,0:T(8,128)S(1)}, f32[64,64]{1,0:T(8,128)S(1)}, u32[]{:S(2)}, u32[]{:S(2)}) collective-permute-start(f32[64,64]{1,0:T(8,128)S(1)} %get-tuple-element.11), channel_id=1, source_target_pairs={{0,8},{1,9},{2,10},{3,11},{4,12},{5,13},{6,14},{7,15},{8,16},{9,17... | collective-permute-start | bytes 49160 | tf_op jit(solution)/shard_map/ppermute | solution.py:25
  323.2 8.4 %collective-permute-start.29 = (f32[64,64]{1,0:T(8,128)S(1)}, f32[64,64]{1,0:T(8,128)S(1)}, u32[]{:S(2)}, u32[]{:S(2)}) collective-permute-start(f32[64,64]{1,0:T(8,128)S(1)} %get-tuple-element.13), channel_id=1, source_target_pairs={{0,4},{1,5},{2,6},{3,7},{4,8},{5,9},{6,10},{7,11},{8,12},{9,13},{1... | collective-permute-start | bytes 49160 | tf_op jit(solution)/shard_map/ppermute | solution.py:25
  349.8 13.5 %gather_fusion.3 = bf16[512,64,64]{2,1,0:T(8,128)(2,1)} fusion(bf16[64,192,64]{2,0,1:T(8,128)(2,1)S(1)} %pad_maximum_fusion.1, s32[1024]{0:T(1024)S(1)} %pad_clamp_fusion), kind=kCustom, calls=%fused_computation.3.clone | custom fusion | bytes 8390656 | tf_op jit(solution)/shard_map/jit(_take)/gather | solution.py:143
  364.8 4.4 reshape.184
  373.1 13.9 %gather_fusion.2 = bf16[512,64,64]{2,1,0:T(8,128)(2,1)} fusion(bf16[64,192,64]{2,0,1:T(8,128)(2,1)S(1)} %copy.147, s32[1024]{0:T(1024)S(1)} %pad_clamp_fusion.1), kind=kCustom, calls=%fused_computation.2.clone | custom fusion | bytes 8390656 | tf_op jit(solution)/shard_map/jit(_take)/gather | solution.py:136
  387.0 14.7 %fusion.51 = f32[64,64,64]{2,1,0:T(8,128)S(1)} fusion(f32[64,64,64]{1,0,2:T(8,128)} %fusion.78, bf16[8,64,64,64]{3,2,1,0:T(8,128)(2,1)} %reshape.188, bf16[64,8,64,64]{3,2,1,0:T(8,128)(2,1)} %bitcast.236, pred[64,8]{1,0:T(8,128)(4,1)S(1)} %copy.131, bf16[64,64,64]{2,1,0:T(8,128)(2,1)} %reshape.186), kind=kOutput, calls=%fused_computation.46 | convolution fusion | flops 304611328 | bytes 11010560 | tf_op jit(solution)/shard_map/pik,kim->pim/dot_general | solution.py:148
  401.7 13.7 %fusion.26 = f32[64,64,64]{2,0,1:T(8,128)S(1)} fusion(f32[64,64,64]{2,1,0:T(8,128)S(1)} %fusion.51, bf16[8,64,64,64]{3,2,1,0:T(8,128)(2,1)} %reshape.185, bf16[64,8,64,64]{3,2,1,0:T(8,128)(2,1)} %bitcast.237, pred[64,8]{1,0:T(8,128)(4,1)S(1)} %copy.126), kind=kOutput, calls=%fused_computation.35 | convolution fusion | flops 270794752 | bytes 10486272 | tf_op jit(solution)/shard_map/pisa,saib->pib/dot_general | solution.py:140
  421.4 189.1 %custom-call.15 = f32[32,64,64]{2,1,0:T(8,128)} custom-call(f32[32,64,64]{2,1,0:T(8,128)} %fusion.74), custom_call_target="Cholesky" | custom-call | tf_op jit(solution)/shard_map/jit(cholesky)/cholesky | solution.py:203
  617.1 15.8 %all-to-all-start = ((f32[32,1,4096]{2,1,0:T(1,128)}), f32[32,1,4096]{2,1,0:T(1,128)}, u32[]{:S(2)}, u32[]{:S(2)}) async-start(f32[32,1,4096]{2,1,0:T(1,128)} %reshape.256), calls=%async_computation | async-start | bytes 1048576 | tf_op jit(solution)/shard_map/all_to_all | solution.py:50
  635.8 67.2 %custom-call.16 = f32[32,1,64,64]{0,2,3,1:T(8,128)S(1)} custom-call(f32[32,1,64,64]{0,3,2,1:T(8,128)} %get-tuple-element.3), custom_call_target="InvertDiagBlocksLowerTriangular" | custom-call | tf_op jit(solution)/shard_map/jit(_solve_triangular)/vmap()/triangular_solve | solution.py:206
  714.6 5.8 cholesky.63
  723.0 67.4 %custom-call.17 = f32[32,1,64,64]{0,2,3,1:T(8,128)} custom-call(f32[32,1,64,64]{0,3,2,1:T(8,128)S(1)} %broadcast_select_fusion), custom_call_target="InvertDiagBlocksLowerTriangular" | custom-call | tf_op jit(solution)/shard_map/jit(_solve_triangular)/vmap()/triangular_solve | solution.py:208
  (198 shorter events, 182.9 us)
Async XLA Ops:
  7.3 113.8 %collective-permute-start.3 = (bf16[64,4096]{1,0:T(8,128)(2,1)}, bf16[64,4096]{1,0:T(8,128)(2,1)}, u32[]{:S(2)}, u32[]{:S(2)}) collective-permute-start(bf16[64,4096]{1,0:T(8,128)(2,1)} %copy.134), channel_id=1, source_target_pairs={{1,0},{2,1},{3,2},{4,3},{5,4},{6,5},{7,6},{8,7},{9,8},{10,9},{11,1... | collective-permute-start | bytes 1572872 | tf_op jit(solution)/shard_map/ppermute | solution.py:37
  8.6 114.9 %collective-permute-start.2 = (bf16[64,4096]{1,0:T(8,128)(2,1)}, bf16[64,4096]{1,0:T(8,128)(2,1)}, u32[]{:S(2)}, u32[]{:S(2)}) collective-permute-start(bf16[64,4096]{1,0:T(8,128)(2,1)} %copy.134), channel_id=1, source_target_pairs={{0,1},{1,2},{2,3},{3,4},{4,5},{5,6},{6,7},{7,8},{8,9},{9,10},{10,1... | collective-permute-start | bytes 1572872 | tf_op jit(solution)/shard_map/ppermute | solution.py:36
  12.5 141.1 %collective-permute-start.1 = (bf16[64,4096]{1,0:T(8,128)(2,1)}, bf16[64,4096]{1,0:T(8,128)(2,1)}, u32[]{:S(2)}, u32[]{:S(2)}) collective-permute-start(bf16[64,4096]{1,0:T(8,128)(2,1)} %param.17), channel_id=1, source_target_pairs={{1,0},{2,1},{3,2},{4,3},{5,4},{6,5},{7,6},{8,7},{9,8},{10,9},{11,1... | collective-permute-start | bytes 1572872 | tf_op jit(solution)/shard_map/ppermute | solution.py:37
  19.4 32.9 %collective-permute-start.9 = (f32[64,64]{1,0:T(8,128)S(1)}, f32[64,64]{1,0:T(8,128)S(1)}, u32[]{:S(2)}, u32[]{:S(2)}) collective-permute-start(f32[64,64]{1,0:T(8,128)S(1)} %convolution_add_fusion.8), channel_id=1, source_target_pairs={{0,2},{2,0},{1,3},{3,1},{4,6},{6,4},{5,7},{7,5},{8,10},{10,8},{9,1... | collective-permute-start | bytes 49160 | tf_op jit(solution)/shard_map/ppermute | solution.py:19
  51.1 6.2 collective-permute-start.6
  52.4 6.2 collective-permute-start.7
  58.6 16.3 %collective-permute-start.11 = (f32[64,64]{1,0:T(8,128)S(1)}, f32[64,64]{1,0:T(8,128)S(1)}, u32[]{:S(2)}, u32[]{:S(2)}) collective-permute-start(f32[64,64]{1,0:T(8,128)S(1)} %get-tuple-element.21), channel_id=1, source_target_pairs={{4,0},{5,1},{6,2},{7,3},{8,4},{9,5},{10,6},{11,7},{12,8},{13,9},{1... | collective-permute-start | bytes 49160 | tf_op jit(solution)/shard_map/ppermute | solution.py:25
  63.3 6.1 collective-permute-start.14
  69.4 7.0 collective-permute-start.12
  74.9 7.3 collective-permute-start.13
  76.4 11.8 %collective-permute-start.16 = (f32[64,64]{1,0:T(8,128)S(1)}, f32[64,64]{1,0:T(8,128)S(1)}, u32[]{:S(2)}, u32[]{:S(2)}) collective-permute-start(f32[64,64]{1,0:T(8,128)S(1)} %get-tuple-element.19), channel_id=1, source_target_pairs={{8,0},{9,1},{10,2},{11,3},{12,4},{13,5},{14,6},{15,7},{16,8},{17,9... | collective-permute-start | bytes 49160 | tf_op jit(solution)/shard_map/ppermute | solution.py:25
  82.2 8.2 %collective-permute-start.17 = (f32[64,64]{1,0:T(8,128)S(1)}, f32[64,64]{1,0:T(8,128)S(1)}, u32[]{:S(2)}, u32[]{:S(2)}) collective-permute-start(f32[64,64]{1,0:T(8,128)S(1)} %get-tuple-element.20), channel_id=1, source_target_pairs={{0,8},{1,9},{2,10},{3,11},{4,12},{5,13},{6,14},{7,15},{8,16},{9,17... | collective-permute-start | bytes 49160 | tf_op jit(solution)/shard_map/ppermute | solution.py:25
  88.2 65.3 %collective-permute-start = (bf16[64,4096]{1,0:T(8,128)(2,1)}, bf16[64,4096]{1,0:T(8,128)(2,1)}, u32[]{:S(2)}, u32[]{:S(2)}) collective-permute-start(bf16[64,4096]{1,0:T(8,128)(2,1)} %param.17), channel_id=1, source_target_pairs={{0,1},{1,2},{2,3},{3,4},{4,5},{5,6},{6,7},{7,8},{8,9},{9,10},{10,1... | collective-permute-start | bytes 1572872 | tf_op jit(solution)/shard_map/ppermute | solution.py:36
  96.2 8.1 %collective-permute-start.15 = (f32[64,64]{1,0:T(8,128)S(1)}, f32[64,64]{1,0:T(8,128)S(1)}, u32[]{:S(2)}, u32[]{:S(2)}) collective-permute-start(f32[64,64]{1,0:T(8,128)S(1)} %get-tuple-element.19), channel_id=1, source_target_pairs={{0,8},{1,9},{2,10},{3,11},{4,12},{5,13},{6,14},{7,15},{8,16},{9,17... | collective-permute-start | bytes 49160 | tf_op jit(solution)/shard_map/ppermute | solution.py:25
  104.2 10.0 %collective-permute-start.10 = (f32[64,64]{1,0:T(8,128)S(1)}, f32[64,64]{1,0:T(8,128)S(1)}, u32[]{:S(2)}, u32[]{:S(2)}) collective-permute-start(f32[64,64]{1,0:T(8,128)S(1)} %get-tuple-element.21), channel_id=1, source_target_pairs={{0,4},{1,5},{2,6},{3,7},{4,8},{5,9},{6,10},{7,11},{8,12},{9,13},{1... | collective-permute-start | bytes 49160 | tf_op jit(solution)/shard_map/ppermute | solution.py:25
  213.8 42.8 %collective-permute-start.28 = (f32[64,64]{1,0:T(8,128)S(1)}, f32[64,64]{1,0:T(8,128)S(1)}, u32[]{:S(2)}, u32[]{:S(2)}) collective-permute-start(f32[64,64]{1,0:T(8,128)S(1)} %convolution_add_fusion.3), channel_id=1, source_target_pairs={{0,2},{2,0},{1,3},{3,1},{4,6},{6,4},{5,7},{7,5},{8,10},{10,8},{9,1... | collective-permute-start | bytes 49160 | tf_op jit(solution)/shard_map/ppermute | solution.py:19
  246.6 94.6 %collective-permute-start.22 = (bf16[64,4096]{1,0:T(8,128)(2,1)}, bf16[64,4096]{1,0:T(8,128)(2,1)}, u32[]{:S(2)}, u32[]{:S(2)}) collective-permute-start(bf16[64,4096]{1,0:T(8,128)(2,1)} %reshape.187), channel_id=1, source_target_pairs={{1,0},{2,1},{3,2},{4,3},{5,4},{6,5},{7,6},{8,7},{9,8},{10,9},{11,1... | collective-permute-start | bytes 1572872 | tf_op jit(solution)/shard_map/ppermute | solution.py:37
  247.9 97.2 %collective-permute-start.21 = (bf16[64,4096]{1,0:T(8,128)(2,1)}, bf16[64,4096]{1,0:T(8,128)(2,1)}, u32[]{:S(2)}, u32[]{:S(2)}) collective-permute-start(bf16[64,4096]{1,0:T(8,128)(2,1)} %reshape.187), channel_id=1, source_target_pairs={{0,1},{1,2},{2,3},{3,4},{4,5},{5,6},{6,7},{7,8},{8,9},{9,10},{10,1... | collective-permute-start | bytes 1572872 | tf_op jit(solution)/shard_map/ppermute | solution.py:36
  254.0 109.3 %collective-permute-start.20 = (bf16[64,4096]{1,0:T(8,128)(2,1)}, bf16[64,4096]{1,0:T(8,128)(2,1)}, u32[]{:S(2)}, u32[]{:S(2)}) collective-permute-start(bf16[64,4096]{1,0:T(8,128)(2,1)} %convert_element_type.69), channel_id=1, source_target_pairs={{1,0},{2,1},{3,2},{4,3},{5,4},{6,5},{7,6},{8,7},{9,8},{10,9},{11,1... | collective-permute-start | bytes 1572872 | tf_op jit(solution)/shard_map/ppermute | solution.py:37
  255.3 10.6 %collective-permute-start.25 = (f32[64,64]{1,0:T(8,128)S(1)}, f32[64,64]{1,0:T(8,128)S(1)}, u32[]{:S(2)}, u32[]{:S(2)}) collective-permute-start(f32[64,64]{1,0:T(8,128)S(1)} %get-tuple-element.15), channel_id=1, source_target_pairs={{2,0},{3,1},{4,2},{5,3},{6,4},{7,5},{8,6},{9,7},{10,8},{11,9},{12,... | collective-permute-start | bytes 49160 | tf_op jit(solution)/shard_map/ppermute | solution.py:25
  256.6 10.6 %collective-permute-start.26 = (f32[64,64]{1,0:T(8,128)S(1)}, f32[64,64]{1,0:T(8,128)S(1)}, u32[]{:S(2)}, u32[]{:S(2)}) collective-permute-start(f32[64,64]{1,0:T(8,128)S(1)} %get-tuple-element.16), channel_id=1, source_target_pairs={{0,2},{1,3},{2,4},{3,5},{4,6},{5,7},{6,8},{7,9},{8,10},{9,11},{10,... | collective-permute-start | bytes 49160 | tf_op jit(solution)/shard_map/ppermute | solution.py:25
  267.3 18.9 %collective-permute-start.30 = (f32[64,64]{1,0:T(8,128)S(1)}, f32[64,64]{1,0:T(8,128)S(1)}, u32[]{:S(2)}, u32[]{:S(2)}) collective-permute-start(f32[64,64]{1,0:T(8,128)S(1)} %get-tuple-element.13), channel_id=1, source_target_pairs={{4,0},{5,1},{6,2},{7,3},{8,4},{9,5},{10,6},{11,7},{12,8},{13,9},{1... | collective-permute-start | bytes 49160 | tf_op jit(solution)/shard_map/ppermute | solution.py:25
  272.0 8.5 %collective-permute-start.33 = (f32[64,64]{1,0:T(8,128)S(1)}, f32[64,64]{1,0:T(8,128)S(1)}, u32[]{:S(2)}, u32[]{:S(2)}) collective-permute-start(f32[64,64]{1,0:T(8,128)S(1)} %convolution_add_fusion.1), channel_id=1, source_target_pairs={{0,4},{4,0},{1,5},{5,1},{2,6},{6,2},{3,7},{7,3},{8,12},{12,8},{9,1... | collective-permute-start | bytes 49160 | tf_op jit(solution)/shard_map/ppermute | solution.py:19
  280.4 7.3 collective-permute-start.31
  286.1 7.3 collective-permute-start.32
  287.7 12.6 %collective-permute-start.35 = (f32[64,64]{1,0:T(8,128)S(1)}, f32[64,64]{1,0:T(8,128)S(1)}, u32[]{:S(2)}, u32[]{:S(2)}) collective-permute-start(f32[64,64]{1,0:T(8,128)S(1)} %get-tuple-element.11), channel_id=1, source_target_pairs={{8,0},{9,1},{10,2},{11,3},{12,4},{13,5},{14,6},{15,7},{16,8},{17,9... | collective-permute-start | bytes 49160 | tf_op jit(solution)/shard_map/ppermute | solution.py:25
  293.5 8.9 %collective-permute-start.36 = (f32[64,64]{1,0:T(8,128)S(1)}, f32[64,64]{1,0:T(8,128)S(1)}, u32[]{:S(2)}, u32[]{:S(2)}) collective-permute-start(f32[64,64]{1,0:T(8,128)S(1)} %get-tuple-element.12), channel_id=1, source_target_pairs={{0,8},{1,9},{2,10},{3,11},{4,12},{5,13},{6,14},{7,15},{8,16},{9,17... | collective-permute-start | bytes 49160 | tf_op jit(solution)/shard_map/ppermute | solution.py:25
  300.3 63.1 %collective-permute-start.19 = (bf16[64,4096]{1,0:T(8,128)(2,1)}, bf16[64,4096]{1,0:T(8,128)(2,1)}, u32[]{:S(2)}, u32[]{:S(2)}) collective-permute-start(bf16[64,4096]{1,0:T(8,128)(2,1)} %convert_element_type.69), channel_id=1, source_target_pairs={{0,1},{1,2},{2,3},{3,4},{4,5},{5,6},{6,7},{7,8},{8,9},{9,10},{10,1... | collective-permute-start | bytes 1572872 | tf_op jit(solution)/shard_map/ppermute | solution.py:36
  302.4 10.7 %collective-permute-start.37 = (f32[64,64]{1,0:T(8,128)S(1)}, f32[64,64]{1,0:T(8,128)S(1)}, u32[]{:S(2)}, u32[]{:S(2)}) collective-permute-start(f32[64,64]{1,0:T(8,128)S(1)} %get-tuple-element.12), channel_id=1, source_target_pairs={{8,0},{9,1},{10,2},{11,3},{12,4},{13,5},{14,6},{15,7},{16,8},{17,9... | collective-permute-start | bytes 49160 | tf_op jit(solution)/shard_map/ppermute | solution.py:25
  313.1 10.1 %collective-permute-start.34 = (f32[64,64]{1,0:T(8,128)S(1)}, f32[64,64]{1,0:T(8,128)S(1)}, u32[]{:S(2)}, u32[]{:S(2)}) collective-permute-start(f32[64,64]{1,0:T(8,128)S(1)} %get-tuple-element.11), channel_id=1, source_target_pairs={{0,8},{1,9},{2,10},{3,11},{4,12},{5,13},{6,14},{7,15},{8,16},{9,17... | collective-permute-start | bytes 49160 | tf_op jit(solution)/shard_map/ppermute | solution.py:25
  323.2 10.0 %collective-permute-start.29 = (f32[64,64]{1,0:T(8,128)S(1)}, f32[64,64]{1,0:T(8,128)S(1)}, u32[]{:S(2)}, u32[]{:S(2)}) collective-permute-start(f32[64,64]{1,0:T(8,128)S(1)} %get-tuple-element.13), channel_id=1, source_target_pairs={{0,4},{1,5},{2,6},{3,7},{4,8},{5,9},{6,10},{7,11},{8,12},{9,13},{1... | collective-permute-start | bytes 49160 | tf_op jit(solution)/shard_map/ppermute | solution.py:25
  617.1 93.5 %all-to-all-start = ((f32[32,1,4096]{2,1,0:T(1,128)}), f32[32,1,4096]{2,1,0:T(1,128)}, u32[]{:S(2)}, u32[]{:S(2)}) async-start(f32[32,1,4096]{2,1,0:T(1,128)} %reshape.256), calls=%async_computation | async-start | bytes 1048576 | tf_op jit(solution)/shard_map/all_to_all | solution.py:50
  (20 other events, 198.8 us)
where the time goes:
time: 812 us; the launch traced here: 797 us
  other arithmetic  347 us (43%)
  local copies, waits for them, and re-layouts  182 us (22%)
  starting transfers between devices  136 us (17%)
  matrix products  89.2 us (11%)
  waiting for transfers between devices  41 us (5%)
    another operation x4, other arithmetic, local(): lower = jnp.linalg.cholesky(gram)  190 us
    ppermute x24, starting transfers between devices, shifted(): return lax.ppermute(x, axis, pairs)  85.8 us
    another operation x3, other arithmetic, local(): pair_q = jax.scipy.linalg.solve_triangular(lower, blocks, lower=True)  70.1 us
    another operation x2, other arithmetic, local(): jax.scipy.linalg.solve_triangular(jnp.broadcast_to(group_lower, lower.sha...  68.5 us
    gather x3, local copies, waits for them, and re-layouts, apply_matrix(): jnp.take(padded_coords.reshape(probe, 3 * leaves, rank), far_index - offs...  39 us
    ppermute x24, waiting for transfers between devices, shifted(): return lax.ppermute(x, axis, pairs)  36.6 us
    dot_general x2, matrix products, apply_matrix(): jnp.einsum('pisa,saib->pib', near_rows, near_local, preferred_element_typ...  31.7 us
    dot_general x2, matrix products, apply_matrix(): jnp.einsum('pik,kim->pim', leaf_coeffs, basis3, preferred_element_type=jn...  29.4 us
  transfers between devices with their start and end apart: 39, of which 19 were waited for; matrix products, arithmetic and copies ran while one was open for 27% of the time, Pallas kernels for 0%

commit v1 on v0

v1 whole, which is shorter than its diff:
```python
import jax
import jax.numpy as jnp
from jax import lax
from jax.experimental import pallas as pl
from jax.experimental.pallas import tpu as pltpu
from jax.sharding import PartitionSpec as P

AXES = ("box", "leaf")
LEAF = 64
TILE = 128
STEPS = 8
bf16 = jnp.bfloat16
f32 = jnp.float32
highest = lax.Precision.HIGHEST

NN = (((1,), (0,)), ((), ()))
NT = (((1,), (1,)), ((), ()))


def dot(a, b, dims=NN, precision=None):
    return lax.dot_general(a, b, dims, precision=precision, preferred_element_type=f32)


def low_half(shape):
    return lax.broadcasted_iota(jnp.int32, shape, len(shape) - 1) < LEAF


def two_blocks(tile):
    low = low_half(tile.shape)
    zero = jnp.zeros_like(tile)
    return jnp.concatenate([jnp.where(low, tile, zero), jnp.where(low, zero, tile)], axis=0)


def swap_halves(tile):
    return jnp.concatenate([tile[:, LEAF:], tile[:, :LEAF]], axis=1)


def twice(block):
    return jnp.concatenate([block, block], axis=1)


def lanes(t):
    return pl.ds(pl.multiple_of(t * TILE, TILE), TILE)


def coarse_payload(sums, tree_ref, scal_ref, pay_ref):
    folded = sums + swap_halves(sums)
    pay_ref[0] = folded.astype(bf16)
    up = dot(folded[:, :LEAF].astype(bf16), tree_ref[0, scal_ref[0]])
    pay_ref[1] = twice(up).astype(bf16)
    up = dot(up.astype(bf16), tree_ref[1, scal_ref[1]])
    pay_ref[2] = twice(up).astype(bf16)


def coords_kernel(scal_ref, rows_ref, basis_ref, transfer_ref, tree_ref, coords_ref, pay_ref):
    def step(g, sums):
        for u in range(4):
            at = lanes(g * 4 + u)
            coords = dot(rows_ref[:, at], two_blocks(basis_ref[:, at]), NT).astype(bf16)
            coords_ref[:, at] = coords
            sums = sums + dot(coords, two_blocks(transfer_ref[:, at]))
        return sums

    count = rows_ref.shape[1] // TILE
    sums = lax.fori_loop(0, count // 4, step, jnp.zeros((LEAF, TILE), f32))
    coarse_payload(sums, tree_ref, scal_ref, pay_ref)


def fill_store(store_ref, sources):
    tiles = sources[0].shape[1] // TILE
    half = store_ref.shape[0] // 2
    for n, source in enumerate(sources):

        def step(g, carry, n=n, source=source):
            for u in range(4):
                t = g * 4 + u
                tile = source[:, lanes(t)]
                store_ref[n * tiles + t] = tile
                store_ref[half + n * tiles + t] = swap_halves(tile)
            return carry

        lax.fori_loop(0, tiles // 4, step, 0)


def gathered(store_ref, index_ref, pair, low):
    rows = []
    for h in range(2):
        base = (2 * pair + h) * 8
        cols = []
        for k in range(4):
            first = store_ref[index_ref[base + 2 * k]]
            second = store_ref[index_ref[base + 2 * k + 1]]
            cols.append(jnp.where(low, first, second))
        rows.append(jnp.concatenate(cols, axis=1))
    return jnp.concatenate(rows, axis=0)


def descend(scal_ref, mine_ref, other_ref, first_ref, second_ref, tree_ref, links_ref):
    b0, b1, b2 = scal_ref[0], scal_ref[1], scal_ref[2]
    odd, has_left, has_right = scal_ref[3], scal_ref[4], scal_ref[5]

    def low_group(n):
        return jnp.where(b2 == 0, mine_ref[n], other_ref[n])

    def high_group(n):
        return jnp.where(b2 == 0, other_ref[n], mine_ref[n])

    def left(n):
        tile = jnp.where(odd == 1, first_ref[n], second_ref[n])
        return jnp.where(has_left == 1, tile, jnp.zeros_like(tile))

    def right(n):
        tile = jnp.where(odd == 1, second_ref[n], first_ref[n])
        return jnp.where(has_right == 1, tile, jnp.zeros_like(tile))

    def pick(j, options):
        tile = options[-1]
        for n in range(len(options) - 2, -1, -1):
            tile = jnp.where(j == n, options[n], tile)
        return tile

    ext0 = [left(2), low_group(0), low_group(1), high_group(0), high_group(1), right(2)]
    ext1 = [left(1), low_group(2), high_group(2), right(1)]
    j0, j1 = b2 * 2 + b1, b2
    around = [
        (pick(j0, ext0[:4]), pick(j0, ext0[2:])),
        (pick(j1, ext1[:2]), pick(j1, ext1[2:])),
        (left(0), right(0)),
    ]
    coupled = []
    for c, parity in enumerate((b0, b1, b2)):
        mid = links_ref[c, 1]
        none = jnp.zeros_like(mid)
        lo = jnp.concatenate([links_ref[c, 0], jnp.where(parity == 1, mid, none)], axis=0)
        hi = jnp.concatenate([jnp.where(parity == 0, mid, none), links_ref[c, 2]], axis=0)
        coupled.append(dot(around[c][0], lo) + dot(around[c][1], hi))
    h = coupled[1] + dot(coupled[2].astype(bf16), tree_ref[1, b1], NT)
    h = coupled[0] + dot(h.astype(bf16), tree_ref[0, b0], NT)
    return twice(h).astype(bf16)


def apply_tile(u, pair, low, refs):
    near_index, far_index, near_ref, far_ref, basis_ref, transfer_ref, rows_store, coords_store, descent = refs
    at = slice(u * TILE, (u + 1) * TILE)
    near = near_ref[:, :, at].reshape(8 * LEAF, TILE)
    far = far_ref[:, :, at].reshape(8 * LEAF, TILE)
    low32 = low_half((LEAF, TILE))
    near_all = dot(gathered(rows_store, near_index, pair, low), near)
    far_all = dot(gathered(coords_store, far_index, pair, low), far)
    near_part = jnp.where(low32, near_all[:LEAF], near_all[LEAF:])
    far_part = jnp.where(low32, far_all[:LEAF], far_all[LEAF:])
    down = dot(descent, two_blocks(transfer_ref[:, at]), NT)
    coeffs = (far_part + down).astype(bf16)
    return near_part + dot(coeffs, two_blocks(basis_ref[:, at]))


def prepare(step, scal_ref, rows_refs, coords_refs, coarse_refs, tree_ref, links_ref, rows_store, coords_store, descent_ref):
    @pl.when(step == 0)
    def _():
        fill_store(rows_store, rows_refs)
        fill_store(coords_store, coords_refs)
        descent_ref[...] = descend(scal_ref, *coarse_refs, tree_ref, links_ref)


def inner_kernel(
    scal_ref, near_index, far_index,
    rows_b, rows_own, rows_a, coords_b, coords_own, coords_a,
    mine_ref, other_ref, first_ref, second_ref, tree_ref, links_ref, next_tree_ref,
    near_ref, far_ref, basis_ref, transfer_ref, next_basis_ref, next_transfer_ref,
    middle_ref, next_coords_ref, pay_ref,
    rows_store, coords_store, descent_ref, sums_ref,
):
    step = pl.program_id(0)
    prepare(
        step, scal_ref, (rows_b, rows_own, rows_a), (coords_b, coords_own, coords_a),
        (mine_ref, other_ref, first_ref, second_ref), tree_ref, links_ref,
        rows_store, coords_store, descent_ref,
    )

    @pl.when(step == 0)
    def _():
        sums_ref[...] = jnp.zeros_like(sums_ref)

    low = low_half((LEAF, TILE))
    refs = (near_index, far_index, near_ref, far_ref, basis_ref, transfer_ref, rows_store, coords_store, descent_ref[...])
    per = near_ref.shape[2] // TILE
    sums = sums_ref[...]
    for u in range(per):
        at = slice(u * TILE, (u + 1) * TILE)
        middle = apply_tile(u, step * per + u, low, refs).astype(bf16)
        middle_ref[:, at] = middle
        coords = dot(middle, two_blocks(next_basis_ref[:, at]), NT).astype(bf16)
        next_coords_ref[:, at] = coords
        sums = sums + dot(coords, two_blocks(next_transfer_ref[:, at]))
    sums_ref[...] = sums

    @pl.when(step == pl.num_programs(0) - 1)
    def _():
        coarse_payload(sums, next_tree_ref, scal_ref, pay_ref)


def outer_kernel(
    scal_ref, near_index, far_index,
    rows_b, rows_own, rows_a, coords_b, coords_own, coords_a,
    mine_ref, other_ref, first_ref, second_ref, tree_ref, links_ref,
    near_ref, far_ref, basis_ref, transfer_ref,
    samples_ref, gram_ref,
    rows_store, coords_store, descent_ref,
):
    step = pl.program_id(0)
    prepare(
        step, scal_ref, (rows_b, rows_own, rows_a), (coords_b, coords_own, coords_a),
        (mine_ref, other_ref, first_ref, second_ref), tree_ref, links_ref,
        rows_store, coords_store, descent_ref,
    )

    @pl.when(step == 0)
    def _():
        gram_ref[...] = jnp.zeros_like(gram_ref)

    low = low_half((LEAF, TILE))
    refs = (near_index, far_index, near_ref, far_ref, basis_ref, transfer_ref, rows_store, coords_store, descent_ref[...])
    per = near_ref.shape[2] // TILE
    gram = gram_ref[...]
    for u in range(per):
        out = apply_tile(u, step * per + u, low, refs)
        samples_ref[:, u * TILE : (u + 1) * TILE] = out
        gram = gram + dot(out, out, NT, highest)
    gram_ref[...] = gram


def eliminate(work_ref):
    count = work_ref.shape[0]
    sub = lax.broadcasted_iota(jnp.int32, (count, 8, TILE), 1)
    for kb in range(LEAF // 8):
        panel = work_ref[:, kb * 8 : kb * 8 + 8, :]
        scaled = []
        for j in range(8):
            k = kb * 8 + j
            inv = lax.rsqrt(panel[:, j : j + 1, k : k + 1])
            row = panel[:, j : j + 1, :] * inv
            again = row * inv
            scaled.append(again)
            factor = jnp.where(sub > j, jnp.broadcast_to(panel[:, :, k : k + 1], sub.shape), 0.0)
            panel = jnp.where(sub == j, row, panel - factor * again)
        work_ref[:, kb * 8 : kb * 8 + 8, :] = panel
        for ib in range(kb + 1, LEAF // 8):
            rest = work_ref[:, ib * 8 : ib * 8 + 8, :]
            for j in range(8):
                k = kb * 8 + j
                rest = rest - rest[:, :, k : k + 1] * scaled[j]
            work_ref[:, ib * 8 : ib * 8 + 8, :] = rest


def identity_half():
    row = lax.broadcasted_iota(jnp.int32, (LEAF, LEAF), 0)
    col = lax.broadcasted_iota(jnp.int32, (LEAF, LEAF), 1)
    return jnp.where(row == col, 1.0, 0.0).astype(f32)


def pair_kernel(samples_ref, basis_ref, work_ref):
    count = samples_ref.shape[1] // TILE
    eye = identity_half()

    def gram_step(g, carry):
        for u in range(4):
            t = g * 4 + u
            tile = samples_ref[:, lanes(t)]
            work_ref[t] = jnp.concatenate([dot(tile, tile, NT, highest) / TILE, eye], axis=1)
        return carry

    lax.fori_loop(0, count // 4, gram_step, 0)
    eliminate(work_ref)

    def solve_step(g, carry):
        for u in range(4):
            t = g * 4 + u
            basis_ref[:, lanes(t)] = dot(work_ref[t][:, LEAF:], samples_ref[:, lanes(t)], NN, highest)
        return carry

    lax.fori_loop(0, count // 4, solve_step, 0)


def group_kernel(gram_ref, work_ref, out_ref, own_ref, *, scale):
    count = work_ref.shape[0]
    own_ref[0] = jnp.concatenate([gram_ref[...] / scale, identity_half()], axis=1)
    eliminate(own_ref)
    inverse = own_ref[0][:, LEAF:]
    row = lax.broadcasted_iota(jnp.int32, (LEAF, LEAF), 0)
    col = lax.broadcasted_iota(jnp.int32, (LEAF, LEAF), 1)
    upper = row <= col

    def step(g, carry):
        for u in range(4):
            t = g * 4 + u
            first = jnp.where(upper, work_ref[2 * t][:, :LEAF], 0.0)
            second = jnp.where(upper, work_ref[2 * t + 1][:, :LEAF], 0.0)
            out_ref[:, lanes(t)] = dot(inverse, jnp.concatenate([first, second], axis=0), NT, highest)
        return carry

    lax.fori_loop(0, count // 8, step, 0)


VMEM = pl.BlockSpec(memory_space=pltpu.VMEM)
SMEM = pl.BlockSpec(memory_space=pltpu.SMEM)


def params(mib):
    return pltpu.CompilerParams(vmem_limit_bytes=mib * 2**20)


def struct(shape, dtype):
    return jax.ShapeDtypeStruct(shape, dtype)


def swap(x, mask):
    count = lax.axis_size(AXES)
    return lax.ppermute(x, AXES, [(i, i ^ mask) for i in range(count)])


def neighbours(x, width, second):
    count = lax.axis_size(AXES)
    blocks = count // width
    route = []
    for b in range(blocks):
        forward = (b % 2 == 0) != second
        to = (b + 1 if forward else b - 1) % blocks
        route += [(b * width + m, to * width + m) for m in range(width)]
    return lax.ppermute(x, AXES, route)


def node_halo(x):
    count = lax.axis_size(AXES)
    route = [(i, (i - 1 if i % 2 == 0 else i + 1) % count) for i in range(count)]
    return lax.ppermute(x, AXES, route), swap(x, 1)


def leaf_table(index, node):
    leaves = index.shape[0]
    place = index - (node - 1) * leaves
    block = place // leaves
    block = jnp.where(node % 2 == 1, 2 - block, block)
    place = block * leaves + place % leaves
    slot = lax.broadcasted_iota(jnp.int32, index.shape, 1)
    return (((place + slot) % 2) * (3 * leaves // 2) + place // 2).reshape(-1)


def coarse_exchange(pay, node):
    low = low_half((LEAF, TILE))
    b0, b1, b2 = node % 2, node // 2 % 2, node // 4 % 2
    odd = node // 8 % 2

    def halves(bit, mine, other):
        return jnp.where(low == (bit == 0), mine, other)

    other = swap(pay, 1)
    z0 = halves(b0, pay[0], other[0])
    stage = jnp.stack([z0, pay[1] + other[1], pay[2] + other[2]])
    other = swap(stage, 2)
    first = jnp.where(b1 == 0, stage[0], other[0])
    second = jnp.where(b1 == 0, other[0], stage[0])
    mine = jnp.stack([first, second, halves(b1, stage[1], other[1]), stage[2] + other[2]])
    other = swap(mine, 6)
    top = halves(b2, mine[3], other[3])
    lo = jnp.where(b2 == 0, mine, other)
    hi = jnp.where(b2 == 0, other, mine)
    rightward = jnp.stack([top, hi[2], hi[1]])
    leftward = jnp.stack([top, lo[2], lo[0]])
    one = neighbours(jnp.where(odd == 0, rightward, leftward), 8, False)
    two = neighbours(jnp.where(odd == 0, leftward, rightward), 8, True)
    return mine, other, one, two


def local(
    probes,
    near_index,
    far_index,
    inner_near,
    inner_basis,
    inner_far,
    inner_transfer,
    inner_tree,
    inner_links,
    outer_near,
    outer_basis,
    outer_far,
    outer_transfer,
    outer_tree,
    outer_links,
):
    node = lax.axis_index(AXES)
    count = lax.axis_size(AXES)
    width = probes.shape[1]
    block = node // 8
    scal = jnp.stack(
        [
            node % 2,
            node // 2 % 2,
            node // 4 % 2,
            block % 2,
            (block > 0).astype(jnp.int32),
            (block < count // 8 - 1).astype(jnp.int32),
        ]
    ).astype(jnp.int32)
    near_table = leaf_table(near_index, node)
    far_table = leaf_table(far_index, node)

    rows_b, rows_a = node_halo(probes)
    coords, pay = pl.pallas_call(
        coords_kernel,
        in_specs=[SMEM, VMEM, VMEM, VMEM, VMEM],
        out_specs=(VMEM, VMEM),
        out_shape=(struct((LEAF, width), bf16), struct((3, LEAF, TILE), bf16)),
        compiler_params=params(16),
        name="coords",
    )(scal, probes, inner_basis, inner_transfer, inner_tree)
    coords_b, coords_a = node_halo(coords)
    coarse = coarse_exchange(pay, node)

    wide = width // STEPS
    big = pl.BlockSpec((8, LEAF, wide), lambda i: (0, 0, i))
    flat = pl.BlockSpec((LEAF, wide), lambda i: (0, i))
    stores = [
        pltpu.VMEM((3 * width // LEAF, LEAF, TILE), bf16),
        pltpu.VMEM((3 * width // LEAF, LEAF, TILE), bf16),
        pltpu.VMEM((LEAF, TILE), bf16),
    ]
    middle, next_coords, pay = pl.pallas_call(
        inner_kernel,
        grid=(STEPS,),
        in_specs=[SMEM] * 3 + [VMEM] * 13 + [big, big, flat, flat, flat, flat],
        out_specs=(flat, flat, VMEM),
        out_shape=(struct((LEAF, width), bf16), struct((LEAF, width), bf16), struct((3, LEAF, TILE), bf16)),
        scratch_shapes=stores + [pltpu.VMEM((LEAF, TILE), f32)],
        compiler_params=params(32),
        name="inner",
    )(
        scal, near_table, far_table,
        rows_b, probes, rows_a, coords_b, coords, coords_a,
        *coarse, inner_tree, inner_links, outer_tree,
        inner_near, inner_far, inner_basis, inner_transfer, outer_basis, outer_transfer,
    )
    rows_b, rows_a = node_halo(middle)
    coords_b, coords_a = node_halo(next_coords)
    coarse = coarse_exchange(pay, node)
    samples, gram = pl.pallas_call(
        outer_kernel,
        grid=(STEPS,),
        in_specs=[SMEM] * 3 + [VMEM] * 12 + [big, big, flat, flat],
        out_specs=(flat, VMEM),
        out_shape=(struct((LEAF, width), f32), struct((LEAF, LEAF), f32)),
        scratch_shapes=stores,
        compiler_params=params(32),
        name="outer",
    )(
        scal, near_table, far_table,
        rows_b, middle, rows_a, coords_b, next_coords, coords_a,
        *coarse, outer_tree, outer_links,
        outer_near, outer_far, outer_basis, outer_transfer,
    )
    for mask in (1, 2, 6, 8, 24):
        gram = gram + swap(gram, mask)
    pairs = width // TILE
    pair_basis, work = pl.pallas_call(
        pair_kernel,
        in_specs=[VMEM],
        out_specs=(VMEM, VMEM),
        out_shape=(struct((LEAF, width), f32), struct((pairs, LEAF, TILE), f32)),
        compiler_params=params(32),
        name="pairs",
    )(samples)
    scale = TILE * pairs * lax.axis_size("leaf")
    group_basis = pl.pallas_call(
        lambda *refs: group_kernel(*refs, scale=scale),
        in_specs=[VMEM, VMEM],
        out_specs=VMEM,
        out_shape=struct((LEAF, pairs * LEAF), f32),
        scratch_shapes=[pltpu.VMEM((1, LEAF, TILE), f32)],
        compiler_params=params(32),
        name="group",
    )(gram, work)
    return (pair_basis, group_basis)


def solution(mesh):
    flat = P(None, AXES)
    index = P(AXES, None)
    blocks = P(None, None, AXES)
    tree = P(None, None, None, AXES)
    factor = (blocks, flat, blocks, flat, tree, tree)
    return jax.shard_map(
        local,
        mesh=mesh,
        in_specs=(flat, index, index) + factor + factor,
        out_specs=(flat, flat),
        check_vma=False,
    )
```

time: 812 us -> 183 us (0.23); the launches traced: 797 us -> 183 us
  other arithmetic: 347 us -> 0.93 us
  local copies, waits for them, and re-layouts: 182 us -> 16.6 us
  starting transfers between devices: 136 us -> 20 us
  matrix products: 89.2 us -> 0 us
  Pallas kernels: 0 us -> 84.1 us
  waiting for transfers between devices: 41 us -> 60 us
    another operation x12 -> x4, other arithmetic: 335 us -> 0.04 us  [the longest x2 0.03 us: coarse_exchange(): jnp.stack([first, second, halves(b1, stage[1], other[1]), stage[2] + othe...]
    ppermute x38 -> x23, starting transfers between devices: 120 us -> 20 us  [the longest x4 17.1 us: node_halo(): return (lax.ppermute(x, AXES, route), swap(x, 1))]
    dot_general x41 -> x0, matrix products: 84.9 us -> none  [the longest x2 31.7 us: apply_matrix(): jnp.einsum('pisa,saib->pib', near_rows, near_local, preferred_element_typ...]
    pallas_call x0 -> x5, Pallas kernels: none -> 84.1 us  [the longest x1 28.4 us: local(): pl.pallas_call(pair_kernel, in_specs=[VMEM], out_specs=(VMEM, VMEM), out_...]
    reshape x17 -> x2, local copies, waits for them, and re-layouts: 83.5 us -> 0.18 us  [leaf_table(): return ((place + slot) % 2 * (3 * leaves // 2) + place // 2).reshape(-1)]
    gather x5 -> x0, local copies, waits for them, and re-layouts: 66.5 us -> none  [the longest x3 39 us: apply_matrix(): jnp.take(padded_coords.reshape(probe, 3 * leaves, rank), far_index - offs...]
    ppermute x38 -> x23, waiting for transfers between devices: 41 us -> 60 us  [the longest x15 33 us: swap(): return lax.ppermute(x, AXES, [(i, i ^ mask) for i in range(count)])]
    all_to_all x1 -> x0, starting transfers between devices: 15.8 us -> none  [from_everyone(): lax.all_to_all(jnp.broadcast_to(x[None], (devices, *x.shape)), axis, 0, 0...]
  transfers between devices with their start and end apart: 39 -> 23, of which waited for: 19 -> 13; matrix products, arithmetic and copies ran while one was open for 27% -> 1% of each run, Pallas kernels for 0% -> 18%
where the time goes in v1:
time: 183 us
  Pallas kernels  84.1 us (46%)
  waiting for transfers between devices  60 us (33%)
  starting transfers between devices  20 us (11%)
  local copies, waits for them, and re-layouts  16.6 us (9%)
    ppermute x15, waiting for transfers between devices, swap(): return lax.ppermute(x, AXES, [(i, i ^ mask) for i in range(count)])  33 us
    pallas_call x1, Pallas kernels, local(): pl.pallas_call(pair_kernel, in_specs=[VMEM], out_specs=(VMEM, VMEM), out_...  28.4 us
    ppermute x4, waiting for transfers between devices, neighbours(): return lax.ppermute(x, AXES, route)  27.1 us
    pallas_call x1, Pallas kernels, local(): pl.pallas_call(inner_kernel, grid=(STEPS,), in_specs=[SMEM] * 3 + [VMEM]...  22.1 us
    pallas_call x1, Pallas kernels, local(): pl.pallas_call(outer_kernel, grid=(STEPS,), in_specs=[SMEM] * 3 + [VMEM]...  20 us
    ppermute x4, starting transfers between devices, node_halo(): return (lax.ppermute(x, AXES, route), swap(x, 1))  17.1 us
    unnamed x38, local copies, waits for them, and re-layouts  16.2 us
    pallas_call x1, Pallas kernels, local(): pl.pallas_call(lambda *refs: group_kernel(*refs, scale=scale), in_specs=[...  9.01 us
  transfers between devices with their start and end apart: 23, of which 13 were waited for; matrix products, arithmetic and copies ran while one was open for 1% of the time, Pallas kernels for 18%

profile of v1, /device:TPU:0, one launch (start us, length us, event | category | flops | bytes accessed | tf_op | source)
XLA Modules:
  0.0 182.6 jit_solution(14116575684595815201)
XLA Ops:
  0.7 8.9 %collective-permute-start = (bf16[64,4096]{1,0:T(8,128)(2,1)}, bf16[64,4096]{1,0:T(8,128)(2,1)S(1)}, u32[]{:S(2)}, u32[]{:S(2)}) collective-permute-start(bf16[64,4096]{1,0:T(8,128)(2,1)} %rows_own.1), channel_id=1, source_target_pairs={{0,127},{1,2},{2,1},{3,4},{4,3},{5,6},{6,5},{7,8},{8,7},{9,10},{10... | collective-permute-start | bytes 1572872 | tf_op jit(solution)/shard_map/ppermute | solution.py:335
  9.7 1.0 copy-done.8
  10.7 1.0 copy-done.10
  11.8 1.0 copy-done.12
  13.7 4.6 %coords.1 = (bf16[64,4096]{1,0:T(8,128)(2,1)S(1)}, bf16[3,64,128]{2,1,0:T(8,128)(2,1)S(1)}) custom-call(s32[6]{0:T(128)S(1)} %stack.77.scal_ref, bf16[64,4096]{1,0:T(8,128)(2,1)S(1)} %copy-done.8, bf16[64,4096]{1,0:T(8,128)(2,1)S(1)} %copy-done.10, bf16[64,4096]{1,0:T(8,128)(2,1)S(1)} %copy-done.12, bf16[2,2,64,64]{3,2,1,0:T(8,128)(2,1)S(1)} %copy-done.15), custom_call_target="tpu_custom_call" | custom-call | tf_op jit(solution)/shard_map/coords/pallas_call | solution.py:409
  19.3 1.2 collective-permute-done.4
  20.5 1.3 collective-permute-start.5
  21.8 6.9 %collective-permute-done.5 = bf16[3,64,128]{2,1,0:T(8,128)(2,1)S(1)} collective-permute-done((bf16[3,64,128]{2,1,0:T(8,128)(2,1)S(1)}, bf16[3,64,128]{2,1,0:T(8,128)(2,1)S(1)}, u32[]{:S(2)}, u32[]{:S(2)}) %collective-permute-start.5) | collective-permute-done | bytes 49184 | tf_op jit(solution)/shard_map/ppermute | solution.py:318
  28.8 5.4 %collective-permute-done.6.other_ref = bf16[4,64,128]{2,1,0:T(8,128)(2,1)S(1)} collective-permute-done((bf16[4,64,128]{2,1,0:T(8,128)(2,1)S(1)}, bf16[4,64,128]{2,1,0:T(8,128)(2,1)S(1)}, u32[]{:S(2)}, u32[]{:S(2)}) %collective-permute-start.6) | collective-permute-done | bytes 65568 | tf_op jit(solution)/shard_map/ppermute | solution.py:318
  35.2 6.7 %collective-permute-done.8.second_ref = bf16[3,64,128]{2,1,0:T(8,128)(2,1)S(1)} collective-permute-done((bf16[3,64,128]{2,1,0:T(8,128)(2,1)S(1)}, bf16[3,64,128]{2,1,0:T(8,128)(2,1)S(1)}, u32[]{:S(2)}, u32[]{:S(2)}) %collective-permute-start.8) | collective-permute-done | bytes 49184 | tf_op jit(solution)/shard_map/ppermute | solution.py:329
  42.9 3.0 %collective-permute-done.7.first_ref = bf16[3,64,128]{2,1,0:T(8,128)(2,1)S(1)} collective-permute-done((bf16[3,64,128]{2,1,0:T(8,128)(2,1)S(1)}, bf16[3,64,128]{2,1,0:T(8,128)(2,1)S(1)}, u32[]{:S(2)}, u32[]{:S(2)}) %collective-permute-start.7) | collective-permute-done | bytes 49184 | tf_op jit(solution)/shard_map/ppermute | solution.py:329
  45.9 2.2 %copy-done.2 = bf16[8,64,4096]{2,1,0:T(8,128)(2,1)S(1)} copy-done((bf16[8,64,4096]{2,1,0:T(8,128)(2,1)S(1)}, bf16[8,64,4096]{2,1,0:T(8,128)(2,1)}, u32[]{:S(2)}) %copy-start.2) | copy-done | bytes 4194328
  48.1 2.2 %copy-done.3 = bf16[8,64,4096]{2,1,0:T(8,128)(2,1)S(1)} copy-done((bf16[8,64,4096]{2,1,0:T(8,128)(2,1)S(1)}, bf16[8,64,4096]{2,1,0:T(8,128)(2,1)}, u32[]{:S(2)}) %copy-start.3) | copy-done | bytes 4194328
  50.3 1.0 copy-done.4
  51.4 1.0 copy-done.6
  52.4 1.0 copy-done.9
  53.4 1.0 copy-done.11
  54.5 1.0 copy-done.13
  58.1 22.1 %inner.1 = (bf16[64,4096]{1,0:T(8,128)(2,1)S(1)}, bf16[64,4096]{1,0:T(8,128)(2,1)S(1)}, bf16[3,64,128]{2,1,0:T(8,128)(2,1)S(1)}) custom-call(s32[6]{0:T(128)S(1)} %stack.77.scal_ref, s32[512]{0:T(512)S(1)} %reshape.60.near_index, s32[512]{0:T(512)S(1)} %reshape.61.far_index, bf16[64,4096]{1,0:T(8,128)(2,1)S(1)} %collective-permute-done.rows_b, ...), custom_call_target="tpu_custom_call" | custom-call | tf_op jit(solution)/shard_map/inner/pallas_call | solution.py:428
  80.3 1.2 collective-permute-done.13
  81.6 4.1 %collective-permute-done.14 = bf16[3,64,128]{2,1,0:T(8,128)(2,1)S(1)} collective-permute-done((bf16[3,64,128]{2,1,0:T(8,128)(2,1)S(1)}, bf16[3,64,128]{2,1,0:T(8,128)(2,1)S(1)}, u32[]{:S(2)}, u32[]{:S(2)}) %collective-permute-start.14) | collective-permute-done | bytes 49184 | tf_op jit(solution)/shard_map/ppermute | solution.py:318
  85.9 3.4 %collective-permute-start.9 = (bf16[64,4096]{1,0:T(8,128)(2,1)S(1)}, bf16[64,4096]{1,0:T(8,128)(2,1)S(1)}, u32[]{:S(2)}, u32[]{:S(2)}) collective-permute-start(bf16[64,4096]{1,0:T(8,128)(2,1)S(1)} %get-tuple-element.13.rows_own), channel_id=1, source_target_pairs={{0,127},{1,2},{2,1},{3,4},{4,3},{5,6},{6,5},{7,8},{8,7},{9,10},{10... | collective-permute-start | bytes 1572872 | tf_op jit(solution)/shard_map/ppermute | solution.py:335
  89.3 3.8 %collective-permute-start.11 = (bf16[64,4096]{1,0:T(8,128)(2,1)S(1)}, bf16[64,4096]{1,0:T(8,128)(2,1)S(1)}, u32[]{:S(2)}, u32[]{:S(2)}) collective-permute-start(bf16[64,4096]{1,0:T(8,128)(2,1)S(1)} %get-tuple-element.14.coords_own), channel_id=1, source_target_pairs={{0,127},{1,2},{2,1},{3,4},{4,3},{5,6},{6,5},{7,8},{8,7},{9,10},{10... | collective-permute-start | bytes 1572872 | tf_op jit(solution)/shard_map/ppermute | solution.py:335
  93.3 13.3 %collective-permute-done.17.second_ref = bf16[3,64,128]{2,1,0:T(8,128)(2,1)S(1)} collective-permute-done((bf16[3,64,128]{2,1,0:T(8,128)(2,1)S(1)}, bf16[3,64,128]{2,1,0:T(8,128)(2,1)S(1)}, u32[]{:S(2)}, u32[]{:S(2)}) %collective-permute-start.17) | collective-permute-done | bytes 49184 | tf_op jit(solution)/shard_map/ppermute | solution.py:329
  106.7 4.1 %collective-permute-done.16.first_ref = bf16[3,64,128]{2,1,0:T(8,128)(2,1)S(1)} collective-permute-done((bf16[3,64,128]{2,1,0:T(8,128)(2,1)S(1)}, bf16[3,64,128]{2,1,0:T(8,128)(2,1)S(1)}, u32[]{:S(2)}, u32[]{:S(2)}) %collective-permute-start.16) | collective-permute-done | bytes 49184 | tf_op jit(solution)/shard_map/ppermute | solution.py:329
  110.9 20.0 %outer.1 = (f32[64,4096]{1,0:T(8,128)S(1)}, f32[64,64]{1,0:T(8,128)S(1)}) custom-call(s32[6]{0:T(128)S(1)} %stack.77.scal_ref, s32[512]{0:T(512)S(1)} %reshape.60.near_index, s32[512]{0:T(512)S(1)} %reshape.61.far_index, bf16[64,4096]{1,0:T(8,128)(2,1)S(1)} %collective-permute-done.9.rows_b, bf16[64,4096]{1,0:T(8,128)(2,1)S(1)} %get-tuple-element.13.rows_own, ...), custom_call_target="tpu_custom_call" | custom-call | tf_op jit(solution)/shard_map/outer/pallas_call | solution.py:446
  131.0 1.2 collective-permute-done.18
  132.2 3.9 %collective-permute-done.19 = f32[64,64]{1,0:T(8,128)S(1)} collective-permute-done((f32[64,64]{1,0:T(8,128)S(1)}, f32[64,64]{1,0:T(8,128)S(1)}, u32[]{:S(2)}, u32[]{:S(2)}) %collective-permute-start.19) | collective-permute-done | bytes 16416 | tf_op jit(solution)/shard_map/ppermute | solution.py:318
  136.1 5.1 %collective-permute-done.20 = f32[64,64]{1,0:T(8,128)S(1)} collective-permute-done((f32[64,64]{1,0:T(8,128)S(1)}, f32[64,64]{1,0:T(8,128)S(1)}, u32[]{:S(2)}, u32[]{:S(2)}) %collective-permute-start.20) | collective-permute-done | bytes 16416 | tf_op jit(solution)/shard_map/ppermute | solution.py:318
  141.2 3.9 %collective-permute-done.21 = f32[64,64]{1,0:T(8,128)S(1)} collective-permute-done((f32[64,64]{1,0:T(8,128)S(1)}, f32[64,64]{1,0:T(8,128)S(1)}, u32[]{:S(2)}, u32[]{:S(2)}) %collective-permute-start.21) | collective-permute-done | bytes 16416 | tf_op jit(solution)/shard_map/ppermute | solution.py:318
  145.2 28.4 %pairs.1 = (f32[64,4096]{1,0:T(8,128)}, f32[32,64,128]{2,1,0:T(8,128)S(1)}) custom-call(f32[64,4096]{1,0:T(8,128)S(1)} %get-tuple-element.16.samples_ref), custom_call_target="tpu_custom_call" | custom-call | tf_op jit(solution)/shard_map/pairs/pallas_call | solution.py:464
  173.6 9.0 %group.1 = f32[64,2048]{1,0:T(8,128)} custom-call(f32[64,64]{1,0:T(8,128)S(1)} %add.142.refs_0_, f32[32,64,128]{2,1,0:T(8,128)S(1)} %get-tuple-element.19.refs_1_), custom_call_target="tpu_custom_call" | custom-call | tf_op jit(solution)/shard_map/group/pallas_call | solution.py:473
  (88 shorter events, 7.4 us)
Async XLA Ops:
  0.6 45.3 %collective-permute-start.1 = (bf16[64,4096]{1,0:T(8,128)(2,1)}, bf16[64,4096]{1,0:T(8,128)(2,1)S(1)}, u32[]{:S(2)}, u32[]{:S(2)}) collective-permute-start(bf16[64,4096]{1,0:T(8,128)(2,1)} %rows_own.1), channel_id=1, source_target_pairs={{0,1},{1,0},{2,3},{3,2},{4,5},{5,4},{6,7},{7,6},{8,9},{9,8},{10,11... | collective-permute-start | bytes 1572872 | tf_op jit(solution)/shard_map/ppermute | solution.py:318
  0.7 45.2 %collective-permute-start = (bf16[64,4096]{1,0:T(8,128)(2,1)}, bf16[64,4096]{1,0:T(8,128)(2,1)S(1)}, u32[]{:S(2)}, u32[]{:S(2)}) collective-permute-start(bf16[64,4096]{1,0:T(8,128)(2,1)} %rows_own.1), channel_id=1, source_target_pairs={{0,127},{1,2},{2,1},{3,4},{4,3},{5,6},{6,5},{7,8},{8,7},{9,10},{10... | collective-permute-start | bytes 1572872 | tf_op jit(solution)/shard_map/ppermute | solution.py:335
  9.7 1.0 copy-start.8
  10.7 1.0 copy-start.10
  18.3 27.7 %collective-permute-start.3 = (bf16[64,4096]{1,0:T(8,128)(2,1)S(1)}, bf16[64,4096]{1,0:T(8,128)(2,1)S(1)}, u32[]{:S(2)}, u32[]{:S(2)}) collective-permute-start(bf16[64,4096]{1,0:T(8,128)(2,1)S(1)} %get-tuple-element.11.coords_own), channel_id=1, source_target_pairs={{0,1},{1,0},{2,3},{3,2},{4,5},{5,4},{6,7},{7,6},{8,9},{9,8},{10,11... | collective-permute-start | bytes 1572872 | tf_op jit(solution)/shard_map/ppermute | solution.py:318
  18.3 27.6 %collective-permute-start.2 = (bf16[64,4096]{1,0:T(8,128)(2,1)S(1)}, bf16[64,4096]{1,0:T(8,128)(2,1)S(1)}, u32[]{:S(2)}, u32[]{:S(2)}) collective-permute-start(bf16[64,4096]{1,0:T(8,128)(2,1)S(1)} %get-tuple-element.11.coords_own), channel_id=1, source_target_pairs={{0,127},{1,2},{2,1},{3,4},{4,3},{5,6},{6,5},{7,8},{8,7},{9,10},{10... | collective-permute-start | bytes 1572872 | tf_op jit(solution)/shard_map/ppermute | solution.py:335
  19.3 1.2 collective-permute-start.4
  20.5 8.1 %collective-permute-start.5 = (bf16[3,64,128]{2,1,0:T(8,128)(2,1)S(1)}, bf16[3,64,128]{2,1,0:T(8,128)(2,1)S(1)}, u32[]{:S(2)}, u32[]{:S(2)}) collective-permute-start(bf16[3,64,128]{2,1,0:T(8,128)(2,1)S(1)} %pad_maximum_fusion.6), channel_id=1, source_target_pairs={{0,2},{1,3},{2,0},{3,1},{4,6},{5,7},{6,4},{7,5},{8,10},{9,11},{10,... | collective-permute-start | bytes 147464 | tf_op jit(solution)/shard_map/ppermute | solution.py:318
  28.7 5.6 %collective-permute-start.6 = (bf16[4,64,128]{2,1,0:T(8,128)(2,1)S(1)}, bf16[4,64,128]{2,1,0:T(8,128)(2,1)S(1)}, u32[]{:S(2)}, u32[]{:S(2)}) collective-permute-start(bf16[4,64,128]{2,1,0:T(8,128)(2,1)S(1)} %pad_maximum_fusion.mine_ref), channel_id=1, source_target_pairs={{0,6},{1,7},{2,4},{3,5},{4,2},{5,3},{6,0},{7,1},{8,14},{9,15},{10,... | collective-permute-start | bytes 196616 | tf_op jit(solution)/shard_map/ppermute | solution.py:318
  34.3 7.5 %collective-permute-start.8 = (bf16[3,64,128]{2,1,0:T(8,128)(2,1)S(1)}, bf16[3,64,128]{2,1,0:T(8,128)(2,1)S(1)}, u32[]{:S(2)}, u32[]{:S(2)}) collective-permute-start(bf16[3,64,128]{2,1,0:T(8,128)(2,1)S(1)} %get-tuple-element.32), channel_id=1, source_target_pairs={{0,120},{1,121},{2,122},{3,123},{4,124},{5,125},{6,126},{7,127},{8... | collective-permute-start | bytes 147464 | tf_op jit(solution)/shard_map/ppermute | solution.py:329
  41.8 4.1 %collective-permute-start.7 = (bf16[3,64,128]{2,1,0:T(8,128)(2,1)S(1)}, bf16[3,64,128]{2,1,0:T(8,128)(2,1)S(1)}, u32[]{:S(2)}, u32[]{:S(2)}) collective-permute-start(bf16[3,64,128]{2,1,0:T(8,128)(2,1)S(1)} %get-tuple-element.33), channel_id=1, source_target_pairs={{0,8},{1,9},{2,10},{3,11},{4,12},{5,13},{6,14},{7,15},{8,0},{9,1},... | collective-permute-start | bytes 147464 | tf_op jit(solution)/shard_map/ppermute | solution.py:329
  42.9 67.9 %copy-start = (bf16[8,64,4096]{2,1,0:T(8,128)(2,1)S(1)}, bf16[8,64,4096]{2,1,0:T(8,128)(2,1)}, u32[]{:S(2)}) copy-start(bf16[8,64,4096]{2,1,0:T(8,128)(2,1)} %near_ref.3) | copy-start | bytes 12582916
  42.9 67.9 %copy-start.1 = (bf16[8,64,4096]{2,1,0:T(8,128)(2,1)S(1)}, bf16[8,64,4096]{2,1,0:T(8,128)(2,1)}, u32[]{:S(2)}) copy-start(bf16[8,64,4096]{2,1,0:T(8,128)(2,1)} %far_ref.3) | copy-start | bytes 12582916
  45.9 2.2 %copy-start.2 = (bf16[8,64,4096]{2,1,0:T(8,128)(2,1)S(1)}, bf16[8,64,4096]{2,1,0:T(8,128)(2,1)}, u32[]{:S(2)}) copy-start(bf16[8,64,4096]{2,1,0:T(8,128)(2,1)} %near_ref.2) | copy-start | bytes 12582916
  48.1 2.2 %copy-start.3 = (bf16[8,64,4096]{2,1,0:T(8,128)(2,1)S(1)}, bf16[8,64,4096]{2,1,0:T(8,128)(2,1)}, u32[]{:S(2)}) copy-start(bf16[8,64,4096]{2,1,0:T(8,128)(2,1)} %far_ref.2) | copy-start | bytes 12582916
  58.1 52.7 %copy-start.5 = (bf16[64,4096]{1,0:T(8,128)(2,1)S(1)}, bf16[64,4096]{1,0:T(8,128)(2,1)}, u32[]{:S(2)}) copy-start(bf16[64,4096]{1,0:T(8,128)(2,1)} %basis_ref.5) | copy-start | bytes 1572868
  58.1 52.7 %copy-start.7 = (bf16[64,4096]{1,0:T(8,128)(2,1)S(1)}, bf16[64,4096]{1,0:T(8,128)(2,1)}, u32[]{:S(2)}) copy-start(bf16[64,4096]{1,0:T(8,128)(2,1)} %transfer_ref.5) | copy-start | bytes 1572868
  58.1 52.7 %copy-start.17 = (bf16[3,3,64,64]{3,2,1,0:T(8,128)(2,1)S(1)}, bf16[3,3,64,64]{3,2,1,0:T(8,128)(2,1)}, u32[]{:S(2)}) copy-start(bf16[3,3,64,64]{3,2,1,0:T(8,128)(2,1)} %links_ref.3) | copy-start | bytes 221188
  80.2 1.3 collective-permute-start.13
  81.5 4.2 %collective-permute-start.14 = (bf16[3,64,128]{2,1,0:T(8,128)(2,1)S(1)}, bf16[3,64,128]{2,1,0:T(8,128)(2,1)S(1)}, u32[]{:S(2)}, u32[]{:S(2)}) collective-permute-start(bf16[3,64,128]{2,1,0:T(8,128)(2,1)S(1)} %pad_maximum_fusion.7), channel_id=1, source_target_pairs={{0,2},{1,3},{2,0},{3,1},{4,6},{5,7},{6,4},{7,5},{8,10},{9,11},{10,... | collective-permute-start | bytes 147464 | tf_op jit(solution)/shard_map/ppermute | solution.py:318
  85.7 7.4 %collective-permute-start.15 = (bf16[4,64,128]{2,1,0:T(8,128)(2,1)S(1)}, bf16[4,64,128]{2,1,0:T(8,128)(2,1)S(1)}, u32[]{:S(2)}, u32[]{:S(2)}) collective-permute-start(bf16[4,64,128]{2,1,0:T(8,128)(2,1)S(1)} %pad_maximum_fusion.1.mine_ref), channel_id=1, source_target_pairs={{0,6},{1,7},{2,4},{3,5},{4,2},{5,3},{6,0},{7,1},{8,14},{9,15},{10,... | collective-permute-start | bytes 196616 | tf_op jit(solution)/shard_map/ppermute | solution.py:318
  85.8 25.0 %collective-permute-start.10 = (bf16[64,4096]{1,0:T(8,128)(2,1)S(1)}, bf16[64,4096]{1,0:T(8,128)(2,1)S(1)}, u32[]{:S(2)}, u32[]{:S(2)}) collective-permute-start(bf16[64,4096]{1,0:T(8,128)(2,1)S(1)} %get-tuple-element.13.rows_own), channel_id=1, source_target_pairs={{0,1},{1,0},{2,3},{3,2},{4,5},{5,4},{6,7},{7,6},{8,9},{9,8},{10,11... | collective-permute-start | bytes 1572872 | tf_op jit(solution)/shard_map/ppermute | solution.py:318
  85.9 24.9 %collective-permute-start.9 = (bf16[64,4096]{1,0:T(8,128)(2,1)S(1)}, bf16[64,4096]{1,0:T(8,128)(2,1)S(1)}, u32[]{:S(2)}, u32[]{:S(2)}) collective-permute-start(bf16[64,4096]{1,0:T(8,128)(2,1)S(1)} %get-tuple-element.13.rows_own), channel_id=1, source_target_pairs={{0,127},{1,2},{2,1},{3,4},{4,3},{5,6},{6,5},{7,8},{8,7},{9,10},{10... | collective-permute-start | bytes 1572872 | tf_op jit(solution)/shard_map/ppermute | solution.py:335
  89.3 21.5 %collective-permute-start.12 = (bf16[64,4096]{1,0:T(8,128)(2,1)S(1)}, bf16[64,4096]{1,0:T(8,128)(2,1)S(1)}, u32[]{:S(2)}, u32[]{:S(2)}) collective-permute-start(bf16[64,4096]{1,0:T(8,128)(2,1)S(1)} %get-tuple-element.14.coords_own), channel_id=1, source_target_pairs={{0,1},{1,0},{2,3},{3,2},{4,5},{5,4},{6,7},{7,6},{8,9},{9,8},{10,11... | collective-permute-start | bytes 1572872 | tf_op jit(solution)/shard_map/ppermute | solution.py:318
  89.3 21.5 %collective-permute-start.11 = (bf16[64,4096]{1,0:T(8,128)(2,1)S(1)}, bf16[64,4096]{1,0:T(8,128)(2,1)S(1)}, u32[]{:S(2)}, u32[]{:S(2)}) collective-permute-start(bf16[64,4096]{1,0:T(8,128)(2,1)S(1)} %get-tuple-element.14.coords_own), channel_id=1, source_target_pairs={{0,127},{1,2},{2,1},{3,4},{4,3},{5,6},{6,5},{7,8},{8,7},{9,10},{10... | collective-permute-start | bytes 1572872 | tf_op jit(solution)/shard_map/ppermute | solution.py:335
  93.3 13.4 %collective-permute-start.17 = (bf16[3,64,128]{2,1,0:T(8,128)(2,1)S(1)}, bf16[3,64,128]{2,1,0:T(8,128)(2,1)S(1)}, u32[]{:S(2)}, u32[]{:S(2)}) collective-permute-start(bf16[3,64,128]{2,1,0:T(8,128)(2,1)S(1)} %get-tuple-element.30), channel_id=1, source_target_pairs={{0,120},{1,121},{2,122},{3,123},{4,124},{5,125},{6,126},{7,127},{8... | collective-permute-start | bytes 147464 | tf_op jit(solution)/shard_map/ppermute | solution.py:329
  106.7 4.1 %collective-permute-start.16 = (bf16[3,64,128]{2,1,0:T(8,128)(2,1)S(1)}, bf16[3,64,128]{2,1,0:T(8,128)(2,1)S(1)}, u32[]{:S(2)}, u32[]{:S(2)}) collective-permute-start(bf16[3,64,128]{2,1,0:T(8,128)(2,1)S(1)} %get-tuple-element.31), channel_id=1, source_target_pairs={{0,8},{1,9},{2,10},{3,11},{4,12},{5,13},{6,14},{7,15},{8,0},{9,1},... | collective-permute-start | bytes 147464 | tf_op jit(solution)/shard_map/ppermute | solution.py:329
  130.9 1.3 collective-permute-start.18
  132.2 3.9 %collective-permute-start.19 = (f32[64,64]{1,0:T(8,128)S(1)}, f32[64,64]{1,0:T(8,128)S(1)}, u32[]{:S(2)}, u32[]{:S(2)}) collective-permute-start(f32[64,64]{1,0:T(8,128)S(1)} %add.138), channel_id=1, source_target_pairs={{0,2},{1,3},{2,0},{3,1},{4,6},{5,7},{6,4},{7,5},{8,10},{9,11},{10,... | collective-permute-start | bytes 49160 | tf_op jit(solution)/shard_map/ppermute | solution.py:318
  136.1 5.1 %collective-permute-start.20 = (f32[64,64]{1,0:T(8,128)S(1)}, f32[64,64]{1,0:T(8,128)S(1)}, u32[]{:S(2)}, u32[]{:S(2)}) collective-permute-start(f32[64,64]{1,0:T(8,128)S(1)} %add.139), channel_id=1, source_target_pairs={{0,6},{1,7},{2,4},{3,5},{4,2},{5,3},{6,0},{7,1},{8,14},{9,15},{10,... | collective-permute-start | bytes 49160 | tf_op jit(solution)/shard_map/ppermute | solution.py:318
  141.2 3.9 %collective-permute-start.21 = (f32[64,64]{1,0:T(8,128)S(1)}, f32[64,64]{1,0:T(8,128)S(1)}, u32[]{:S(2)}, u32[]{:S(2)}) collective-permute-start(f32[64,64]{1,0:T(8,128)S(1)} %add.140), channel_id=1, source_target_pairs={{0,8},{1,9},{2,10},{3,11},{4,12},{5,13},{6,14},{7,15},{8,0},{9,1},... | collective-permute-start | bytes 49160 | tf_op jit(solution)/shard_map/ppermute | solution.py:318
  145.1 28.4 %collective-permute-start.22 = (f32[64,64]{1,0:T(8,128)S(1)}, f32[64,64]{1,0:T(8,128)S(1)}, u32[]{:S(2)}, u32[]{:S(2)}) collective-permute-start(f32[64,64]{1,0:T(8,128)S(1)} %add.141), channel_id=1, source_target_pairs={{0,24},{1,25},{2,26},{3,27},{4,28},{5,29},{6,30},{7,31},{8,16},{9,... | collective-permute-start | bytes 49160 | tf_op jit(solution)/shard_map/ppermute | solution.py:318
  (10 other events, 9.7 us)

commit v2 on v1

v2 whole, which is shorter than its diff:
```python
import jax
import jax.numpy as jnp
from jax import lax
from jax.experimental import pallas as pl
from jax.experimental.pallas import tpu as pltpu
from jax.sharding import PartitionSpec as P

AXES = ("box", "leaf")
LEAF = 64
TILE = 128
STEPS = 8
bf16 = jnp.bfloat16
f32 = jnp.float32
highest = lax.Precision.HIGHEST

NN = (((1,), (0,)), ((), ()))
NT = (((1,), (1,)), ((), ()))


def dot(a, b, dims=NN, precision=None):
    return lax.dot_general(a, b, dims, precision=precision, preferred_element_type=f32)


def low_half(shape):
    return lax.broadcasted_iota(jnp.int32, shape, len(shape) - 1) < LEAF


def two_blocks(tile):
    low = low_half(tile.shape)
    zero = jnp.zeros_like(tile)
    return jnp.concatenate([jnp.where(low, tile, zero), jnp.where(low, zero, tile)], axis=0)


def swap_halves(tile):
    return jnp.concatenate([tile[:, LEAF:], tile[:, :LEAF]], axis=1)


def twice(block):
    return jnp.concatenate([block, block], axis=1)


def lanes(t):
    return pl.ds(pl.multiple_of(t * TILE, TILE), TILE)


def coarse_payload(sums, tree_ref, scal_ref, pay_ref):
    folded = sums + swap_halves(sums)
    pay_ref[0] = folded.astype(bf16)
    up = dot(folded[:, :LEAF].astype(bf16), tree_ref[0, scal_ref[0]])
    pay_ref[1] = twice(up).astype(bf16)
    up = dot(up.astype(bf16), tree_ref[1, scal_ref[1]])
    pay_ref[2] = twice(up).astype(bf16)


def split(x):
    high = x.astype(bf16)
    return high, (x - high.astype(f32)).astype(bf16)


def dot3(a, b, dims=NN):
    ah, al = split(a)
    bh, bl = split(b)
    side = dims[0][1][0]
    return dot(jnp.concatenate([ah, ah, al], axis=1), jnp.concatenate([bh, bl, bh], axis=side), dims)


def fetch(sources, targets, sems, chunks):
    def piece(n, g):
        source, target = sources[n], targets[n]
        wide = source.shape[-1] // chunks
        at = (slice(None),) * (len(source.shape) - 1) + (pl.ds(g * wide, wide),)
        return pltpu.make_async_copy(source.at[at], target.at[at], sems.at[n, g])

    for g in range(chunks):
        for n in range(len(sources)):
            piece(n, g).start()

    def wait(g):
        for n in range(len(sources)):
            piece(n, g).wait()

    return wait


def coords_kernel(scal_ref, tree_ref, probes_hbm, basis_hbm, transfer_hbm, coords_ref, pay_ref, rows_ref, basis_ref, transfer_ref, sems):
    wait = fetch((probes_hbm, basis_hbm, transfer_hbm), (rows_ref, basis_ref, transfer_ref), sems, STEPS // 2)
    per = rows_ref.shape[1] // TILE // (STEPS // 2)
    for g in range(STEPS // 2):
        wait(g)
        for u in range(per):
            at = slice((g * per + u) * TILE, (g * per + u + 1) * TILE)
            coords_ref[:, at] = dot(rows_ref[:, at], two_blocks(basis_ref[:, at]), NT).astype(bf16)
    coarse_payload(node_sums(coords_ref, transfer_ref), tree_ref, scal_ref, pay_ref)


def node_sums(coords_ref, transfer_ref):
    def step(g, sums):
        for u in range(8):
            at = lanes(g * 8 + u)
            sums = sums + dot(coords_ref[:, at], two_blocks(transfer_ref[:, at]))
        return sums

    return lax.fori_loop(0, coords_ref.shape[1] // TILE // 8, step, jnp.zeros((LEAF, TILE), f32))


def by_tiles(count, one):
    def step(g, carry):
        for u in range(8):
            one(lanes(g * 8 + u))
        return carry

    lax.fori_loop(0, count // 8, step, 0)


def store_tile(store_ref, t, tile):
    store_ref[t] = tile
    store_ref[store_ref.shape[0] // 2 + t] = swap_halves(tile)


def fill_store(store_ref, sources, bases):
    tiles = sources[0].shape[1] // TILE
    for n, (source, basis) in enumerate(zip(sources, bases)):

        def step(g, carry, n=n, source=source, basis=basis):
            for u in range(8):
                t = g * 8 + u
                tile = source[:, lanes(t)]
                if basis is not None:
                    tile = dot(tile, two_blocks(basis[:, lanes(t)]), NT).astype(bf16)
                store_tile(store_ref, n * tiles + t, tile)
            return carry

        lax.fori_loop(0, tiles // 8, step, 0)


def gathered(store_ref, index_ref, pair, low):
    rows = []
    for h in range(2):
        base = (2 * pair + h) * 8
        cols = []
        for k in range(4):
            first = store_ref[index_ref[base + 2 * k]]
            second = store_ref[index_ref[base + 2 * k + 1]]
            cols.append(jnp.where(low, first, second))
        rows.append(jnp.concatenate(cols, axis=1))
    return jnp.concatenate(rows, axis=0)


def interact_kernel(index_ref, before_ref, own_ref, after_ref, *refs):
    *bases, blocks_ref, out_ref, store_ref = refs
    bases = (bases[0], None, bases[1]) if bases else (None, None, None)
    fill_store(store_ref, (before_ref, own_ref, after_ref), bases)
    low = low_half((LEAF, TILE))

    def step(g, carry):
        for u in range(4):
            pair = g * 4 + u
            blocks = blocks_ref[:, :, lanes(pair)].reshape(8 * LEAF, TILE)
            both = dot(gathered(store_ref, index_ref, pair, low), blocks)
            out_ref[:, lanes(pair)] = jnp.where(low, both[:LEAF], both[LEAF:])
        return carry

    lax.fori_loop(0, own_ref.shape[1] // TILE // 4, step, 0)


def descend(scal_ref, mine_ref, other_ref, first_ref, second_ref, tree_ref, links_ref):
    b0, b1, b2 = scal_ref[0], scal_ref[1], scal_ref[2]
    odd, has_left, has_right = scal_ref[3], scal_ref[4], scal_ref[5]

    def low_group(n):
        return jnp.where(b2 == 0, mine_ref[n], other_ref[n])

    def high_group(n):
        return jnp.where(b2 == 0, other_ref[n], mine_ref[n])

    def left(n):
        tile = jnp.where(odd == 1, first_ref[n], second_ref[n])
        return jnp.where(has_left == 1, tile, jnp.zeros_like(tile))

    def right(n):
        tile = jnp.where(odd == 1, second_ref[n], first_ref[n])
        return jnp.where(has_right == 1, tile, jnp.zeros_like(tile))

    def pick(j, options):
        tile = options[-1]
        for n in range(len(options) - 2, -1, -1):
            tile = jnp.where(j == n, options[n], tile)
        return tile

    ext0 = [left(2), low_group(0), low_group(1), high_group(0), high_group(1), right(2)]
    ext1 = [left(1), low_group(2), high_group(2), right(1)]
    j0, j1 = b2 * 2 + b1, b2
    around = [
        (pick(j0, ext0[:4]), pick(j0, ext0[2:])),
        (pick(j1, ext1[:2]), pick(j1, ext1[2:])),
        (left(0), right(0)),
    ]
    coupled = []
    for c, parity in enumerate((b0, b1, b2)):
        mid = links_ref[c, 1]
        none = jnp.zeros_like(mid)
        lo = jnp.concatenate([links_ref[c, 0], jnp.where(parity == 1, mid, none)], axis=0)
        hi = jnp.concatenate([jnp.where(parity == 0, mid, none), links_ref[c, 2]], axis=0)
        coupled.append(dot(around[c][0], lo) + dot(around[c][1], hi))
    h = coupled[1] + dot(coupled[2].astype(bf16), tree_ref[1, b1], NT)
    h = coupled[0] + dot(h.astype(bf16), tree_ref[0, b0], NT)
    return twice(h).astype(bf16)


def finish(near_ref, far_ref, basis_ref, transfer_ref, descent, coeffs_ref, out_ref):
    def coeffs(at):
        down = dot(descent, two_blocks(transfer_ref[:, at]), NT)
        coeffs_ref[:, at] = (far_ref[:, at] + down).astype(bf16)

    def result(at):
        out = near_ref[:, at] + dot(coeffs_ref[:, at], two_blocks(basis_ref[:, at]))
        out_ref[:, at] = out.astype(out_ref.dtype)

    count = near_ref.shape[1] // TILE
    by_tiles(count, coeffs)
    by_tiles(count, result)


def inner_kernel(
    scal_ref, near_ref, far_ref, basis_ref, transfer_ref,
    mine_ref, other_ref, first_ref, second_ref, tree_ref, links_ref, next_tree_ref, next_basis_ref, next_transfer_ref,
    middle_ref, coords_ref, pay_ref, coeffs_ref,
):
    descent = descend(scal_ref, mine_ref, other_ref, first_ref, second_ref, tree_ref, links_ref)
    finish(near_ref, far_ref, basis_ref, transfer_ref, descent, coeffs_ref, middle_ref)

    def next_coords(at):
        coords_ref[:, at] = dot(middle_ref[:, at], two_blocks(next_basis_ref[:, at]), NT).astype(bf16)

    by_tiles(middle_ref.shape[1] // TILE, next_coords)
    coarse_payload(node_sums(coords_ref, next_transfer_ref), next_tree_ref, scal_ref, pay_ref)


def outer_kernel(
    scal_ref, near_ref, far_ref, basis_ref, transfer_ref,
    mine_ref, other_ref, first_ref, second_ref, tree_ref, links_ref,
    samples_ref, work_ref, gram_ref, coeffs_ref,
):
    descent = descend(scal_ref, mine_ref, other_ref, first_ref, second_ref, tree_ref, links_ref)
    finish(near_ref, far_ref, basis_ref, transfer_ref, descent, coeffs_ref, samples_ref)
    low = low_half((LEAF, TILE))

    def step(g, total):
        for u in range(4):
            t = g * 4 + u
            both = jnp.concatenate([samples_ref[:, lanes(2 * t)], samples_ref[:, lanes(2 * t + 1)]], axis=0)
            both = dot3(both, both, NT)
            gram = jnp.where(low, both[:LEAF], both[LEAF:]) / TILE
            work_ref[t] = gram
            total = total + gram
        return total

    total = lax.fori_loop(0, work_ref.shape[0] // 4, step, jnp.zeros((LEAF, TILE), f32))
    gram_ref[...] = total + swap_halves(total)


def lane_take(tile, index):
    return jnp.take_along_axis(tile, index, axis=1, mode="promise_in_bounds")


def each(count, unroll, one):
    unroll = min(unroll, count)

    def step(g, carry):
        for u in range(unroll):
            one(g * unroll + u)
        return carry

    lax.fori_loop(0, count // unroll, step, 0)


def eliminate(work_ref, tee_ref):
    count = work_ref.shape[0]
    per = min(count, 4)
    groups = count // per
    sub = lax.broadcasted_iota(jnp.int32, (8, TILE), 0)
    lane = lax.broadcasted_iota(jnp.int32, (8, TILE), 1)
    col, half = lane % LEAF, lane // LEAF
    panels = LEAF // 8
    for kb in range(panels):
        base = kb * 8
        rows = slice(base, base + 8)
        inside = (col >= base) & (col < base + 8)
        cols = []
        for g in range(groups):
            tiles = [work_ref[g * per + t, rows, :] for t in range(per)]
            packed = []
            for j in range(8):
                index = lane // 16 % 2 * LEAF + (base + j)
                value = lane_take(tiles[0], index)
                for t in range(1, per):
                    value = jnp.where(lane // 32 == t, lane_take(tiles[t], index), value)
                packed.append(value)
            cols.append(packed)
        tees = [[] for _ in range(groups)]
        for j in range(8):
            for c, tee in zip(cols, tees):
                inv = lax.rsqrt(c[j][j : j + 1, :])
                lower = c[j] * inv
                below = jnp.where(sub > j, lower, 0.0)
                for n in range(j + 1, 8):
                    c[n] = c[n] - lower * lower[n : n + 1, :]
                for n in range(j):
                    row = tee[n][j : j + 1, :] * inv
                    tee[n] = jnp.where(sub == j, row, tee[n] - below * row)
                tee.append(jnp.where(sub == j, inv, -below * inv))
        for g in range(groups):
            for j in range(8):
                tee_ref[g * 8 + j] = tees[g][j]

        for tt in range(per):
            index = tt * 32 + half * 16
            for g in range(groups):
                t = g * per + tt
                panel = work_ref[t, rows, :]
                spread = [lane_take(tee_ref[g * 8 + j], index) for j in range(8)]
                done = spread[0] * panel[:1, :]
                for j in range(1, 8):
                    done = done + spread[j] * panel[j : j + 1, :]
                for j in range(8):
                    done = jnp.where((col == base + j) & (sub >= j), spread[j], done)
                work_ref[t, rows, :] = done
        if kb == panels - 1:
            break

        def update(t):
            left = work_ref[t, rows, :]
            right = jnp.where(inside & (col > base + sub), 0.0, left)
            left = stacked(left, (0, 0, 1))
            right = stacked(right, (0, 1, 0))
            both = lax.dot_general(left, right, (((0,), (0,)), ((), ())), preferred_element_type=f32)
            for ib in range(kb + 1, panels):
                at = slice(ib * 8, ib * 8 + 8)
                other = slice(LEAF + ib * 8, LEAF + ib * 8 + 8)
                rest = jnp.where(inside, 0.0, work_ref[t, at, :])
                work_ref[t, at, :] = rest - jnp.where(half == 0, both[at], both[other])

        each(count, 4, update)


def stacked(x, order):
    high = x.astype(bf16).astype(f32)
    pieces = (high, x - high)
    return jnp.concatenate([pieces[n] for n in order] + [jnp.zeros_like(x)], axis=0).astype(bf16)


def parts(tile):
    row = lax.broadcasted_iota(jnp.int32, tile.shape, 0)
    col = lax.broadcasted_iota(jnp.int32, tile.shape, 1) % LEAF
    return row, col


def pair_kernel(gram_ref, samples_ref, work_ref, basis_ref, *scratch):
    work_ref[...] = gram_ref[...]
    eliminate(work_ref, *scratch)

    def solve(t):
        tile = work_ref[t]
        row, col = parts(tile)
        inverse = two_blocks(jnp.where(col <= row, tile, 0.0))
        one, two = lanes(2 * t), lanes(2 * t + 1)
        solved = dot3(inverse, jnp.concatenate([samples_ref[:, one], samples_ref[:, two]], axis=0))
        basis_ref[:, one] = solved[:LEAF]
        basis_ref[:, two] = solved[LEAF:]

    each(work_ref.shape[0], 4, solve)


def group_kernel(gram_ref, work_ref, out_ref, own_ref, *scratch, scale):
    own_ref[0] = gram_ref[...] / scale
    eliminate(own_ref, *scratch)
    tile = own_ref[0]
    row, col = parts(tile)
    inverse = jnp.where(col <= row, tile, 0.0)

    def solve(t):
        tile = work_ref[t]
        upper = jnp.where(col > row, tile, jnp.where(col == row, 1.0 / tile, 0.0))
        out_ref[:, lanes(t)] = dot3(inverse, two_blocks(upper), NT)

    each(work_ref.shape[0], 4, solve)


HBM = pl.BlockSpec(memory_space=pltpu.HBM)
VMEM = pl.BlockSpec(memory_space=pltpu.VMEM)
SMEM = pl.BlockSpec(memory_space=pltpu.SMEM)


def params(mib):
    return pltpu.CompilerParams(vmem_limit_bytes=mib * 2**20)


def elimination(count):
    return [
        pltpu.VMEM((max(count // 4, 1) * 8, 8, TILE), f32),
    ]


def struct(shape, dtype):
    return jax.ShapeDtypeStruct(shape, dtype)


def swap(x, mask):
    count = lax.axis_size(AXES)
    return lax.ppermute(x, AXES, [(i, i ^ mask) for i in range(count)])


def neighbours(x, width, second):
    count = lax.axis_size(AXES)
    blocks = count // width
    route = []
    for b in range(blocks):
        forward = (b % 2 == 0) != second
        to = (b + 1 if forward else b - 1) % blocks
        route += [(b * width + m, to * width + m) for m in range(width)]
    return lax.ppermute(x, AXES, route)


def node_halo(x):
    count = lax.axis_size(AXES)
    route = [(i, (i - 1 if i % 2 == 0 else i + 1) % count) for i in range(count)]
    return lax.ppermute(x, AXES, route), swap(x, 1)


def leaf_table(index, node):
    leaves = index.shape[0]
    place = index - (node - 1) * leaves
    block = place // leaves
    block = jnp.where(node % 2 == 1, 2 - block, block)
    place = block * leaves + place % leaves
    slot = lax.broadcasted_iota(jnp.int32, index.shape, 1)
    return (((place + slot) % 2) * (3 * leaves // 2) + place // 2).reshape(-1)


def coarse_near(pay, node):
    low = low_half((LEAF, TILE))
    b0, b1 = node % 2, node // 2 % 2

    def halves(bit, mine, other):
        return jnp.where(low == (bit == 0), mine, other)

    other = swap(pay, 1)
    z0 = halves(b0, pay[0], other[0])
    stage = jnp.stack([z0, pay[1] + other[1], pay[2] + other[2]])
    other = swap(stage, 2)
    first = jnp.where(b1 == 0, stage[0], other[0])
    second = jnp.where(b1 == 0, other[0], stage[0])
    return jnp.stack([first, second, halves(b1, stage[1], other[1]), stage[2] + other[2]])


def coarse_far(mine, other, node):
    low = low_half((LEAF, TILE))
    b2, odd = node // 4 % 2, node // 8 % 2
    top = jnp.where(low == (b2 == 0), mine[3], other[3])
    lo = jnp.where(b2 == 0, mine, other)
    hi = jnp.where(b2 == 0, other, mine)
    rightward = jnp.stack([top, hi[2], hi[1]])
    leftward = jnp.stack([top, lo[2], lo[0]])
    one = neighbours(jnp.where(odd == 0, rightward, leftward), 8, False)
    two = neighbours(jnp.where(odd == 0, leftward, rightward), 8, True)
    return one, two


def after(x, *values):
    return lax.optimization_barrier((x, *values))[0]


def local(
    probes,
    near_index,
    far_index,
    inner_near,
    inner_basis,
    inner_far,
    inner_transfer,
    inner_tree,
    inner_links,
    outer_near,
    outer_basis,
    outer_far,
    outer_transfer,
    outer_tree,
    outer_links,
):
    node = lax.axis_index(AXES)
    count = lax.axis_size(AXES)
    width = probes.shape[1]
    block = node // 8
    scal = jnp.stack(
        [
            node % 2,
            node // 2 % 2,
            node // 4 % 2,
            block % 2,
            (block > 0).astype(jnp.int32),
            (block < count // 8 - 1).astype(jnp.int32),
        ]
    ).astype(jnp.int32)
    near_table = leaf_table(near_index, node)
    far_table = leaf_table(far_index, node)

    def interact(index, rows, blocks, bases=()):
        return pl.pallas_call(
            interact_kernel,
            in_specs=[SMEM] + [VMEM] * (4 + len(bases)),
            out_specs=VMEM,
            out_shape=struct((LEAF, width), f32),
            scratch_shapes=[pltpu.VMEM((3 * width // LEAF, LEAF, TILE), bf16)],
            compiler_params=params(6),
            name="interact",
        )(index, *rows, *bases, blocks)

    row = struct((LEAF, width), bf16)
    payload = struct((3, LEAF, TILE), bf16)
    pairs = width // TILE

    rows_b, rows_a = node_halo(probes)
    coords, pay, rows, basis, transfer = pl.pallas_call(
        coords_kernel,
        in_specs=[SMEM, VMEM, HBM, HBM, HBM],
        out_specs=(VMEM,) * 5,
        out_shape=(row, payload, row, row, row),
        scratch_shapes=[pltpu.SemaphoreType.DMA((3, STEPS // 2))],
        compiler_params=params(56),
        name="coords",
    )(scal, inner_tree, probes, inner_basis, inner_transfer)
    mine = coarse_near(pay, node)
    other = swap(mine, 6)
    coords_b, coords_a = node_halo(after(coords, mine))
    one, two = coarse_far(mine, other, node)
    basis_b, basis_a = node_halo(after(outer_basis, other))
    near_part = interact(near_table, (rows_b, rows, rows_a), inner_near)
    far_part = interact(far_table, (coords_b, coords, coords_a), inner_far)
    far_part, basis_b, basis_a = lax.optimization_barrier((far_part, basis_b, basis_a))
    middle, coords, pay = pl.pallas_call(
        inner_kernel,
        in_specs=[SMEM] + [VMEM] * 13,
        out_specs=(VMEM,) * 3,
        out_shape=(row, row, payload),
        scratch_shapes=[pltpu.VMEM((LEAF, width), bf16)],
        compiler_params=params(6),
        name="inner",
    )(
        scal, near_part, far_part, basis, transfer,
        mine, other, one, two, inner_tree, inner_links, outer_tree, outer_basis, outer_transfer,
    )
    middle_b, middle_a = node_halo(middle)
    mine = coarse_near(pay, node)
    other = swap(mine, 6)
    one, two = coarse_far(mine, other, node)
    near_part = interact(near_table, (middle_b, middle, middle_a), outer_near)
    far_part = interact(far_table, (middle_b, coords, middle_a), outer_far, (basis_b, basis_a))
    samples, grams, gram = pl.pallas_call(
        outer_kernel,
        in_specs=[SMEM] + [VMEM] * 10,
        out_specs=(VMEM,) * 3,
        out_shape=(
            struct((LEAF, width), f32),
            struct((pairs // 2, LEAF, TILE), f32),
            struct((LEAF, TILE), f32),
        ),
        scratch_shapes=[pltpu.VMEM((LEAF, width), bf16)],
        compiler_params=params(6),
        name="outer",
    )(scal, near_part, far_part, outer_basis, outer_transfer, mine, other, one, two, outer_tree, outer_links)
    for mask in (1, 2, 6, 8, 24):
        gram = gram + swap(gram, mask)
    work, pair_basis = pl.pallas_call(
        pair_kernel,
        in_specs=[VMEM, VMEM],
        out_specs=(VMEM, VMEM),
        out_shape=(struct(grams.shape, f32), struct((LEAF, width), f32)),
        scratch_shapes=elimination(pairs // 2),
        compiler_params=params(6),
        name="pairs",
    )(grams, samples)
    scale = pairs * lax.axis_size("leaf")
    group_basis = pl.pallas_call(
        lambda *refs: group_kernel(*refs, scale=scale),
        in_specs=[VMEM, VMEM],
        out_specs=VMEM,
        out_shape=struct((LEAF, pairs * LEAF), f32),
        scratch_shapes=[pltpu.VMEM((1, LEAF, TILE), f32)] + elimination(1),
        compiler_params=params(6),
        name="group",
    )(gram, work)
    return (pair_basis, group_basis)


def solution(mesh):
    flat = P(None, AXES)
    index = P(AXES, None)
    blocks = P(None, None, AXES)
    tree = P(None, None, None, AXES)
    factor = (blocks, flat, blocks, flat, tree, tree)
    return jax.shard_map(
        local,
        mesh=mesh,
        in_specs=(flat, index, index) + factor + factor,
        out_specs=(flat, flat),
        check_vma=False,
    )
```

time: 183 us -> 127 us (0.69)
  Pallas kernels: 84.1 us -> 54.5 us
  waiting for transfers between devices: 60 us -> 40.8 us
  local copies, waits for them, and re-layouts: 16.6 us -> 4.34 us
  starting transfers between devices: 20 us -> 23.6 us
    ppermute x4, waiting for transfers between devices: 27.1 us -> 0.01 us  [neighbours(): return lax.ppermute(x, AXES, route)]
    pallas_call x4 -> x8, Pallas kernels: 75.1 us -> 49.3 us  [the longest x4 22 us: interact(): pl.pallas_call(interact_kernel, in_specs=[SMEM] + [VMEM] * (4 + len(bases...]
    unnamed x38 -> x30, local copies, waits for them, and re-layouts: 16.2 us -> 3.31 us
    ppermute x4, waiting for transfers between devices: 0.01 us -> 12 us  [node_halo(): return (lax.ppermute(x, AXES, route), swap(x, 1))]
    ppermute x15, waiting for transfers between devices: 33 us -> 28.8 us  [swap(): return lax.ppermute(x, AXES, [(i, i ^ mask) for i in range(count)])]
    ppermute x4, starting transfers between devices: 0.91 us -> 4.72 us  [neighbours(): return lax.ppermute(x, AXES, route)]
    pallas_call x1, Pallas kernels: 9.01 us -> 5.27 us  [local(): pl.pallas_call(lambda *refs: group_kernel(*refs, scale=scale), in_specs=[...]
  transfers between devices with their start and end apart: 23 -> 23, of which waited for: 13 -> 11; matrix products, arithmetic and copies ran while one was open for 1% -> 2% of each run, Pallas kernels for 18% -> 31%
where the time goes in v2:
time: 127 us; the launch traced here: 126 us
  Pallas kernels  54.5 us (43%)
  waiting for transfers between devices  40.8 us (32%)
  starting transfers between devices  23.6 us (19%)
  local copies, waits for them, and re-layouts  4.34 us (3%)
  other arithmetic  1.68 us (1%)
    ppermute x15, waiting for transfers between devices, swap(): return lax.ppermute(x, AXES, [(i, i ^ mask) for i in range(count)])  28.8 us
    pallas_call x4, Pallas kernels, interact(): pl.pallas_call(interact_kernel, in_specs=[SMEM] + [VMEM] * (4 + len(bases...  22 us
    ppermute x4, starting transfers between devices, node_halo(): return (lax.ppermute(x, AXES, route), swap(x, 1))  15.6 us
    pallas_call x1, Pallas kernels, local(): pl.pallas_call(pair_kernel, in_specs=[VMEM, VMEM], out_specs=(VMEM, VMEM)...  12.4 us
    ppermute x4, waiting for transfers between devices, node_halo(): return (lax.ppermute(x, AXES, route), swap(x, 1))  12 us
    pallas_call x1, Pallas kernels, local(): pl.pallas_call(inner_kernel, in_specs=[SMEM] + [VMEM] * 13, out_specs=(VM...  5.35 us
    pallas_call x1, Pallas kernels, local(): pl.pallas_call(lambda *refs: group_kernel(*refs, scale=scale), in_specs=[...  5.27 us
    pallas_call x1, Pallas kernels, local(): pl.pallas_call(coords_kernel, in_specs=[SMEM, VMEM, HBM, HBM, HBM], out_s...  5.13 us
  transfers between devices with their start and end apart: 23, of which 11 were waited for; matrix products, arithmetic and copies ran while one was open for 2% of the time, Pallas kernels for 31%

profile of v2, /device:TPU:0, one launch (start us, length us, event | category | flops | bytes accessed | tf_op | source)
XLA Modules:
  0.0 126.1 jit_solution(2633179346429866948)
XLA Ops:
  0.6 8.3 %collective-permute-start = (bf16[64,4096]{1,0:T(8,128)(2,1)}, bf16[64,4096]{1,0:T(8,128)(2,1)S(1)}, u32[]{:S(2)}, u32[]{:S(2)}) collective-permute-start(bf16[64,4096]{1,0:T(8,128)(2,1)} %probes_hbm.1), channel_id=1, source_target_pairs={{0,127},{1,2},{2,1},{3,4},{4,3},{5,6},{6,5},{7,8},{8,7},{9,10},{10... | collective-permute-start | bytes 1572872 | tf_op jit(solution)/shard_map/ppermute | solution.py:427
  8.9 0.7 stack.77.scal_ref
  9.6 5.1 %coords.1 = (bf16[64,4096]{1,0:T(8,128)(2,1)}, bf16[3,64,128]{2,1,0:T(8,128)(2,1)}, bf16[64,4096]{1,0:T(8,128)(2,1)}, bf16[64,4096]{1,0:T(8,128)(2,1)}, bf16[64,4096]{1,0:T(8,128)(2,1)}) custom-call(s32[6]{0:T(128)} %stack.77.scal_ref, bf16[2,2,64,64]{3,2,1,0:T(8,128)(2,1)} %tree_ref.4, bf16[64,4096]{1,0:T(8,128)(2,1)} %probes_hbm.1, ...), custom_call_target="tpu_custom_call" | custom-call | tf_op jit(solution)/shard_map/coords/pallas_call | solution.py:523
  14.8 0.6 collective-permute-start.2
  15.3 1.1 collective-permute-done.2
  16.4 0.8 slice_select_fusion.5
  17.3 4.0 %collective-permute-done.3 = bf16[3,64,128]{2,1,0:T(8,128)(2,1)S(1)} collective-permute-done((bf16[3,64,128]{2,1,0:T(8,128)(2,1)S(1)}, bf16[3,64,128]{2,1,0:T(8,128)(2,1)S(1)}, u32[]{:S(2)}, u32[]{:S(2)}) %collective-permute-start.3) | collective-permute-done | bytes 49184 | tf_op jit(solution)/shard_map/ppermute | solution.py:410
  21.5 1.9 %collective-permute-start.4 = (bf16[64,4096]{1,0:T(8,128)(2,1)}, bf16[64,4096]{1,0:T(8,128)(2,1)S(1)}, u32[]{:S(2)}, u32[]{:S(2)}) collective-permute-start(bf16[64,4096]{1,0:T(8,128)(2,1)} %get-tuple-element.23.own_ref), channel_id=1, source_target_pairs={{0,127},{1,2},{2,1},{3,4},{4,3},{5,6},{6,5},{7,8},{8,7},{9,10},{10... | collective-permute-start | bytes 1572872 | tf_op jit(solution)/shard_map/ppermute | solution.py:427
  23.4 4.2 %collective-permute-done.6.other_ref = bf16[4,64,128]{2,1,0:T(8,128)(2,1)S(1)} collective-permute-done((bf16[4,64,128]{2,1,0:T(8,128)(2,1)S(1)}, bf16[4,64,128]{2,1,0:T(8,128)(2,1)S(1)}, u32[]{:S(2)}, u32[]{:S(2)}) %collective-permute-start.6) | collective-permute-done | bytes 65568 | tf_op jit(solution)/shard_map/ppermute | solution.py:410
  27.7 1.1 collective-permute-start.7
  29.1 6.8 %collective-permute-done.4.before_ref = bf16[64,4096]{1,0:T(8,128)(2,1)S(1)} collective-permute-done((bf16[64,4096]{1,0:T(8,128)(2,1)}, bf16[64,4096]{1,0:T(8,128)(2,1)S(1)}, u32[]{:S(2)}, u32[]{:S(2)}) %collective-permute-start.4) | collective-permute-done | bytes 524320 | tf_op jit(solution)/shard_map/ppermute | solution.py:427
  35.9 0.7 fusion.8
  37.0 2.2 %copy-done = bf16[8,64,4096]{2,1,0:T(8,128)(2,1)S(1)} copy-done((bf16[8,64,4096]{2,1,0:T(8,128)(2,1)S(1)}, bf16[8,64,4096]{2,1,0:T(8,128)(2,1)}, u32[]{:S(2)}) %copy-start) | copy-done | bytes 4194328
  39.2 1.0 copy-done.9
  40.2 4.8 %interact.4.near_ref = f32[64,4096]{1,0:T(8,128)S(1)} custom-call(s32[512]{0:T(512)S(1)} %reshape.60.index_ref, bf16[64,4096]{1,0:T(8,128)(2,1)S(1)} %collective-permute-done.before_ref, bf16[64,4096]{1,0:T(8,128)(2,1)S(1)} %copy-done.9, bf16[64,4096]{1,0:T(8,128)(2,1)S(1)} %collective-permute-done.1.after_ref, bf16[8,64,4096]{2,1,0:T(8,128)(2,1)S(1)} %copy-done), custom_call_target="tpu_custom_call" | custom-call | tf_op jit(solution)/shard_map/interact/pallas_call | solution.py:508
  45.2 5.5 %interact.5.far_ref = f32[64,4096]{1,0:T(8,128)S(1)} custom-call(s32[512]{0:T(512)S(1)} %reshape.61.index_ref, bf16[64,4096]{1,0:T(8,128)(2,1)S(1)} %collective-permute-done.4.before_ref, bf16[64,4096]{1,0:T(8,128)(2,1)S(1)} %copy-done.8, bf16[64,4096]{1,0:T(8,128)(2,1)} %collective-permute-done.5.after_ref, bf16[8,64,4096]{2,1,0:T(8,128)(2,1)S(1)} %copy-done.1), custom_call_target="tpu_custom_call" | custom-call | tf_op jit(solution)/shard_map/interact/pallas_call | solution.py:508
  50.8 5.4 %inner.1 = (bf16[64,4096]{1,0:T(8,128)(2,1)S(1)}, bf16[64,4096]{1,0:T(8,128)(2,1)S(1)}, bf16[3,64,128]{2,1,0:T(8,128)(2,1)S(1)}) custom-call(s32[6]{0:T(128)S(1)} %copy-done.14, f32[64,4096]{1,0:T(8,128)S(1)} %interact.4.near_ref, f32[64,4096]{1,0:T(8,128)S(1)} %interact.5.far_ref, bf16[64,4096]{1,0:T(8,128)(2,1)S(1)} %copy-done.6, ...), custom_call_target="tpu_custom_call" | custom-call | tf_op jit(solution)/shard_map/inner/pallas_call | solution.py:540
  56.2 1.2 collective-permute-done.13
  57.6 4.1 %collective-permute-done.14 = bf16[3,64,128]{2,1,0:T(8,128)(2,1)S(1)} collective-permute-done((bf16[3,64,128]{2,1,0:T(8,128)(2,1)S(1)}, bf16[3,64,128]{2,1,0:T(8,128)(2,1)S(1)}, u32[]{:S(2)}, u32[]{:S(2)}) %collective-permute-start.14) | collective-permute-done | bytes 49184 | tf_op jit(solution)/shard_map/ppermute | solution.py:410
  61.7 2.2 %collective-permute-start.15 = (bf16[4,64,128]{2,1,0:T(8,128)(2,1)S(1)}, bf16[4,64,128]{2,1,0:T(8,128)(2,1)S(1)}, u32[]{:S(2)}, u32[]{:S(2)}) collective-permute-start(bf16[4,64,128]{2,1,0:T(8,128)(2,1)S(1)} %pad_maximum_fusion.1.mine_ref), channel_id=1, source_target_pairs={{0,6},{1,7},{2,4},{3,5},{4,2},{5,3},{6,0},{7,1},{8,14},{9,15},{10,... | collective-permute-start | bytes 196616 | tf_op jit(solution)/shard_map/ppermute | solution.py:410
  63.9 4.2 %collective-permute-start.11 = (bf16[64,4096]{1,0:T(8,128)(2,1)S(1)}, bf16[64,4096]{1,0:T(8,128)(2,1)S(1)}, u32[]{:S(2)}, u32[]{:S(2)}) collective-permute-start(bf16[64,4096]{1,0:T(8,128)(2,1)S(1)} %get-tuple-element.28.own_ref), channel_id=1, source_target_pairs={{0,127},{1,2},{2,1},{3,4},{4,3},{5,6},{6,5},{7,8},{8,7},{9,10},{10... | collective-permute-start | bytes 1572872 | tf_op jit(solution)/shard_map/ppermute | solution.py:427
  68.3 4.5 %collective-permute-start.17 = (bf16[3,64,128]{2,1,0:T(8,128)(2,1)S(1)}, bf16[3,64,128]{2,1,0:T(8,128)(2,1)S(1)}, u32[]{:S(2)}, u32[]{:S(2)}) collective-permute-start(bf16[3,64,128]{2,1,0:T(8,128)(2,1)S(1)} %get-tuple-element.48), channel_id=1, source_target_pairs={{0,120},{1,121},{2,122},{3,123},{4,124},{5,125},{6,126},{7,127},{8... | collective-permute-start | bytes 147464 | tf_op jit(solution)/shard_map/ppermute | solution.py:421
  72.8 5.2 %collective-permute-done.11.before_ref = bf16[64,4096]{1,0:T(8,128)(2,1)S(1)} collective-permute-done((bf16[64,4096]{1,0:T(8,128)(2,1)S(1)}, bf16[64,4096]{1,0:T(8,128)(2,1)S(1)}, u32[]{:S(2)}, u32[]{:S(2)}) %collective-permute-start.11) | collective-permute-done | bytes 524320 | tf_op jit(solution)/shard_map/ppermute | solution.py:427
  78.0 4.8 %interact.6.near_ref = f32[64,4096]{1,0:T(8,128)S(1)} custom-call(s32[512]{0:T(512)S(1)} %reshape.60.index_ref, bf16[64,4096]{1,0:T(8,128)(2,1)S(1)} %collective-permute-done.11.before_ref, bf16[64,4096]{1,0:T(8,128)(2,1)S(1)} %get-tuple-element.28.own_ref, bf16[64,4096]{1,0:T(8,128)(2,1)S(1)} %collective-permute-done.12.after_ref, ...), custom_call_target="tpu_custom_call" | custom-call | tf_op jit(solution)/shard_map/interact/pallas_call | solution.py:508
  82.9 6.9 %interact.7.far_ref = f32[64,4096]{1,0:T(8,128)S(1)} custom-call(s32[512]{0:T(512)S(1)} %reshape.61.index_ref, bf16[64,4096]{1,0:T(8,128)(2,1)S(1)} %collective-permute-done.11.before_ref, bf16[64,4096]{1,0:T(8,128)(2,1)S(1)} %get-tuple-element.29.own_ref, bf16[64,4096]{1,0:T(8,128)(2,1)S(1)} %collective-permute-done.12.after_ref, ...), custom_call_target="tpu_custom_call" | custom-call | tf_op jit(solution)/shard_map/interact/pallas_call | solution.py:508
  89.8 4.3 %outer.1 = (f32[64,4096]{1,0:T(8,128)S(1)}, f32[16,64,128]{2,1,0:T(8,128)S(1)}, f32[64,128]{1,0:T(8,128)S(1)}) custom-call(s32[6]{0:T(128)S(1)} %copy-done.14, f32[64,4096]{1,0:T(8,128)S(1)} %interact.6.near_ref, f32[64,4096]{1,0:T(8,128)S(1)} %interact.7.far_ref, bf16[64,4096]{1,0:T(8,128)(2,1)S(1)} %copy-done.4, bf16[64,4096]{1,0:T(8,128)(2,1)S(1)} %copy-done.5, ...), custom_call_target="tpu_custom_call" | custom-call | tf_op jit(solution)/shard_map/outer/pallas_call | solution.py:558
  94.2 1.2 collective-permute-done.18
  95.4 3.9 %collective-permute-done.19 = f32[64,128]{1,0:T(8,128)S(1)} collective-permute-done((f32[64,128]{1,0:T(8,128)S(1)}, f32[64,128]{1,0:T(8,128)S(1)}, u32[]{:S(2)}, u32[]{:S(2)}) %collective-permute-start.19) | collective-permute-done | bytes 32800 | tf_op jit(solution)/shard_map/ppermute | solution.py:410
  99.4 5.1 %collective-permute-done.20 = f32[64,128]{1,0:T(8,128)S(1)} collective-permute-done((f32[64,128]{1,0:T(8,128)S(1)}, f32[64,128]{1,0:T(8,128)S(1)}, u32[]{:S(2)}, u32[]{:S(2)}) %collective-permute-start.20) | collective-permute-done | bytes 32800 | tf_op jit(solution)/shard_map/ppermute | solution.py:410
  104.5 3.9 %collective-permute-done.21 = f32[64,128]{1,0:T(8,128)S(1)} collective-permute-done((f32[64,128]{1,0:T(8,128)S(1)}, f32[64,128]{1,0:T(8,128)S(1)}, u32[]{:S(2)}, u32[]{:S(2)}) %collective-permute-start.21) | collective-permute-done | bytes 32800 | tf_op jit(solution)/shard_map/ppermute | solution.py:410
  108.4 12.4 %pairs.1 = (f32[16,64,128]{2,1,0:T(8,128)S(1)}, f32[64,4096]{1,0:T(8,128)}) custom-call(f32[16,64,128]{2,1,0:T(8,128)S(1)} %get-tuple-element.33.gram_ref, f32[64,4096]{1,0:T(8,128)S(1)} %get-tuple-element.34.samples_ref), custom_call_target="tpu_custom_call" | custom-call | tf_op jit(solution)/shard_map/pairs/pallas_call | solution.py:573
  120.9 5.3 %group.1 = f32[64,2048]{1,0:T(8,128)} custom-call(f32[64,128]{1,0:T(8,128)S(1)} %add.142.refs_0_, f32[16,64,128]{2,1,0:T(8,128)S(1)} %get-tuple-element.37.refs_1_), custom_call_target="tpu_custom_call" | custom-call | tf_op jit(solution)/shard_map/group/pallas_call | solution.py:583
  (84 shorter events, 1.4 us)
Async XLA Ops:
  0.6 28.2 %collective-permute-start = (bf16[64,4096]{1,0:T(8,128)(2,1)}, bf16[64,4096]{1,0:T(8,128)(2,1)S(1)}, u32[]{:S(2)}, u32[]{:S(2)}) collective-permute-start(bf16[64,4096]{1,0:T(8,128)(2,1)} %probes_hbm.1), channel_id=1, source_target_pairs={{0,127},{1,2},{2,1},{3,4},{4,3},{5,6},{6,5},{7,8},{8,7},{9,10},{10... | collective-permute-start | bytes 1572872 | tf_op jit(solution)/shard_map/ppermute | solution.py:427
  8.9 20.0 %collective-permute-start.1 = (bf16[64,4096]{1,0:T(8,128)(2,1)}, bf16[64,4096]{1,0:T(8,128)(2,1)S(1)}, u32[]{:S(2)}, u32[]{:S(2)}) collective-permute-start(bf16[64,4096]{1,0:T(8,128)(2,1)} %probes_hbm.1), channel_id=1, source_target_pairs={{0,1},{1,0},{2,3},{3,2},{4,5},{5,4},{6,7},{7,6},{8,9},{9,8},{10,11... | collective-permute-start | bytes 1572872 | tf_op jit(solution)/shard_map/ppermute | solution.py:410
  14.7 30.4 %copy-start.8 = (bf16[64,4096]{1,0:T(8,128)(2,1)S(1)}, bf16[64,4096]{1,0:T(8,128)(2,1)}, u32[]{:S(2)}) copy-start(bf16[64,4096]{1,0:T(8,128)(2,1)} %get-tuple-element.23.own_ref) | copy-start | bytes 1572868
  14.8 1.7 %collective-permute-start.2 = (bf16[3,64,128]{2,1,0:T(8,128)(2,1)}, bf16[3,64,128]{2,1,0:T(8,128)(2,1)S(1)}, u32[]{:S(2)}, u32[]{:S(2)}) collective-permute-start(bf16[3,64,128]{2,1,0:T(8,128)(2,1)} %get-tuple-element.22), channel_id=1, source_target_pairs={{0,1},{1,0},{2,3},{3,2},{4,5},{5,4},{6,7},{7,6},{8,9},{9,8},{10,11... | collective-permute-start | bytes 147464 | tf_op jit(solution)/shard_map/ppermute | solution.py:410
  17.2 4.2 %collective-permute-start.3 = (bf16[3,64,128]{2,1,0:T(8,128)(2,1)S(1)}, bf16[3,64,128]{2,1,0:T(8,128)(2,1)S(1)}, u32[]{:S(2)}, u32[]{:S(2)}) collective-permute-start(bf16[3,64,128]{2,1,0:T(8,128)(2,1)S(1)} %pad_maximum_fusion.6), channel_id=1, source_target_pairs={{0,2},{1,3},{2,0},{3,1},{4,6},{5,7},{6,4},{7,5},{8,10},{9,11},{10,... | collective-permute-start | bytes 147464 | tf_op jit(solution)/shard_map/ppermute | solution.py:410
  21.4 6.3 %collective-permute-start.6 = (bf16[4,64,128]{2,1,0:T(8,128)(2,1)S(1)}, bf16[4,64,128]{2,1,0:T(8,128)(2,1)S(1)}, u32[]{:S(2)}, u32[]{:S(2)}) collective-permute-start(bf16[4,64,128]{2,1,0:T(8,128)(2,1)S(1)} %pad_maximum_fusion.mine_ref), channel_id=1, source_target_pairs={{0,6},{1,7},{2,4},{3,5},{4,2},{5,3},{6,0},{7,1},{8,14},{9,15},{10,... | collective-permute-start | bytes 196616 | tf_op jit(solution)/shard_map/ppermute | solution.py:410
  21.5 14.4 %collective-permute-start.4 = (bf16[64,4096]{1,0:T(8,128)(2,1)}, bf16[64,4096]{1,0:T(8,128)(2,1)S(1)}, u32[]{:S(2)}, u32[]{:S(2)}) collective-permute-start(bf16[64,4096]{1,0:T(8,128)(2,1)} %get-tuple-element.23.own_ref), channel_id=1, source_target_pairs={{0,127},{1,2},{2,1},{3,4},{4,3},{5,6},{6,5},{7,8},{8,7},{9,10},{10... | collective-permute-start | bytes 1572872 | tf_op jit(solution)/shard_map/ppermute | solution.py:427
  23.4 21.7 %collective-permute-start.5 = (bf16[64,4096]{1,0:T(8,128)(2,1)}, bf16[64,4096]{1,0:T(8,128)(2,1)}, u32[]{:S(2)}, u32[]{:S(2)}) collective-permute-start(bf16[64,4096]{1,0:T(8,128)(2,1)} %get-tuple-element.23.own_ref), channel_id=1, source_target_pairs={{0,1},{1,0},{2,3},{3,2},{4,5},{5,4},{6,7},{7,6},{8,9},{9,8},{10,11... | collective-permute-start | bytes 1572872 | tf_op jit(solution)/shard_map/ppermute | solution.py:410
  27.7 23.0 %collective-permute-start.7 = (bf16[64,4096]{1,0:T(8,128)(2,1)}, bf16[64,4096]{1,0:T(8,128)(2,1)S(1)}, u32[]{:S(2)}, u32[]{:S(2)}) collective-permute-start(bf16[64,4096]{1,0:T(8,128)(2,1)} %basis_ref.1), channel_id=1, source_target_pairs={{0,127},{1,2},{2,1},{3,4},{4,3},{5,6},{6,5},{7,8},{8,7},{9,10},{10... | collective-permute-start | bytes 1572872 | tf_op jit(solution)/shard_map/ppermute | solution.py:427
  28.8 21.8 %collective-permute-start.8 = (bf16[64,4096]{1,0:T(8,128)(2,1)}, bf16[64,4096]{1,0:T(8,128)(2,1)S(1)}, u32[]{:S(2)}, u32[]{:S(2)}) collective-permute-start(bf16[64,4096]{1,0:T(8,128)(2,1)} %basis_ref.1), channel_id=1, source_target_pairs={{0,1},{1,0},{2,3},{3,2},{4,5},{5,4},{6,7},{7,6},{8,9},{9,8},{10,11... | collective-permute-start | bytes 1572872 | tf_op jit(solution)/shard_map/ppermute | solution.py:410
  29.0 21.7 %collective-permute-start.9 = (bf16[3,64,128]{2,1,0:T(8,128)(2,1)S(1)}, bf16[3,64,128]{2,1,0:T(8,128)(2,1)S(1)}, u32[]{:S(2)}, u32[]{:S(2)}) collective-permute-start(bf16[3,64,128]{2,1,0:T(8,128)(2,1)S(1)} %get-tuple-element.51), channel_id=1, source_target_pairs={{0,8},{1,9},{2,10},{3,11},{4,12},{5,13},{6,14},{7,15},{8,0},{9,1},... | collective-permute-start | bytes 147464 | tf_op jit(solution)/shard_map/ppermute | solution.py:421
  35.9 14.8 %collective-permute-start.10 = (bf16[3,64,128]{2,1,0:T(8,128)(2,1)S(1)}, bf16[3,64,128]{2,1,0:T(8,128)(2,1)S(1)}, u32[]{:S(2)}, u32[]{:S(2)}) collective-permute-start(bf16[3,64,128]{2,1,0:T(8,128)(2,1)S(1)} %get-tuple-element.50), channel_id=1, source_target_pairs={{0,120},{1,121},{2,122},{3,123},{4,124},{5,125},{6,126},{7,127},{8... | collective-permute-start | bytes 147464 | tf_op jit(solution)/shard_map/ppermute | solution.py:421
  45.0 5.7 %copy-start.4 = (bf16[64,4096]{1,0:T(8,128)(2,1)S(1)}, bf16[64,4096]{1,0:T(8,128)(2,1)}, u32[]{:S(2)}) copy-start(bf16[64,4096]{1,0:T(8,128)(2,1)} %basis_ref.1) | copy-start | bytes 1572868
  45.1 5.7 %copy-start.5 = (bf16[64,4096]{1,0:T(8,128)(2,1)S(1)}, bf16[64,4096]{1,0:T(8,128)(2,1)}, u32[]{:S(2)}) copy-start(bf16[64,4096]{1,0:T(8,128)(2,1)} %transfer_ref.1) | copy-start | bytes 1572868
  45.1 5.7 %copy-start.6 = (bf16[64,4096]{1,0:T(8,128)(2,1)S(1)}, bf16[64,4096]{1,0:T(8,128)(2,1)}, u32[]{:S(2)}) copy-start(bf16[64,4096]{1,0:T(8,128)(2,1)} %get-tuple-element.26.basis_ref) | copy-start | bytes 1572868
  45.1 5.7 %copy-start.7 = (bf16[64,4096]{1,0:T(8,128)(2,1)S(1)}, bf16[64,4096]{1,0:T(8,128)(2,1)}, u32[]{:S(2)}) copy-start(bf16[64,4096]{1,0:T(8,128)(2,1)} %get-tuple-element.27.transfer_ref) | copy-start | bytes 1572868
  45.1 5.7 %copy-start.10 = (bf16[2,2,64,64]{3,2,1,0:T(8,128)(2,1)S(1)}, bf16[2,2,64,64]{3,2,1,0:T(8,128)(2,1)}, u32[]{:S(2)}) copy-start(bf16[2,2,64,64]{3,2,1,0:T(8,128)(2,1)} %tree_ref.5) | copy-start | bytes 98308
  50.6 27.4 %copy-start.2 = (bf16[8,64,4096]{2,1,0:T(8,128)(2,1)S(1)}, bf16[8,64,4096]{2,1,0:T(8,128)(2,1)}, u32[]{:S(2)}) copy-start(bf16[8,64,4096]{2,1,0:T(8,128)(2,1)} %refs_0_.5) | copy-start | bytes 12582916
  56.1 26.8 %copy-start.3 = (bf16[8,64,4096]{2,1,0:T(8,128)(2,1)S(1)}, bf16[8,64,4096]{2,1,0:T(8,128)(2,1)}, u32[]{:S(2)}) copy-start(bf16[8,64,4096]{2,1,0:T(8,128)(2,1)} %refs_2_.1) | copy-start | bytes 12582916
  56.1 1.3 %collective-permute-start.13 = (bf16[3,64,128]{2,1,0:T(8,128)(2,1)S(1)}, bf16[3,64,128]{2,1,0:T(8,128)(2,1)S(1)}, u32[]{:S(2)}, u32[]{:S(2)}) collective-permute-start(bf16[3,64,128]{2,1,0:T(8,128)(2,1)S(1)} %get-tuple-element.32), channel_id=1, source_target_pairs={{0,1},{1,0},{2,3},{3,2},{4,5},{5,4},{6,7},{7,6},{8,9},{9,8},{10,11... | collective-permute-start | bytes 147464 | tf_op jit(solution)/shard_map/ppermute | solution.py:410
  57.5 4.2 %collective-permute-start.14 = (bf16[3,64,128]{2,1,0:T(8,128)(2,1)S(1)}, bf16[3,64,128]{2,1,0:T(8,128)(2,1)S(1)}, u32[]{:S(2)}, u32[]{:S(2)}) collective-permute-start(bf16[3,64,128]{2,1,0:T(8,128)(2,1)S(1)} %pad_maximum_fusion.7), channel_id=1, source_target_pairs={{0,2},{1,3},{2,0},{3,1},{4,6},{5,7},{6,4},{7,5},{8,10},{9,11},{10,... | collective-permute-start | bytes 147464 | tf_op jit(solution)/shard_map/ppermute | solution.py:410
  61.7 6.4 %collective-permute-start.15 = (bf16[4,64,128]{2,1,0:T(8,128)(2,1)S(1)}, bf16[4,64,128]{2,1,0:T(8,128)(2,1)S(1)}, u32[]{:S(2)}, u32[]{:S(2)}) collective-permute-start(bf16[4,64,128]{2,1,0:T(8,128)(2,1)S(1)} %pad_maximum_fusion.1.mine_ref), channel_id=1, source_target_pairs={{0,6},{1,7},{2,4},{3,5},{4,2},{5,3},{6,0},{7,1},{8,14},{9,15},{10,... | collective-permute-start | bytes 196616 | tf_op jit(solution)/shard_map/ppermute | solution.py:410
  63.9 14.1 %collective-permute-start.11 = (bf16[64,4096]{1,0:T(8,128)(2,1)S(1)}, bf16[64,4096]{1,0:T(8,128)(2,1)S(1)}, u32[]{:S(2)}, u32[]{:S(2)}) collective-permute-start(bf16[64,4096]{1,0:T(8,128)(2,1)S(1)} %get-tuple-element.28.own_ref), channel_id=1, source_target_pairs={{0,127},{1,2},{2,1},{3,4},{4,3},{5,6},{6,5},{7,8},{8,7},{9,10},{10... | collective-permute-start | bytes 1572872 | tf_op jit(solution)/shard_map/ppermute | solution.py:427
  68.1 9.9 %collective-permute-start.12 = (bf16[64,4096]{1,0:T(8,128)(2,1)S(1)}, bf16[64,4096]{1,0:T(8,128)(2,1)S(1)}, u32[]{:S(2)}, u32[]{:S(2)}) collective-permute-start(bf16[64,4096]{1,0:T(8,128)(2,1)S(1)} %get-tuple-element.28.own_ref), channel_id=1, source_target_pairs={{0,1},{1,0},{2,3},{3,2},{4,5},{5,4},{6,7},{7,6},{8,9},{9,8},{10,11... | collective-permute-start | bytes 1572872 | tf_op jit(solution)/shard_map/ppermute | solution.py:410
  68.2 21.6 %collective-permute-start.16 = (bf16[3,64,128]{2,1,0:T(8,128)(2,1)S(1)}, bf16[3,64,128]{2,1,0:T(8,128)(2,1)S(1)}, u32[]{:S(2)}, u32[]{:S(2)}) collective-permute-start(bf16[3,64,128]{2,1,0:T(8,128)(2,1)S(1)} %get-tuple-element.49), channel_id=1, source_target_pairs={{0,8},{1,9},{2,10},{3,11},{4,12},{5,13},{6,14},{7,15},{8,0},{9,1},... | collective-permute-start | bytes 147464 | tf_op jit(solution)/shard_map/ppermute | solution.py:421
  68.3 21.5 %collective-permute-start.17 = (bf16[3,64,128]{2,1,0:T(8,128)(2,1)S(1)}, bf16[3,64,128]{2,1,0:T(8,128)(2,1)S(1)}, u32[]{:S(2)}, u32[]{:S(2)}) collective-permute-start(bf16[3,64,128]{2,1,0:T(8,128)(2,1)S(1)} %get-tuple-element.48), channel_id=1, source_target_pairs={{0,120},{1,121},{2,122},{3,123},{4,124},{5,125},{6,126},{7,127},{8... | collective-permute-start | bytes 147464 | tf_op jit(solution)/shard_map/ppermute | solution.py:421
  82.9 6.9 %copy-start.13 = (bf16[3,3,64,64]{3,2,1,0:T(8,128)(2,1)S(1)}, bf16[3,3,64,64]{3,2,1,0:T(8,128)(2,1)}, u32[]{:S(2)}) copy-start(bf16[3,3,64,64]{3,2,1,0:T(8,128)(2,1)} %links_ref.3) | copy-start | bytes 221188
  94.1 1.3 %collective-permute-start.18 = (f32[64,128]{1,0:T(8,128)S(1)}, f32[64,128]{1,0:T(8,128)S(1)}, u32[]{:S(2)}, u32[]{:S(2)}) collective-permute-start(f32[64,128]{1,0:T(8,128)S(1)} %get-tuple-element.36), channel_id=1, source_target_pairs={{0,1},{1,0},{2,3},{3,2},{4,5},{5,4},{6,7},{7,6},{8,9},{9,8},{10,11... | collective-permute-start | bytes 98312 | tf_op jit(solution)/shard_map/ppermute | solution.py:410
  95.4 3.9 %collective-permute-start.19 = (f32[64,128]{1,0:T(8,128)S(1)}, f32[64,128]{1,0:T(8,128)S(1)}, u32[]{:S(2)}, u32[]{:S(2)}) collective-permute-start(f32[64,128]{1,0:T(8,128)S(1)} %add.138), channel_id=1, source_target_pairs={{0,2},{1,3},{2,0},{3,1},{4,6},{5,7},{6,4},{7,5},{8,10},{9,11},{10,... | collective-permute-start | bytes 98312 | tf_op jit(solution)/shard_map/ppermute | solution.py:410
  99.4 5.1 %collective-permute-start.20 = (f32[64,128]{1,0:T(8,128)S(1)}, f32[64,128]{1,0:T(8,128)S(1)}, u32[]{:S(2)}, u32[]{:S(2)}) collective-permute-start(f32[64,128]{1,0:T(8,128)S(1)} %add.139), channel_id=1, source_target_pairs={{0,6},{1,7},{2,4},{3,5},{4,2},{5,3},{6,0},{7,1},{8,14},{9,15},{10,... | collective-permute-start | bytes 98312 | tf_op jit(solution)/shard_map/ppermute | solution.py:410
  104.5 3.9 %collective-permute-start.21 = (f32[64,128]{1,0:T(8,128)S(1)}, f32[64,128]{1,0:T(8,128)S(1)}, u32[]{:S(2)}, u32[]{:S(2)}) collective-permute-start(f32[64,128]{1,0:T(8,128)S(1)} %add.140), channel_id=1, source_target_pairs={{0,8},{1,9},{2,10},{3,11},{4,12},{5,13},{6,14},{7,15},{8,0},{9,1},... | collective-permute-start | bytes 98312 | tf_op jit(solution)/shard_map/ppermute | solution.py:410
  108.4 12.4 %collective-permute-start.22 = (f32[64,128]{1,0:T(8,128)S(1)}, f32[64,128]{1,0:T(8,128)S(1)}, u32[]{:S(2)}, u32[]{:S(2)}) collective-permute-start(f32[64,128]{1,0:T(8,128)S(1)} %add.141), channel_id=1, source_target_pairs={{0,24},{1,25},{2,26},{3,27},{4,28},{5,29},{6,30},{7,31},{8,16},{9,... | collective-permute-start | bytes 98312 | tf_op jit(solution)/shard_map/ppermute | solution.py:410
  (6 other events, 25.1 us)

commit v3 on v2

--- a/solution.py
+++ b/solution.py
@@ -9,6 +9,7 @@
 LEAF = 64
 TILE = 128
 STEPS = 8
+STREAM = (True, False)
 bf16 = jnp.bfloat16
 f32 = jnp.float32
 highest = lax.Precision.HIGHEST
@@ -146,21 +147,35 @@
     return jnp.concatenate(rows, axis=0)
 
 
-def interact_kernel(index_ref, before_ref, own_ref, after_ref, *refs):
-    *bases, blocks_ref, out_ref, store_ref = refs
+def interact_kernel(index_ref, before_ref, own_ref, after_ref, *refs, streamed):
+    if streamed:
+        *bases, blocks_hbm, out_ref, store_ref, blocks_ref, sems = refs
+        wide = blocks_ref.shape[2] // STEPS
+
+        def piece(g):
+            at = (slice(None), slice(None), pl.ds(pl.multiple_of(g * wide, wide), wide))
+            return pltpu.make_async_copy(blocks_hbm.at[at], blocks_ref.at[at], sems.at[g])
+
+        for g in range(STEPS):
+            piece(g).start()
+    else:
+        *bases, blocks_ref, out_ref, store_ref = refs
     bases = (bases[0], None, bases[1]) if bases else (None, None, None)
     fill_store(store_ref, (before_ref, own_ref, after_ref), bases)
     low = low_half((LEAF, TILE))
+    per = own_ref.shape[1] // TILE // STEPS
 
     def step(g, carry):
-        for u in range(4):
-            pair = g * 4 + u
+        if streamed:
+            piece(g).wait()
+        for u in range(per):
+            pair = g * per + u
             blocks = blocks_ref[:, :, lanes(pair)].reshape(8 * LEAF, TILE)
             both = dot(gathered(store_ref, index_ref, pair, low), blocks)
             out_ref[:, lanes(pair)] = jnp.where(low, both[:LEAF], both[LEAF:])
         return carry
 
-    lax.fori_loop(0, own_ref.shape[1] // TILE // 4, step, 0)
+    lax.fori_loop(0, STEPS, step, 0)
 
 
 def descend(scal_ref, mine_ref, other_ref, first_ref, second_ref, tree_ref, links_ref):
@@ -173,12 +188,14 @@
     def high_group(n):
         return jnp.where(b2 == 0, other_ref[n], mine_ref[n])
 
+    crossed = (odd == 1) == (b0 == 0)
+
     def left(n):
-        tile = jnp.where(odd == 1, first_ref[n], second_ref[n])
+        tile = jnp.where(crossed, first_ref[n], second_ref[n])
         return jnp.where(has_left == 1, tile, jnp.zeros_like(tile))
 
     def right(n):
-        tile = jnp.where(odd == 1, second_ref[n], first_ref[n])
+        tile = jnp.where(crossed, second_ref[n], first_ref[n])
         return jnp.where(has_right == 1, tile, jnp.zeros_like(tile))
 
     def pick(j, options):
@@ -223,17 +240,19 @@
 
 def inner_kernel(
     scal_ref, near_ref, far_ref, basis_ref, transfer_ref,
-    mine_ref, other_ref, first_ref, second_ref, tree_ref, links_ref, next_tree_ref, next_basis_ref, next_transfer_ref,
-    middle_ref, coords_ref, pay_ref, coeffs_ref,
+    mine_ref, other_ref, first_ref, second_ref, tree_ref, links_ref,
+    middle_ref, coeffs_ref,
 ):
     descent = descend(scal_ref, mine_ref, other_ref, first_ref, second_ref, tree_ref, links_ref)
     finish(near_ref, far_ref, basis_ref, transfer_ref, descent, coeffs_ref, middle_ref)
 
-    def next_coords(at):
-        coords_ref[:, at] = dot(middle_ref[:, at], two_blocks(next_basis_ref[:, at]), NT).astype(bf16)
-
-    by_tiles(middle_ref.shape[1] // TILE, next_coords)
-    coarse_payload(node_sums(coords_ref, next_transfer_ref), next_tree_ref, scal_ref, pay_ref)
+
+def next_kernel(scal_ref, tree_ref, rows_ref, basis_ref, transfer_ref, coords_ref, pay_ref):
+    def coords(at):
+        coords_ref[:, at] = dot(rows_ref[:, at], two_blocks(basis_ref[:, at]), NT).astype(bf16)
+
+    by_tiles(rows_ref.shape[1] // TILE, coords)
+    coarse_payload(node_sums(coords_ref, transfer_ref), tree_ref, scal_ref, pay_ref)
 
 
 def outer_kernel(
@@ -274,7 +293,7 @@
     lax.fori_loop(0, count // unroll, step, 0)
 
 
-def eliminate(work_ref, tee_ref):
+def eliminate(work_ref, tee_ref, first=0, last=LEAF // 8):
     count = work_ref.shape[0]
     per = min(count, 4)
     groups = count // per
@@ -282,7 +301,7 @@
     lane = lax.broadcasted_iota(jnp.int32, (8, TILE), 1)
     col, half = lane % LEAF, lane // LEAF
     panels = LEAF // 8
-    for kb in range(panels):
+    for kb in range(first, last):
         base = kb * 8
         rows = slice(base, base + 8)
         inside = (col >= base) & (col < base + 8)
@@ -328,17 +347,19 @@
         if kb == panels - 1:
             break
 
+        rest_rows = LEAF - base - 8
+
         def update(t):
             left = work_ref[t, rows, :]
             right = jnp.where(inside & (col > base + sub), 0.0, left)
-            left = stacked(left, (0, 0, 1))
-            right = stacked(right, (0, 1, 0))
-            both = lax.dot_general(left, right, (((0,), (0,)), ((), ())), preferred_element_type=f32)
+            turned = stacked(left, (0, 0, 1)).T.astype(bf16)
+            turned = jnp.concatenate([turned[base + 8 : LEAF], turned[LEAF + base + 8 :]], axis=0)
+            both = dot(turned, stacked(right, (0, 1, 0)).astype(bf16))
             for ib in range(kb + 1, panels):
                 at = slice(ib * 8, ib * 8 + 8)
-                other = slice(LEAF + ib * 8, LEAF + ib * 8 + 8)
+                n = (ib - kb - 1) * 8
                 rest = jnp.where(inside, 0.0, work_ref[t, at, :])
-                work_ref[t, at, :] = rest - jnp.where(half == 0, both[at], both[other])
+                work_ref[t, at, :] = rest - jnp.where(half == 0, both[n : n + 8], both[rest_rows + n : rest_rows + n + 8])
 
         each(count, 4, update)
 
@@ -346,7 +367,7 @@
 def stacked(x, order):
     high = x.astype(bf16).astype(f32)
     pieces = (high, x - high)
-    return jnp.concatenate([pieces[n] for n in order] + [jnp.zeros_like(x)], axis=0).astype(bf16)
+    return jnp.concatenate([pieces[n] for n in order] + [jnp.zeros_like(x)], axis=0)
 
 
 def parts(tile):
@@ -355,10 +376,12 @@
     return row, col
 
 
-def pair_kernel(gram_ref, samples_ref, work_ref, basis_ref, *scratch):
-    work_ref[...] = gram_ref[...]
-    eliminate(work_ref, *scratch)
-
+def pair_kernel(before_ref, work_ref, tee_ref, *, first, last):
+    work_ref[...] = before_ref[...]
+    eliminate(work_ref, tee_ref, first, last)
+
+
+def solve_kernel(work_ref, samples_ref, basis_ref):
     def solve(t):
         tile = work_ref[t]
         row, col = parts(tile)
@@ -371,9 +394,60 @@
     each(work_ref.shape[0], 4, solve)
 
 
-def group_kernel(gram_ref, work_ref, out_ref, own_ref, *scratch, scale):
+def eliminate_few(load, save, count):
+    shape = (count, 8, TILE)
+    sub = lax.broadcasted_iota(jnp.int32, shape, 1)
+    lane = lax.broadcasted_iota(jnp.int32, shape, 2)
+    low = lane < LEAF
+    col = lane % LEAF
+    panels = LEAF // 8
+    for kb in range(panels):
+        panel = load(kb)
+        cols = []
+        for j in range(8):
+            k = kb * 8 + j
+            one = jnp.broadcast_to(panel[:, :, k : k + 1], shape)
+            two = jnp.broadcast_to(panel[:, :, LEAF + k : LEAF + k + 1], shape)
+            cols.append(jnp.where(low, one, two))
+        rows = []
+        for j in range(8):
+            k = kb * 8 + j
+            inv = lax.rsqrt(cols[j][:, j : j + 1, :])
+            lower = cols[j] * inv
+            for n in range(j + 1, 8):
+                cols[n] = cols[n] - lower * lower[:, n : n + 1, :]
+            row = jnp.where(col[:, :1] == k, inv, panel[:, j : j + 1, :] * inv)
+            below = sub > j
+            kept = jnp.where(below & (col == k), 0.0, panel)
+            panel = jnp.where(sub == j, row, kept - jnp.where(below, lower, 0.0) * row)
+            rows.append(row)
+        save(kb, panel)
+        if kb == panels - 1:
+            break
+        turned = jnp.swapaxes(panel, 1, 2)
+        inside = (col >= kb * 8) & (col < kb * 8 + 8)
+        for j in range(8):
+            k = kb * 8 + j
+            rows[j] = jnp.where((col[:, :1] > k) & (col[:, :1] < kb * 8 + 8), 0.0, rows[j])
+        for ib in range(kb + 1, panels):
+            rest = jnp.where(inside, 0.0, load(ib))
+            for j in range(8):
+                one = jnp.broadcast_to(turned[:, ib * 8 : ib * 8 + 8, j : j + 1], shape)
+                two = jnp.broadcast_to(turned[:, LEAF + ib * 8 : LEAF + ib * 8 + 8, j : j + 1], shape)
+                rest = rest - jnp.where(low, one, two) * rows[j]
+            save(ib, rest)
+
+
+def group_kernel(gram_ref, work_ref, out_ref, own_ref, *, scale):
     own_ref[0] = gram_ref[...] / scale
-    eliminate(own_ref, *scratch)
+
+    def load(b):
+        return own_ref[:, b * 8 : b * 8 + 8, :]
+
+    def save(b, value):
+        own_ref[:, b * 8 : b * 8 + 8, :] = value
+
+    eliminate_few(load, save, 1)
     tile = own_ref[0]
     row, col = parts(tile)
     inverse = jnp.where(col <= row, tile, 0.0)
@@ -410,14 +484,12 @@
     return lax.ppermute(x, AXES, [(i, i ^ mask) for i in range(count)])
 
 
-def neighbours(x, width, second):
+def adjacent_rows(x):
     count = lax.axis_size(AXES)
-    blocks = count // width
     route = []
-    for b in range(blocks):
-        forward = (b % 2 == 0) != second
-        to = (b + 1 if forward else b - 1) % blocks
-        route += [(b * width + m, to * width + m) for m in range(width)]
+    for i in range(count):
+        forward = (i // 8 % 2 == 0) == (i % 2 == 0)
+        route.append((i, (i + 8 if forward else i - 8) % count))
     return lax.ppermute(x, AXES, route)
 
 
@@ -453,7 +525,7 @@
     return jnp.stack([first, second, halves(b1, stage[1], other[1]), stage[2] + other[2]])
 
 
-def coarse_far(mine, other, node):
+def far_payload(mine, other, node):
     low = low_half((LEAF, TILE))
     b2, odd = node // 4 % 2, node // 8 % 2
     top = jnp.where(low == (b2 == 0), mine[3], other[3])
@@ -461,9 +533,7 @@
     hi = jnp.where(b2 == 0, other, mine)
     rightward = jnp.stack([top, hi[2], hi[1]])
     leftward = jnp.stack([top, lo[2], lo[0]])
-    one = neighbours(jnp.where(odd == 0, rightward, leftward), 8, False)
-    two = neighbours(jnp.where(odd == 0, leftward, rightward), 8, True)
-    return one, two
+    return jnp.where((odd == 0) == (node % 2 == 0), rightward, leftward)
 
 
 def after(x, *values):
@@ -504,14 +574,17 @@
     near_table = leaf_table(near_index, node)
     far_table = leaf_table(far_index, node)
 
-    def interact(index, rows, blocks, bases=()):
+    def interact(index, rows, blocks, bases=(), streamed=False):
+        scratch = [pltpu.VMEM((3 * width // LEAF, LEAF, TILE), bf16)]
+        if streamed:
+            scratch += [pltpu.VMEM(blocks.shape, bf16), pltpu.SemaphoreType.DMA((STEPS,))]
         return pl.pallas_call(
-            interact_kernel,
-            in_specs=[SMEM] + [VMEM] * (4 + len(bases)),
+            lambda *refs: interact_kernel(*refs, streamed=streamed),
+            in_specs=[SMEM] + [VMEM] * (3 + len(bases)) + [HBM if streamed else VMEM],
             out_specs=VMEM,
             out_shape=struct((LEAF, width), f32),
-            scratch_shapes=[pltpu.VMEM((3 * width // LEAF, LEAF, TILE), bf16)],
-            compiler_params=params(6),
+            scratch_shapes=scratch,
+            compiler_params=params(56 if streamed else 6),
             name="interact",
         )(index, *rows, *bases, blocks)
 
@@ -530,31 +603,43 @@
         name="coords",
     )(scal, inner_tree, probes, inner_basis, inner_transfer)
     mine = coarse_near(pay, node)
+    mine, near_table, far_table = lax.optimization_barrier((mine, near_table, far_table))
     other = swap(mine, 6)
     coords_b, coords_a = node_halo(after(coords, mine))
-    one, two = coarse_far(mine, other, node)
-    basis_b, basis_a = node_halo(after(outer_basis, other))
-    near_part = interact(near_table, (rows_b, rows, rows_a), inner_near)
-    far_part = interact(far_table, (coords_b, coords, coords_a), inner_far)
+    basis_b, basis_a = node_halo(after(outer_basis, mine))
+    near_part = interact(near_table, (rows_b, after(rows, mine), rows_a), inner_near, streamed=STREAM[0])
+    other, near_part = lax.optimization_barrier((other, near_part))
+    one = adjacent_rows(far_payload(mine, other, node))
+    far_part = interact(far_table, (coords_b, coords, coords_a), inner_far, streamed=STREAM[1])
     far_part, basis_b, basis_a = lax.optimization_barrier((far_part, basis_b, basis_a))
-    middle, coords, pay = pl.pallas_call(
+    one, far_part = lax.optimization_barrier((one, far_part))
+    two = swap(one, 1)
+    middle = pl.pallas_call(
         inner_kernel,
-        in_specs=[SMEM] + [VMEM] * 13,
-        out_specs=(VMEM,) * 3,
-        out_shape=(row, row, payload),
+        in_specs=[SMEM] + [VMEM] * 10,
+        out_specs=VMEM,
+        out_shape=row,
         scratch_shapes=[pltpu.VMEM((LEAF, width), bf16)],
         compiler_params=params(6),
         name="inner",
-    )(
-        scal, near_part, far_part, basis, transfer,
-        mine, other, one, two, inner_tree, inner_links, outer_tree, outer_basis, outer_transfer,
-    )
+    )(scal, near_part, far_part, basis, transfer, mine, other, one, two, inner_tree, inner_links)
     middle_b, middle_a = node_halo(middle)
+    coords, pay = pl.pallas_call(
+        next_kernel,
+        in_specs=[SMEM] + [VMEM] * 4,
+        out_specs=(VMEM, VMEM),
+        out_shape=(row, payload),
+        compiler_params=params(6),
+        name="next",
+    )(scal, outer_tree, after(middle, middle_a), outer_basis, outer_transfer)
     mine = coarse_near(pay, node)
     other = swap(mine, 6)
-    one, two = coarse_far(mine, other, node)
-    near_part = interact(near_table, (middle_b, middle, middle_a), outer_near)
+    near_part = interact(near_table, (middle_b, after(middle, mine), middle_a), outer_near)
+    other, near_part = lax.optimization_barrier((other, near_part))
+    one = adjacent_rows(far_payload(mine, other, node))
     far_part = interact(far_table, (middle_b, coords, middle_a), outer_far, (basis_b, basis_a))
+    one, far_part = lax.optimization_barrier((one, far_part))
+    two = swap(one, 1)
     samples, grams, gram = pl.pallas_call(
         outer_kernel,
         in_specs=[SMEM] + [VMEM] * 10,
@@ -568,24 +653,40 @@
         compiler_params=params(6),
         name="outer",
     )(scal, near_part, far_part, outer_basis, outer_transfer, mine, other, one, two, outer_tree, outer_links)
-    for mask in (1, 2, 6, 8, 24):
-        gram = gram + swap(gram, mask)
-    work, pair_basis = pl.pallas_call(
-        pair_kernel,
+    def piece(n, work):
+        return pl.pallas_call(
+            lambda *refs: pair_kernel(*refs, first=2 * n, last=2 * n + 2),
+            in_specs=[VMEM],
+            out_specs=VMEM,
+            out_shape=struct(work.shape, f32),
+            scratch_shapes=elimination(pairs // 2),
+            input_output_aliases={0: 0},
+            compiler_params=params(6),
+            name="pairs",
+        )(work)
+
+    work = grams
+    for n, mask in enumerate((1, 2, 6, 8)):
+        other = swap(gram, mask)
+        work = piece(n, work)
+        gram, work = lax.optimization_barrier((gram + other, work))
+    other = swap(gram, 24)
+    pair_basis = pl.pallas_call(
+        solve_kernel,
         in_specs=[VMEM, VMEM],
-        out_specs=(VMEM, VMEM),
-        out_shape=(struct(grams.shape, f32), struct((LEAF, width), f32)),
-        scratch_shapes=elimination(pairs // 2),
+        out_specs=VMEM,
+        out_shape=struct((LEAF, width), f32),
         compiler_params=params(6),
-        name="pairs",
-    )(grams, samples)
+        name="solve",
+    )(work, samples)
+    gram = gram + other
     scale = pairs * lax.axis_size("leaf")
     group_basis = pl.pallas_call(
         lambda *refs: group_kernel(*refs, scale=scale),
         in_specs=[VMEM, VMEM],
         out_specs=VMEM,
         out_shape=struct((LEAF, pairs * LEAF), f32),
-        scratch_shapes=[pltpu.VMEM((1, LEAF, TILE), f32)] + elimination(1),
+        scratch_shapes=[pltpu.VMEM((1, LEAF, TILE), f32)],
         compiler_params=params(6),
         name="group",
     )(gram, work)

time: 127 us -> 112 us (0.88)
  waiting for transfers between devices: 40.8 us -> 22.9 us
  starting transfers between devices: 23.6 us -> 27.7 us
  local copies, waits for them, and re-layouts: 4.34 us -> 1.66 us
  Pallas kernels: 54.5 us -> 56.9 us
    ppermute x15 -> x17, waiting for transfers between devices: 28.8 us -> 19.4 us  [swap(): return lax.ppermute(x, AXES, [(i, i ^ mask) for i in range(count)])]
    ppermute x4, waiting for transfers between devices: 12 us -> 3.54 us  [node_halo(): return (lax.ppermute(x, AXES, route), swap(x, 1))]
    ppermute x4, starting transfers between devices: 15.6 us -> 20.1 us  [node_halo(): return (lax.ppermute(x, AXES, route), swap(x, 1))]
    ppermute x4 -> x2, starting transfers between devices: 4.72 us -> 0.17 us  [adjacent_rows(): return lax.ppermute(x, AXES, route)]
    ppermute x15 -> x17, starting transfers between devices: 3.32 us -> 7.44 us  [swap(): return lax.ppermute(x, AXES, [(i, i ^ mask) for i in range(count)])]
    unnamed x30 -> x34, local copies, waits for them, and re-layouts: 3.31 us -> 0.1 us
    pallas_call x6 -> x11, Pallas kernels: 39.8 us -> 42.8 us  [the longest x4 23.4 us: interact(): pl.pallas_call(lambda *refs: interact_kernel(*refs, streamed=streamed), i...]
  transfers between devices with their start and end apart: 23 -> 23, of which waited for: 11 -> 11; matrix products, arithmetic and copies ran while one was open for 2% -> 3% of each run, Pallas kernels for 31% -> 38%
where the time goes in v3:
time: 112 us
  Pallas kernels  56.9 us (51%)
  starting transfers between devices  27.7 us (25%)
  waiting for transfers between devices  22.9 us (20%)
  other arithmetic  1.73 us (2%)
  local copies, waits for them, and re-layouts  1.66 us (1%)
  between operations  1.26 us (1%)
    pallas_call x4, Pallas kernels, interact(): pl.pallas_call(lambda *refs: interact_kernel(*refs, streamed=streamed), i...  23.4 us
    ppermute x4, starting transfers between devices, node_halo(): return (lax.ppermute(x, AXES, route), swap(x, 1))  20.1 us
    ppermute x17, waiting for transfers between devices, swap(): return lax.ppermute(x, AXES, [(i, i ^ mask) for i in range(count)])  19.4 us
    pallas_call x4, Pallas kernels, piece(): pl.pallas_call(lambda *refs: pair_kernel(*refs, first=2 * n, last=2 * n +...  11.5 us
    ppermute x17, starting transfers between devices, swap(): return lax.ppermute(x, AXES, [(i, i ^ mask) for i in range(count)])  7.44 us
    pallas_call x1, Pallas kernels, local(): pl.pallas_call(coords_kernel, in_specs=[SMEM, VMEM, HBM, HBM, HBM], out_s...  5.13 us
    pallas_call x1, Pallas kernels, local(): pl.pallas_call(lambda *refs: group_kernel(*refs, scale=scale), in_specs=[...  4.61 us
    pallas_call x1, Pallas kernels, local(): pl.pallas_call(outer_kernel, in_specs=[SMEM] + [VMEM] * 10, out_specs=(VM...  4.31 us
  transfers between devices with their start and end apart: 23, of which 11 were waited for; matrix products, arithmetic and copies ran while one was open for 3% of the time, Pallas kernels for 38%

profile of v3, /device:TPU:0, one launch (start us, length us, event | category | flops | bytes accessed | tf_op | source)
XLA Modules:
  0.0 112.1 jit_solution(8985912685453753272)
XLA Ops:
  0.7 8.9 %collective-permute-start.3 = (bf16[64,4096]{1,0:T(8,128)(2,1)}, bf16[64,4096]{1,0:T(8,128)(2,1)S(1)}, u32[]{:S(2)}, u32[]{:S(2)}) collective-permute-start(bf16[64,4096]{1,0:T(8,128)(2,1)} %probes_hbm.1), channel_id=1, source_target_pairs={{0,127},{1,2},{2,1},{3,4},{4,3},{5,6},{6,5},{7,8},{8,7},{9,10},{10... | collective-permute-start | bytes 1572872 | tf_op jit(solution)/shard_map/ppermute | solution.py:499
  10.2 5.1 %coords.1 = (bf16[64,4096]{1,0:T(8,128)(2,1)}, bf16[3,64,128]{2,1,0:T(8,128)(2,1)}, bf16[64,4096]{1,0:T(8,128)(2,1)}, bf16[64,4096]{1,0:T(8,128)(2,1)}, bf16[64,4096]{1,0:T(8,128)(2,1)}) custom-call(s32[6]{0:T(128)} %stack.77.scal_ref, bf16[2,2,64,64]{3,2,1,0:T(8,128)(2,1)} %tree_ref.5, bf16[64,4096]{1,0:T(8,128)(2,1)} %probes_hbm.1, ...), custom_call_target="tpu_custom_call" | custom-call | tf_op jit(solution)/shard_map/coords/pallas_call | solution.py:596
  15.5 0.8 fusion.10
  16.9 0.8 slice_select_fusion.3
  17.9 0.7 reshape.60.refs_0_
  18.7 3.1 %collective-permute-done.1 = bf16[3,64,128]{2,1,0:T(8,128)(2,1)S(1)} collective-permute-done((bf16[3,64,128]{2,1,0:T(8,128)(2,1)S(1)}, bf16[3,64,128]{2,1,0:T(8,128)(2,1)S(1)}, u32[]{:S(2)}, u32[]{:S(2)}) %collective-permute-start.1) | collective-permute-done | bytes 49184 | tf_op jit(solution)/shard_map/ppermute | solution.py:484
  22.1 3.4 %collective-permute-start.6 = (bf16[64,4096]{1,0:T(8,128)(2,1)}, bf16[64,4096]{1,0:T(8,128)(2,1)S(1)}, u32[]{:S(2)}, u32[]{:S(2)}) collective-permute-start(bf16[64,4096]{1,0:T(8,128)(2,1)} %get-tuple-element.48.refs_2_), channel_id=1, source_target_pairs={{0,127},{1,2},{2,1},{3,4},{4,3},{5,6},{6,5},{7,8},{8,7},{9,10},{10... | collective-permute-start | bytes 1572872 | tf_op jit(solution)/shard_map/ppermute | solution.py:499
  25.5 3.9 %collective-permute-start.8 = (bf16[64,4096]{1,0:T(8,128)(2,1)}, bf16[64,4096]{1,0:T(8,128)(2,1)S(1)}, u32[]{:S(2)}, u32[]{:S(2)}) collective-permute-start(bf16[64,4096]{1,0:T(8,128)(2,1)} %basis_ref.3), channel_id=1, source_target_pairs={{0,127},{1,2},{2,1},{3,4},{4,3},{5,6},{6,5},{7,8},{8,7},{9,10},{10... | collective-permute-start | bytes 1572872 | tf_op jit(solution)/shard_map/ppermute | solution.py:499
  29.4 6.8 %interact.4.near_ref = f32[64,4096]{1,0:T(8,128)} custom-call(s32[512]{0:T(512)} %reshape.60.refs_0_, bf16[64,4096]{1,0:T(8,128)(2,1)} %copy-done.16, bf16[64,4096]{1,0:T(8,128)(2,1)} %get-tuple-element.43.refs_2_, bf16[64,4096]{1,0:T(8,128)(2,1)} %copy-done.15, bf16[8,64,4096]{2,1,0:T(8,128)(2,1)} %refs_4_.3), custom_call_target="tpu_custom_call" | custom-call | tf_op jit(solution)/shard_map/interact/pallas_call | solution.py:581
  36.6 4.9 %interact.5.far_ref = f32[64,4096]{1,0:T(8,128)S(1)} custom-call(s32[512]{0:T(512)S(1)} %reshape.61.refs_0_, bf16[64,4096]{1,0:T(8,128)(2,1)S(1)} %collective-permute-done.6.refs_1_, bf16[64,4096]{1,0:T(8,128)(2,1)S(1)} %copy-done.8, bf16[64,4096]{1,0:T(8,128)(2,1)S(1)} %collective-permute-done.7.refs_3_, bf16[8,64,4096]{2,1,0:T(8,128)(2,1)S(1)} %copy-done), custom_call_target="tpu_custom_call" | custom-call | tf_op jit(solution)/shard_map/interact/pallas_call | solution.py:581
  42.4 1.0 collective-permute-done.10.second_ref
  43.4 3.0 %inner.1.rows_ref.refs_2_ = bf16[64,4096]{1,0:T(8,128)(2,1)S(1)} custom-call(s32[6]{0:T(128)S(1)} %copy-done.14, f32[64,4096]{1,0:T(8,128)S(1)} %copy-done.3, f32[64,4096]{1,0:T(8,128)S(1)} %interact.5.far_ref, bf16[64,4096]{1,0:T(8,128)(2,1)S(1)} %copy-done.6, bf16[64,4096]{1,0:T(8,128)(2,1)S(1)} %copy-done.7, ...), custom_call_target="tpu_custom_call" | custom-call | tf_op jit(solution)/shard_map/inner/pallas_call | solution.py:617
  46.7 1.7 %collective-permute-done.11.refs_3_ = bf16[64,4096]{1,0:T(8,128)(2,1)S(1)} collective-permute-done((bf16[64,4096]{1,0:T(8,128)(2,1)S(1)}, bf16[64,4096]{1,0:T(8,128)(2,1)S(1)}, u32[]{:S(2)}, u32[]{:S(2)}) %collective-permute-start.11) | collective-permute-done | bytes 524320 | tf_op jit(solution)/shard_map/ppermute | solution.py:484
  48.4 2.9 %next.1 = (bf16[64,4096]{1,0:T(8,128)(2,1)S(1)}, bf16[3,64,128]{2,1,0:T(8,128)(2,1)S(1)}) custom-call(s32[6]{0:T(128)S(1)} %copy-done.14, bf16[2,2,64,64]{3,2,1,0:T(8,128)(2,1)S(1)} %copy-done.10, bf16[64,4096]{1,0:T(8,128)(2,1)S(1)} %inner.1.rows_ref.refs_2_, bf16[64,4096]{1,0:T(8,128)(2,1)S(1)} %copy-done.4, bf16[64,4096]{1,0:T(8,128)(2,1)S(1)} %copy-done.5), custom_call_target="tpu_custom_call" | custom-call | tf_op jit(solution)/shard_map/next/pallas_call | solution.py:627
  51.6 3.9 %collective-permute-start.15 = (bf16[64,4096]{1,0:T(8,128)(2,1)S(1)}, bf16[64,4096]{1,0:T(8,128)(2,1)S(1)}, u32[]{:S(2)}, u32[]{:S(2)}) collective-permute-start(bf16[64,4096]{1,0:T(8,128)(2,1)S(1)} %inner.1.rows_ref.refs_2_), channel_id=1, source_target_pairs={{0,127},{1,2},{2,1},{3,4},{4,3},{5,6},{6,5},{7,8},{8,7},{9,10},{10... | collective-permute-start | bytes 1572872 | tf_op jit(solution)/shard_map/ppermute | solution.py:499
  55.7 6.1 %collective-permute-done.13 = bf16[3,64,128]{2,1,0:T(8,128)(2,1)S(1)} collective-permute-done((bf16[3,64,128]{2,1,0:T(8,128)(2,1)S(1)}, bf16[3,64,128]{2,1,0:T(8,128)(2,1)S(1)}, u32[]{:S(2)}, u32[]{:S(2)}) %collective-permute-start.13) | collective-permute-done | bytes 49184 | tf_op jit(solution)/shard_map/ppermute | solution.py:484
  61.8 1.0 collective-permute-start.14
  62.8 2.9 %collective-permute-done.15.refs_1_ = bf16[64,4096]{1,0:T(8,128)(2,1)S(1)} collective-permute-done((bf16[64,4096]{1,0:T(8,128)(2,1)S(1)}, bf16[64,4096]{1,0:T(8,128)(2,1)S(1)}, u32[]{:S(2)}, u32[]{:S(2)}) %collective-permute-start.15) | collective-permute-done | bytes 524320 | tf_op jit(solution)/shard_map/ppermute | solution.py:499
  65.7 4.8 %interact.6.near_ref = f32[64,4096]{1,0:T(8,128)S(1)} custom-call(s32[512]{0:T(512)S(1)} %copy-done.13, bf16[64,4096]{1,0:T(8,128)(2,1)S(1)} %collective-permute-done.15.refs_1_, bf16[64,4096]{1,0:T(8,128)(2,1)S(1)} %inner.1.rows_ref.refs_2_, bf16[64,4096]{1,0:T(8,128)(2,1)S(1)} %collective-permute-done.11.refs_3_, bf16[8,64,4096]{2,1,0:T(8,128)(2,1)S(1)} %copy-done.1), custom_call_target="tpu_custom_call" | custom-call | tf_op jit(solution)/shard_map/interact/pallas_call | solution.py:581
  70.7 6.9 %interact.7.far_ref = f32[64,4096]{1,0:T(8,128)S(1)} custom-call(s32[512]{0:T(512)S(1)} %reshape.61.refs_0_, bf16[64,4096]{1,0:T(8,128)(2,1)S(1)} %collective-permute-done.15.refs_1_, bf16[64,4096]{1,0:T(8,128)(2,1)S(1)} %get-tuple-element.60.refs_2_, bf16[64,4096]{1,0:T(8,128)(2,1)S(1)} %collective-permute-done.11.refs_3_, ...), custom_call_target="tpu_custom_call" | custom-call | tf_op jit(solution)/shard_map/interact/pallas_call | solution.py:581
  77.7 1.2 %collective-permute-done.17.second_ref = bf16[3,64,128]{2,1,0:T(8,128)(2,1)S(1)} collective-permute-done((bf16[3,64,128]{2,1,0:T(8,128)(2,1)S(1)}, bf16[3,64,128]{2,1,0:T(8,128)(2,1)S(1)}, u32[]{:S(2)}, u32[]{:S(2)}) %collective-permute-start.17) | collective-permute-done | bytes 49184 | tf_op jit(solution)/shard_map/ppermute | solution.py:484
  78.9 4.3 %outer.1 = (f32[64,4096]{1,0:T(8,128)S(1)}, f32[16,64,128]{2,1,0:T(8,128)S(1)}, f32[64,128]{1,0:T(8,128)S(1)}) custom-call(s32[6]{0:T(128)S(1)} %copy-done.14, f32[64,4096]{1,0:T(8,128)S(1)} %interact.6.near_ref, f32[64,4096]{1,0:T(8,128)S(1)} %interact.7.far_ref, bf16[64,4096]{1,0:T(8,128)(2,1)S(1)} %copy-done.4, bf16[64,4096]{1,0:T(8,128)(2,1)S(1)} %copy-done.5, ...), custom_call_target="tpu_custom_call" | custom-call | tf_op jit(solution)/shard_map/outer/pallas_call | solution.py:643
  83.5 3.2 %pairs.4.refs_0_ = f32[16,64,128]{2,1,0:T(8,128)S(1)} custom-call(f32[16,64,128]{2,1,0:T(8,128)S(1)} %get-tuple-element.66.refs_0_), custom_call_target="tpu_custom_call", output_to_operand_aliasing={{}: (0, {})} | custom-call | tf_op jit(solution)/shard_map/pairs/pallas_call | solution.py:657
  87.0 3.2 %pairs.5.refs_0_ = f32[16,64,128]{2,1,0:T(8,128)S(1)} custom-call(f32[16,64,128]{2,1,0:T(8,128)S(1)} %pairs.4.refs_0_), custom_call_target="tpu_custom_call", output_to_operand_aliasing={{}: (0, {})} | custom-call | tf_op jit(solution)/shard_map/pairs/pallas_call | solution.py:657
  90.2 0.7 collective-permute-done.19
  90.9 4.4 %collective-permute-start.20 = (f32[64,128]{1,0:T(8,128)S(1)}, f32[64,128]{1,0:T(8,128)S(1)}, u32[]{:S(2)}, u32[]{:S(2)}) collective-permute-start(f32[64,128]{1,0:T(8,128)S(1)} %add.139), channel_id=1, source_target_pairs={{0,6},{1,7},{2,4},{3,5},{4,2},{5,3},{6,0},{7,1},{8,14},{9,15},{10,... | collective-permute-start | bytes 98312 | tf_op jit(solution)/shard_map/ppermute | solution.py:484
  95.3 3.0 %pairs.6.refs_0_ = f32[16,64,128]{2,1,0:T(8,128)S(1)} custom-call(f32[16,64,128]{2,1,0:T(8,128)S(1)} %pairs.5.refs_0_), custom_call_target="tpu_custom_call", output_to_operand_aliasing={{}: (0, {})} | custom-call | tf_op jit(solution)/shard_map/pairs/pallas_call | solution.py:657
  98.5 2.1 %pairs.7.work_ref.refs_1_ = f32[16,64,128]{2,1,0:T(8,128)S(1)} custom-call(f32[16,64,128]{2,1,0:T(8,128)S(1)} %pairs.6.refs_0_), custom_call_target="tpu_custom_call", output_to_operand_aliasing={{}: (0, {})} | custom-call | tf_op jit(solution)/shard_map/pairs/pallas_call | solution.py:657
  100.6 1.8 %collective-permute-done.21 = f32[64,128]{1,0:T(8,128)S(1)} collective-permute-done((f32[64,128]{1,0:T(8,128)S(1)}, f32[64,128]{1,0:T(8,128)S(1)}, u32[]{:S(2)}, u32[]{:S(2)}) %collective-permute-start.21) | collective-permute-done | bytes 32800 | tf_op jit(solution)/shard_map/ppermute | solution.py:484
  102.4 2.0 %solve.1 = f32[64,4096]{1,0:T(8,128)} custom-call(f32[16,64,128]{2,1,0:T(8,128)S(1)} %pairs.7.work_ref.refs_1_, f32[64,4096]{1,0:T(8,128)S(1)} %get-tuple-element.74.samples_ref), custom_call_target="tpu_custom_call" | custom-call | tf_op jit(solution)/shard_map/solve/pallas_call | solution.py:674
  104.4 3.1 %collective-permute-done.22 = f32[64,128]{1,0:T(8,128)S(1)} collective-permute-done((f32[64,128]{1,0:T(8,128)S(1)}, f32[64,128]{1,0:T(8,128)S(1)}, u32[]{:S(2)}, u32[]{:S(2)}) %collective-permute-start.22) | collective-permute-done | bytes 32800 | tf_op jit(solution)/shard_map/ppermute | solution.py:484
  107.5 4.6 %group.1 = f32[64,2048]{1,0:T(8,128)} custom-call(f32[64,128]{1,0:T(8,128)S(1)} %add.142.refs_0_, f32[16,64,128]{2,1,0:T(8,128)S(1)} %pairs.7.work_ref.refs_1_), custom_call_target="tpu_custom_call" | custom-call | tf_op jit(solution)/shard_map/group/pallas_call | solution.py:684
  (94 shorter events, 4.7 us)
Async XLA Ops:
  0.6 24.9 %collective-permute-start.4 = (bf16[64,4096]{1,0:T(8,128)(2,1)}, bf16[64,4096]{1,0:T(8,128)(2,1)S(1)}, u32[]{:S(2)}, u32[]{:S(2)}) collective-permute-start(bf16[64,4096]{1,0:T(8,128)(2,1)} %probes_hbm.1), channel_id=1, source_target_pairs={{0,1},{1,0},{2,3},{3,2},{4,5},{5,4},{6,7},{7,6},{8,9},{9,8},{10,11... | collective-permute-start | bytes 1572872 | tf_op jit(solution)/shard_map/ppermute | solution.py:484
  0.7 24.8 %collective-permute-start.3 = (bf16[64,4096]{1,0:T(8,128)(2,1)}, bf16[64,4096]{1,0:T(8,128)(2,1)S(1)}, u32[]{:S(2)}, u32[]{:S(2)}) collective-permute-start(bf16[64,4096]{1,0:T(8,128)(2,1)} %probes_hbm.1), channel_id=1, source_target_pairs={{0,127},{1,2},{2,1},{3,4},{4,3},{5,6},{6,5},{7,8},{8,7},{9,10},{10... | collective-permute-start | bytes 1572872 | tf_op jit(solution)/shard_map/ppermute | solution.py:499
  15.4 21.2 %copy-start.8 = (bf16[64,4096]{1,0:T(8,128)(2,1)S(1)}, bf16[64,4096]{1,0:T(8,128)(2,1)}, u32[]{:S(2)}) copy-start(bf16[64,4096]{1,0:T(8,128)(2,1)} %get-tuple-element.48.refs_2_) | copy-start | bytes 1572868
  15.4 1.5 %collective-permute-start = (bf16[3,64,128]{2,1,0:T(8,128)(2,1)}, bf16[3,64,128]{2,1,0:T(8,128)(2,1)S(1)}, u32[]{:S(2)}, u32[]{:S(2)}) collective-permute-start(bf16[3,64,128]{2,1,0:T(8,128)(2,1)} %get-tuple-element.39), channel_id=1, source_target_pairs={{0,1},{1,0},{2,3},{3,2},{4,5},{5,4},{6,7},{7,6},{8,9},{9,8},{10,11... | collective-permute-start | bytes 147464 | tf_op jit(solution)/shard_map/ppermute | solution.py:484
  17.7 4.2 %collective-permute-start.1 = (bf16[3,64,128]{2,1,0:T(8,128)(2,1)S(1)}, bf16[3,64,128]{2,1,0:T(8,128)(2,1)S(1)}, u32[]{:S(2)}, u32[]{:S(2)}) collective-permute-start(bf16[3,64,128]{2,1,0:T(8,128)(2,1)S(1)} %pad_maximum_fusion.6), channel_id=1, source_target_pairs={{0,2},{1,3},{2,0},{3,1},{4,6},{5,7},{6,4},{7,5},{8,10},{9,11},{10,... | collective-permute-start | bytes 147464 | tf_op jit(solution)/shard_map/ppermute | solution.py:484
  18.7 17.8 %copy-start = (bf16[8,64,4096]{2,1,0:T(8,128)(2,1)S(1)}, bf16[8,64,4096]{2,1,0:T(8,128)(2,1)}, u32[]{:S(2)}) copy-start(bf16[8,64,4096]{2,1,0:T(8,128)(2,1)} %refs_4_.4) | copy-start | bytes 12582916
  21.9 14.4 %collective-permute-start.2 = (bf16[4,64,128]{2,1,0:T(8,128)(2,1)S(1)}, bf16[4,64,128]{2,1,0:T(8,128)(2,1)S(1)}, u32[]{:S(2)}, u32[]{:S(2)}) collective-permute-start(bf16[4,64,128]{2,1,0:T(8,128)(2,1)S(1)} %pad_maximum_fusion.mine_ref), channel_id=1, source_target_pairs={{0,6},{1,7},{2,4},{3,5},{4,2},{5,3},{6,0},{7,1},{8,14},{9,15},{10,... | collective-permute-start | bytes 196616 | tf_op jit(solution)/shard_map/ppermute | solution.py:484
  22.0 14.5 %collective-permute-start.7 = (bf16[64,4096]{1,0:T(8,128)(2,1)}, bf16[64,4096]{1,0:T(8,128)(2,1)S(1)}, u32[]{:S(2)}, u32[]{:S(2)}) collective-permute-start(bf16[64,4096]{1,0:T(8,128)(2,1)} %get-tuple-element.48.refs_2_), channel_id=1, source_target_pairs={{0,1},{1,0},{2,3},{3,2},{4,5},{5,4},{6,7},{7,6},{8,9},{9,8},{10,11... | collective-permute-start | bytes 1572872 | tf_op jit(solution)/shard_map/ppermute | solution.py:484
  22.1 14.4 %collective-permute-start.6 = (bf16[64,4096]{1,0:T(8,128)(2,1)}, bf16[64,4096]{1,0:T(8,128)(2,1)S(1)}, u32[]{:S(2)}, u32[]{:S(2)}) collective-permute-start(bf16[64,4096]{1,0:T(8,128)(2,1)} %get-tuple-element.48.refs_2_), channel_id=1, source_target_pairs={{0,127},{1,2},{2,1},{3,4},{4,3},{5,6},{6,5},{7,8},{8,7},{9,10},{10... | collective-permute-start | bytes 1572872 | tf_op jit(solution)/shard_map/ppermute | solution.py:499
  25.5 16.0 %collective-permute-start.9 = (bf16[64,4096]{1,0:T(8,128)(2,1)}, bf16[64,4096]{1,0:T(8,128)(2,1)S(1)}, u32[]{:S(2)}, u32[]{:S(2)}) collective-permute-start(bf16[64,4096]{1,0:T(8,128)(2,1)} %basis_ref.3), channel_id=1, source_target_pairs={{0,1},{1,0},{2,3},{3,2},{4,5},{5,4},{6,7},{7,6},{8,9},{9,8},{10,11... | collective-permute-start | bytes 1572872 | tf_op jit(solution)/shard_map/ppermute | solution.py:484
  25.5 16.6 %collective-permute-start.8 = (bf16[64,4096]{1,0:T(8,128)(2,1)}, bf16[64,4096]{1,0:T(8,128)(2,1)S(1)}, u32[]{:S(2)}, u32[]{:S(2)}) collective-permute-start(bf16[64,4096]{1,0:T(8,128)(2,1)} %basis_ref.3), channel_id=1, source_target_pairs={{0,127},{1,2},{2,1},{3,4},{4,3},{5,6},{6,5},{7,8},{8,7},{9,10},{10... | collective-permute-start | bytes 1572872 | tf_op jit(solution)/shard_map/ppermute | solution.py:499
  36.4 12.0 %copy-start.4 = (bf16[64,4096]{1,0:T(8,128)(2,1)S(1)}, bf16[64,4096]{1,0:T(8,128)(2,1)}, u32[]{:S(2)}) copy-start(bf16[64,4096]{1,0:T(8,128)(2,1)} %basis_ref.3) | copy-start | bytes 1572868
  36.4 12.0 %copy-start.5 = (bf16[64,4096]{1,0:T(8,128)(2,1)S(1)}, bf16[64,4096]{1,0:T(8,128)(2,1)}, u32[]{:S(2)}) copy-start(bf16[64,4096]{1,0:T(8,128)(2,1)} %transfer_ref.3) | copy-start | bytes 1572868
  36.4 12.0 %copy-start.10 = (bf16[2,2,64,64]{3,2,1,0:T(8,128)(2,1)S(1)}, bf16[2,2,64,64]{3,2,1,0:T(8,128)(2,1)}, u32[]{:S(2)}) copy-start(bf16[2,2,64,64]{3,2,1,0:T(8,128)(2,1)} %tree_ref.7) | copy-start | bytes 98308
  36.4 5.7 %collective-permute-start.5 = (bf16[3,64,128]{2,1,0:T(8,128)(2,1)S(1)}, bf16[3,64,128]{2,1,0:T(8,128)(2,1)S(1)}, u32[]{:S(2)}, u32[]{:S(2)}) collective-permute-start(bf16[3,64,128]{2,1,0:T(8,128)(2,1)S(1)} %fusion.4), channel_id=1, source_target_pairs={{0,8},{1,121},{2,10},{3,123},{4,12},{5,125},{6,14},{7,127},{8,0},{... | collective-permute-start | bytes 147464 | tf_op jit(solution)/shard_map/ppermute | solution.py:493
  41.5 24.2 %copy-start.1 = (bf16[8,64,4096]{2,1,0:T(8,128)(2,1)S(1)}, bf16[8,64,4096]{2,1,0:T(8,128)(2,1)}, u32[]{:S(2)}) copy-start(bf16[8,64,4096]{2,1,0:T(8,128)(2,1)} %refs_4_.5) | copy-start | bytes 12582916
  41.5 24.2 %copy-start.13 = (s32[512]{0:T(512)S(1)}, s32[512]{0:T(512)}, u32[]{:S(2)}) copy-start(s32[512]{0:T(512)} %reshape.60.refs_0_) | copy-start | bytes 6148
  42.1 1.2 %collective-permute-start.10 = (bf16[3,64,128]{2,1,0:T(8,128)(2,1)S(1)}, bf16[3,64,128]{2,1,0:T(8,128)(2,1)S(1)}, u32[]{:S(2)}, u32[]{:S(2)}) collective-permute-start(bf16[3,64,128]{2,1,0:T(8,128)(2,1)S(1)} %collective-permute-done.5.first_ref), channel_id=1, source_target_pairs={{0,1},{1,0},{2,3},{3,2},{4,5},{5,4},{6,7},{7,6},{8,9},{9,8},{10,11... | collective-permute-start | bytes 147464 | tf_op jit(solution)/shard_map/ppermute | solution.py:484
  46.4 2.0 %collective-permute-start.11 = (bf16[64,4096]{1,0:T(8,128)(2,1)S(1)}, bf16[64,4096]{1,0:T(8,128)(2,1)S(1)}, u32[]{:S(2)}, u32[]{:S(2)}) collective-permute-start(bf16[64,4096]{1,0:T(8,128)(2,1)S(1)} %inner.1.rows_ref.refs_2_), channel_id=1, source_target_pairs={{0,1},{1,0},{2,3},{3,2},{4,5},{5,4},{6,7},{7,6},{8,9},{9,8},{10,11... | collective-permute-start | bytes 1572872 | tf_op jit(solution)/shard_map/ppermute | solution.py:484
  51.3 19.4 %copy-start.2 = (bf16[8,64,4096]{2,1,0:T(8,128)(2,1)S(1)}, bf16[8,64,4096]{2,1,0:T(8,128)(2,1)}, u32[]{:S(2)}) copy-start(bf16[8,64,4096]{2,1,0:T(8,128)(2,1)} %refs_6_.1) | copy-start | bytes 12582916
  51.3 4.2 %collective-permute-start.12 = (bf16[3,64,128]{2,1,0:T(8,128)(2,1)S(1)}, bf16[3,64,128]{2,1,0:T(8,128)(2,1)S(1)}, u32[]{:S(2)}, u32[]{:S(2)}) collective-permute-start(bf16[3,64,128]{2,1,0:T(8,128)(2,1)S(1)} %get-tuple-element.56), channel_id=1, source_target_pairs={{0,1},{1,0},{2,3},{3,2},{4,5},{5,4},{6,7},{7,6},{8,9},{9,8},{10,11... | collective-permute-start | bytes 147464 | tf_op jit(solution)/shard_map/ppermute | solution.py:484
  51.6 14.0 %collective-permute-start.15 = (bf16[64,4096]{1,0:T(8,128)(2,1)S(1)}, bf16[64,4096]{1,0:T(8,128)(2,1)S(1)}, u32[]{:S(2)}, u32[]{:S(2)}) collective-permute-start(bf16[64,4096]{1,0:T(8,128)(2,1)S(1)} %inner.1.rows_ref.refs_2_), channel_id=1, source_target_pairs={{0,127},{1,2},{2,1},{3,4},{4,3},{5,6},{6,5},{7,8},{8,7},{9,10},{10... | collective-permute-start | bytes 1572872 | tf_op jit(solution)/shard_map/ppermute | solution.py:499
  55.6 6.2 %collective-permute-start.13 = (bf16[3,64,128]{2,1,0:T(8,128)(2,1)S(1)}, bf16[3,64,128]{2,1,0:T(8,128)(2,1)S(1)}, u32[]{:S(2)}, u32[]{:S(2)}) collective-permute-start(bf16[3,64,128]{2,1,0:T(8,128)(2,1)S(1)} %pad_maximum_fusion.7), channel_id=1, source_target_pairs={{0,2},{1,3},{2,0},{3,1},{4,6},{5,7},{6,4},{7,5},{8,10},{9,11},{10,... | collective-permute-start | bytes 147464 | tf_op jit(solution)/shard_map/ppermute | solution.py:484
  61.8 8.8 %collective-permute-start.14 = (bf16[4,64,128]{2,1,0:T(8,128)(2,1)S(1)}, bf16[4,64,128]{2,1,0:T(8,128)(2,1)S(1)}, u32[]{:S(2)}, u32[]{:S(2)}) collective-permute-start(bf16[4,64,128]{2,1,0:T(8,128)(2,1)S(1)} %pad_maximum_fusion.1.mine_ref), channel_id=1, source_target_pairs={{0,6},{1,7},{2,4},{3,5},{4,2},{5,3},{6,0},{7,1},{8,14},{9,15},{10,... | collective-permute-start | bytes 196616 | tf_op jit(solution)/shard_map/ppermute | solution.py:484
  70.6 8.4 %copy-start.12 = (bf16[3,3,64,64]{3,2,1,0:T(8,128)(2,1)S(1)}, bf16[3,3,64,64]{3,2,1,0:T(8,128)(2,1)}, u32[]{:S(2)}) copy-start(bf16[3,3,64,64]{3,2,1,0:T(8,128)(2,1)} %links_ref.3) | copy-start | bytes 221188
  70.6 7.0 %collective-permute-start.16 = (bf16[3,64,128]{2,1,0:T(8,128)(2,1)S(1)}, bf16[3,64,128]{2,1,0:T(8,128)(2,1)S(1)}, u32[]{:S(2)}, u32[]{:S(2)}) collective-permute-start(bf16[3,64,128]{2,1,0:T(8,128)(2,1)S(1)} %fusion.1), channel_id=1, source_target_pairs={{0,8},{1,121},{2,10},{3,123},{4,12},{5,125},{6,14},{7,127},{8,0},{... | collective-permute-start | bytes 147464 | tf_op jit(solution)/shard_map/ppermute | solution.py:493
  77.6 1.3 %collective-permute-start.17 = (bf16[3,64,128]{2,1,0:T(8,128)(2,1)S(1)}, bf16[3,64,128]{2,1,0:T(8,128)(2,1)S(1)}, u32[]{:S(2)}, u32[]{:S(2)}) collective-permute-start(bf16[3,64,128]{2,1,0:T(8,128)(2,1)S(1)} %collective-permute-done.16.first_ref), channel_id=1, source_target_pairs={{0,1},{1,0},{2,3},{3,2},{4,5},{5,4},{6,7},{7,6},{8,9},{9,8},{10,11... | collective-permute-start | bytes 147464 | tf_op jit(solution)/shard_map/ppermute | solution.py:484
  83.3 3.5 %collective-permute-start.18 = (f32[64,128]{1,0:T(8,128)S(1)}, f32[64,128]{1,0:T(8,128)S(1)}, u32[]{:S(2)}, u32[]{:S(2)}) collective-permute-start(f32[64,128]{1,0:T(8,128)S(1)} %get-tuple-element.65), channel_id=1, source_target_pairs={{0,1},{1,0},{2,3},{3,2},{4,5},{5,4},{6,7},{7,6},{8,9},{9,8},{10,11... | collective-permute-start | bytes 98312 | tf_op jit(solution)/shard_map/ppermute | solution.py:484
  86.8 4.2 %collective-permute-start.19 = (f32[64,128]{1,0:T(8,128)S(1)}, f32[64,128]{1,0:T(8,128)S(1)}, u32[]{:S(2)}, u32[]{:S(2)}) collective-permute-start(f32[64,128]{1,0:T(8,128)S(1)} %add.138), channel_id=1, source_target_pairs={{0,2},{1,3},{2,0},{3,1},{4,6},{5,7},{6,4},{7,5},{8,10},{9,11},{10,... | collective-permute-start | bytes 98312 | tf_op jit(solution)/shard_map/ppermute | solution.py:484
  90.9 7.4 %collective-permute-start.20 = (f32[64,128]{1,0:T(8,128)S(1)}, f32[64,128]{1,0:T(8,128)S(1)}, u32[]{:S(2)}, u32[]{:S(2)}) collective-permute-start(f32[64,128]{1,0:T(8,128)S(1)} %add.139), channel_id=1, source_target_pairs={{0,6},{1,7},{2,4},{3,5},{4,2},{5,3},{6,0},{7,1},{8,14},{9,15},{10,... | collective-permute-start | bytes 98312 | tf_op jit(solution)/shard_map/ppermute | solution.py:484
  98.4 4.0 %collective-permute-start.21 = (f32[64,128]{1,0:T(8,128)S(1)}, f32[64,128]{1,0:T(8,128)S(1)}, u32[]{:S(2)}, u32[]{:S(2)}) collective-permute-start(f32[64,128]{1,0:T(8,128)S(1)} %add.140), channel_id=1, source_target_pairs={{0,8},{1,9},{2,10},{3,11},{4,12},{5,13},{6,14},{7,15},{8,0},{9,1},... | collective-permute-start | bytes 98312 | tf_op jit(solution)/shard_map/ppermute | solution.py:484
  102.4 5.1 %collective-permute-start.22 = (f32[64,128]{1,0:T(8,128)S(1)}, f32[64,128]{1,0:T(8,128)S(1)}, u32[]{:S(2)}, u32[]{:S(2)}) collective-permute-start(f32[64,128]{1,0:T(8,128)S(1)} %add.141), channel_id=1, source_target_pairs={{0,24},{1,25},{2,26},{3,27},{4,28},{5,29},{6,30},{7,31},{8,16},{9,... | collective-permute-start | bytes 98312 | tf_op jit(solution)/shard_map/ppermute | solution.py:484
  (8 other events, 50.6 us)

commit v4 on v3

--- a/solution.py
+++ b/solution.py
@@ -5,14 +5,14 @@
 from jax.experimental.pallas import tpu as pltpu
 from jax.sharding import PartitionSpec as P
 
+
 AXES = ("box", "leaf")
 LEAF = 64
 TILE = 128
 STEPS = 8
-STREAM = (True, False)
+STREAM = (False, False)
 bf16 = jnp.bfloat16
 f32 = jnp.float32
-highest = lax.Precision.HIGHEST
 
 NN = (((1,), (0,)), ((), ()))
 NT = (((1,), (1,)), ((), ()))
@@ -47,9 +47,9 @@
 def coarse_payload(sums, tree_ref, scal_ref, pay_ref):
     folded = sums + swap_halves(sums)
     pay_ref[0] = folded.astype(bf16)
-    up = dot(folded[:, :LEAF].astype(bf16), tree_ref[0, scal_ref[0]])
+    up = dot(folded[:, :LEAF].astype(bf16), tree_ref[0, scal_ref[0] % 2])
     pay_ref[1] = twice(up).astype(bf16)
-    up = dot(up.astype(bf16), tree_ref[1, scal_ref[1]])
+    up = dot(up.astype(bf16), tree_ref[1, scal_ref[0] // 2 % 2])
     pay_ref[2] = twice(up).astype(bf16)
 
 
@@ -83,34 +83,37 @@
     return wait
 
 
-def coords_kernel(scal_ref, tree_ref, probes_hbm, basis_hbm, transfer_hbm, coords_ref, pay_ref, rows_ref, basis_ref, transfer_ref, sems):
+def coords_kernel(scal_ref, tree_hbm, probes_hbm, basis_hbm, transfer_hbm, coords_ref, pay_ref, rows_ref, basis_ref, transfer_ref, tree_ref, sems, tree_sem):
+    tree = pltpu.make_async_copy(tree_hbm, tree_ref, tree_sem)
     wait = fetch((probes_hbm, basis_hbm, transfer_hbm), (rows_ref, basis_ref, transfer_ref), sems, STEPS // 2)
+    tree.start()
     per = rows_ref.shape[1] // TILE // (STEPS // 2)
     for g in range(STEPS // 2):
         wait(g)
         for u in range(per):
             at = slice((g * per + u) * TILE, (g * per + u + 1) * TILE)
             coords_ref[:, at] = dot(rows_ref[:, at], two_blocks(basis_ref[:, at]), NT).astype(bf16)
+    tree.wait()
     coarse_payload(node_sums(coords_ref, transfer_ref), tree_ref, scal_ref, pay_ref)
 
 
 def node_sums(coords_ref, transfer_ref):
     def step(g, sums):
-        for u in range(8):
-            at = lanes(g * 8 + u)
+        for u in range(16):
+            at = lanes(g * 16 + u)
             sums = sums + dot(coords_ref[:, at], two_blocks(transfer_ref[:, at]))
         return sums
 
-    return lax.fori_loop(0, coords_ref.shape[1] // TILE // 8, step, jnp.zeros((LEAF, TILE), f32))
+    return lax.fori_loop(0, coords_ref.shape[1] // TILE // 16, step, jnp.zeros((LEAF, TILE), f32))
 
 
 def by_tiles(count, one):
     def step(g, carry):
-        for u in range(8):
-            one(lanes(g * 8 + u))
+        for u in range(16):
+            one(lanes(g * 16 + u))
         return carry
 
-    lax.fori_loop(0, count // 8, step, 0)
+    lax.fori_loop(0, count // 16, step, 0)
 
 
 def store_tile(store_ref, t, tile):
@@ -123,15 +126,15 @@
     for n, (source, basis) in enumerate(zip(sources, bases)):
 
         def step(g, carry, n=n, source=source, basis=basis):
-            for u in range(8):
-                t = g * 8 + u
+            for u in range(16):
+                t = g * 16 + u
                 tile = source[:, lanes(t)]
                 if basis is not None:
                     tile = dot(tile, two_blocks(basis[:, lanes(t)]), NT).astype(bf16)
                 store_tile(store_ref, n * tiles + t, tile)
             return carry
 
-        lax.fori_loop(0, tiles // 8, step, 0)
+        lax.fori_loop(0, tiles // 16, step, 0)
 
 
 def gathered(store_ref, index_ref, pair, low):
@@ -163,7 +166,8 @@
     bases = (bases[0], None, bases[1]) if bases else (None, None, None)
     fill_store(store_ref, (before_ref, own_ref, after_ref), bases)
     low = low_half((LEAF, TILE))
-    per = own_ref.shape[1] // TILE // STEPS
+    steps = STEPS if streamed else STEPS // 4
+    per = own_ref.shape[1] // TILE // steps
 
     def step(g, carry):
         if streamed:
@@ -175,12 +179,14 @@
             out_ref[:, lanes(pair)] = jnp.where(low, both[:LEAF], both[LEAF:])
         return carry
 
-    lax.fori_loop(0, STEPS, step, 0)
-
-
-def descend(scal_ref, mine_ref, other_ref, first_ref, second_ref, tree_ref, links_ref):
-    b0, b1, b2 = scal_ref[0], scal_ref[1], scal_ref[2]
-    odd, has_left, has_right = scal_ref[3], scal_ref[4], scal_ref[5]
+    lax.fori_loop(0, steps, step, 0)
+
+
+def descend(scal_ref, mine_ref, other_ref, first_ref, second_ref, tree_ref, links_ref, blocks):
+    node = scal_ref[0]
+    b0, b1, b2 = node % 2, node // 2 % 2, node // 4 % 2
+    block = node // 8
+    odd, has_left, has_right = block % 2, block > 0, block < blocks - 1
 
     def low_group(n):
         return jnp.where(b2 == 0, mine_ref[n], other_ref[n])
@@ -192,11 +198,11 @@
 
     def left(n):
         tile = jnp.where(crossed, first_ref[n], second_ref[n])
-        return jnp.where(has_left == 1, tile, jnp.zeros_like(tile))
+        return jnp.where(has_left, tile, jnp.zeros_like(tile))
 
     def right(n):
         tile = jnp.where(crossed, second_ref[n], first_ref[n])
-        return jnp.where(has_right == 1, tile, jnp.zeros_like(tile))
+        return jnp.where(has_right, tile, jnp.zeros_like(tile))
 
     def pick(j, options):
         tile = options[-1]
@@ -241,9 +247,9 @@
 def inner_kernel(
     scal_ref, near_ref, far_ref, basis_ref, transfer_ref,
     mine_ref, other_ref, first_ref, second_ref, tree_ref, links_ref,
-    middle_ref, coeffs_ref,
+    middle_ref, coeffs_ref, *, blocks,
 ):
-    descent = descend(scal_ref, mine_ref, other_ref, first_ref, second_ref, tree_ref, links_ref)
+    descent = descend(scal_ref, mine_ref, other_ref, first_ref, second_ref, tree_ref, links_ref, blocks)
     finish(near_ref, far_ref, basis_ref, transfer_ref, descent, coeffs_ref, middle_ref)
 
 
@@ -258,15 +264,15 @@
 def outer_kernel(
     scal_ref, near_ref, far_ref, basis_ref, transfer_ref,
     mine_ref, other_ref, first_ref, second_ref, tree_ref, links_ref,
-    samples_ref, work_ref, gram_ref, coeffs_ref,
+    samples_ref, work_ref, gram_ref, coeffs_ref, *, blocks,
 ):
-    descent = descend(scal_ref, mine_ref, other_ref, first_ref, second_ref, tree_ref, links_ref)
+    descent = descend(scal_ref, mine_ref, other_ref, first_ref, second_ref, tree_ref, links_ref, blocks)
     finish(near_ref, far_ref, basis_ref, transfer_ref, descent, coeffs_ref, samples_ref)
     low = low_half((LEAF, TILE))
 
     def step(g, total):
-        for u in range(4):
-            t = g * 4 + u
+        for u in range(8):
+            t = g * 8 + u
             both = jnp.concatenate([samples_ref[:, lanes(2 * t)], samples_ref[:, lanes(2 * t + 1)]], axis=0)
             both = dot3(both, both, NT)
             gram = jnp.where(low, both[:LEAF], both[LEAF:]) / TILE
@@ -274,7 +280,7 @@
             total = total + gram
         return total
 
-    total = lax.fori_loop(0, work_ref.shape[0] // 4, step, jnp.zeros((LEAF, TILE), f32))
+    total = lax.fori_loop(0, work_ref.shape[0] // 8, step, jnp.zeros((LEAF, TILE), f32))
     gram_ref[...] = total + swap_halves(total)
 
 
@@ -361,7 +367,7 @@
                 rest = jnp.where(inside, 0.0, work_ref[t, at, :])
                 work_ref[t, at, :] = rest - jnp.where(half == 0, both[n : n + 8], both[rest_rows + n : rest_rows + n + 8])
 
-        each(count, 4, update)
+        each(count, 16, update)
 
 
 def stacked(x, order):
@@ -391,7 +397,7 @@
         basis_ref[:, one] = solved[:LEAF]
         basis_ref[:, two] = solved[LEAF:]
 
-    each(work_ref.shape[0], 4, solve)
+    each(work_ref.shape[0], 8, solve)
 
 
 def eliminate_few(load, save, count):
@@ -457,7 +463,7 @@
         upper = jnp.where(col > row, tile, jnp.where(col == row, 1.0 / tile, 0.0))
         out_ref[:, lanes(t)] = dot3(inverse, two_blocks(upper), NT)
 
-    each(work_ref.shape[0], 4, solve)
+    each(work_ref.shape[0], 8, solve)
 
 
 HBM = pl.BlockSpec(memory_space=pltpu.HBM)
@@ -496,7 +502,9 @@
 def node_halo(x):
     count = lax.axis_size(AXES)
     route = [(i, (i - 1 if i % 2 == 0 else i + 1) % count) for i in range(count)]
-    return lax.ppermute(x, AXES, route), swap(x, 1)
+    far = lax.ppermute(x, AXES, route)
+    near = swap(x, 1)
+    return far, near
 
 
 def leaf_table(index, node):
@@ -560,17 +568,7 @@
     node = lax.axis_index(AXES)
     count = lax.axis_size(AXES)
     width = probes.shape[1]
-    block = node // 8
-    scal = jnp.stack(
-        [
-            node % 2,
-            node // 2 % 2,
-            node // 4 % 2,
-            block % 2,
-            (block > 0).astype(jnp.int32),
-            (block < count // 8 - 1).astype(jnp.int32),
-        ]
-    ).astype(jnp.int32)
+    scal = node.reshape(1).astype(jnp.int32)
     near_table = leaf_table(near_index, node)
     far_table = leaf_table(far_index, node)
 
@@ -595,27 +593,30 @@
     rows_b, rows_a = node_halo(probes)
     coords, pay, rows, basis, transfer = pl.pallas_call(
         coords_kernel,
-        in_specs=[SMEM, VMEM, HBM, HBM, HBM],
+        in_specs=[SMEM, HBM, HBM, HBM, HBM],
         out_specs=(VMEM,) * 5,
         out_shape=(row, payload, row, row, row),
-        scratch_shapes=[pltpu.SemaphoreType.DMA((3, STEPS // 2))],
-        compiler_params=params(56),
+        scratch_shapes=[
+            pltpu.VMEM(inner_tree.shape, bf16),
+            pltpu.SemaphoreType.DMA((3, STEPS // 2)),
+            pltpu.SemaphoreType.DMA,
+        ],
+        compiler_params=params(52),
         name="coords",
     )(scal, inner_tree, probes, inner_basis, inner_transfer)
     mine = coarse_near(pay, node)
     mine, near_table, far_table = lax.optimization_barrier((mine, near_table, far_table))
     other = swap(mine, 6)
     coords_b, coords_a = node_halo(after(coords, mine))
-    basis_b, basis_a = node_halo(after(outer_basis, mine))
     near_part = interact(near_table, (rows_b, after(rows, mine), rows_a), inner_near, streamed=STREAM[0])
     other, near_part = lax.optimization_barrier((other, near_part))
     one = adjacent_rows(far_payload(mine, other, node))
+    basis_b, basis_a = node_halo(after(outer_basis, near_part))
     far_part = interact(far_table, (coords_b, coords, coords_a), inner_far, streamed=STREAM[1])
-    far_part, basis_b, basis_a = lax.optimization_barrier((far_part, basis_b, basis_a))
     one, far_part = lax.optimization_barrier((one, far_part))
     two = swap(one, 1)
     middle = pl.pallas_call(
-        inner_kernel,
+        lambda *refs: inner_kernel(*refs, blocks=count // 8),
         in_specs=[SMEM] + [VMEM] * 10,
         out_specs=VMEM,
         out_shape=row,
@@ -641,7 +642,7 @@
     one, far_part = lax.optimization_barrier((one, far_part))
     two = swap(one, 1)
     samples, grams, gram = pl.pallas_call(
-        outer_kernel,
+        lambda *refs: outer_kernel(*refs, blocks=count // 8),
         in_specs=[SMEM] + [VMEM] * 10,
         out_specs=(VMEM,) * 3,
         out_shape=(
@@ -653,6 +654,7 @@
         compiler_params=params(6),
         name="outer",
     )(scal, near_part, far_part, outer_basis, outer_transfer, mine, other, one, two, outer_tree, outer_links)
+
     def piece(n, work):
         return pl.pallas_call(
             lambda *refs: pair_kernel(*refs, first=2 * n, last=2 * n + 2),

time: 112 us -> 103 us (0.920)
  waiting for transfers between devices: 22.9 us -> 41.3 us
  Pallas kernels: 56.9 us -> 39.4 us
  starting transfers between devices: 27.7 us -> 16.8 us
  local copies, waits for them, and re-layouts: 1.66 us -> 3.46 us
    ppermute x4, waiting for transfers between devices: 3.54 us -> 13.9 us  [node_halo(): far = lax.ppermute(x, AXES, route)]
    ppermute x17, waiting for transfers between devices: 19.4 us -> 27.4 us  [swap(): return lax.ppermute(x, AXES, [(i, i ^ mask) for i in range(count)])]
    pallas_call x4, Pallas kernels: 23.4 us -> 16.1 us  [interact(): pl.pallas_call(lambda *refs: interact_kernel(*refs, streamed=streamed), i...]
    ppermute x4, starting transfers between devices: 20.1 us -> 13.1 us  [node_halo(): far = lax.ppermute(x, AXES, route)]
    ppermute x17, starting transfers between devices: 7.44 us -> 1.98 us  [swap(): return lax.ppermute(x, AXES, [(i, i ^ mask) for i in range(count)])]
    pallas_call x4, Pallas kernels: 11.5 us -> 6.78 us  [piece(): pl.pallas_call(lambda *refs: pair_kernel(*refs, first=2 * n, last=2 * n +...]
    pallas_call x3, Pallas kernels: 12.4 us -> 8.6 us  [the longest x1 3.61 us: local(): pl.pallas_call(coords_kernel, in_specs=[SMEM, HBM, HBM, HBM, HBM], out_sp...]
    unnamed x34 -> x24, local copies, waits for them, and re-layouts: 0.1 us -> 3.09 us
  transfers between devices with their start and end apart: 23 -> 23, of which waited for: 11 -> 13; matrix products, arithmetic and copies ran while one was open for 3% -> 1% of each run, Pallas kernels for 38% -> 27%
where the time goes in v4:
time: 103 us
  waiting for transfers between devices  41.3 us (40%)
  Pallas kernels  39.4 us (38%)
  starting transfers between devices  16.8 us (16%)
  local copies, waits for them, and re-layouts  3.46 us (3%)
  between operations  1.17 us (1%)
    ppermute x17, waiting for transfers between devices, swap(): return lax.ppermute(x, AXES, [(i, i ^ mask) for i in range(count)])  27.4 us
    pallas_call x4, Pallas kernels, interact(): pl.pallas_call(lambda *refs: interact_kernel(*refs, streamed=streamed), i...  16.1 us
    ppermute x4, waiting for transfers between devices, node_halo(): far = lax.ppermute(x, AXES, route)  13.9 us
    ppermute x4, starting transfers between devices, node_halo(): far = lax.ppermute(x, AXES, route)  13.1 us
    pallas_call x4, Pallas kernels, piece(): pl.pallas_call(lambda *refs: pair_kernel(*refs, first=2 * n, last=2 * n +...  6.78 us
    pallas_call x1, Pallas kernels, local(): pl.pallas_call(lambda *refs: group_kernel(*refs, scale=scale), in_specs=[...  4.31 us
    pallas_call x1, Pallas kernels, local(): pl.pallas_call(coords_kernel, in_specs=[SMEM, HBM, HBM, HBM, HBM], out_sp...  3.61 us
    unnamed x24, local copies, waits for them, and re-layouts  3.09 us
  transfers between devices with their start and end apart: 23, of which 13 were waited for; matrix products, arithmetic and copies ran while one was open for 1% of the time, Pallas kernels for 27%

profile of v4, /device:TPU:0, one launch (start us, length us, event | category | flops | bytes accessed | tf_op | source)
XLA Modules:
  0.0 103.0 jit_solution(9999623110370128495)
XLA Ops:
  0.6 8.3 %collective-permute-start.3 = (bf16[64,4096]{1,0:T(8,128)(2,1)}, bf16[64,4096]{1,0:T(8,128)(2,1)S(1)}, u32[]{:S(2)}, u32[]{:S(2)}) collective-permute-start(bf16[64,4096]{1,0:T(8,128)(2,1)} %probes_hbm.1), channel_id=1, source_target_pairs={{0,127},{1,2},{2,1},{3,4},{4,3},{5,6},{6,5},{7,8},{8,7},{9,10},{10... | collective-permute-start | bytes 1572872 | tf_op jit(solution)/shard_map/ppermute | solution.py:505
  9.8 3.6 %coords.1 = (bf16[64,4096]{1,0:T(8,128)(2,1)S(1)}, bf16[3,64,128]{2,1,0:T(8,128)(2,1)S(1)}, bf16[64,4096]{1,0:T(8,128)(2,1)S(1)}, bf16[64,4096]{1,0:T(8,128)(2,1)S(1)}, bf16[64,4096]{1,0:T(8,128)(2,1)}) custom-call(s32[1]{0:T(128)} %bitcast.scal_ref.refs_0_, bf16[2,2,64,64]{3,2,1,0:T(8,128)(2,1)S(1)} %copy-done.7, bf16[64,4096]{1,0:T(8,128)(2,1)} %probes_hbm.1, ...), custom_call_target="tpu_custom_call" | custom-call | tf_op jit(solution)/shard_map/coords/pallas_call | solution.py:594
  15.4 3.6 %collective-permute-done.1 = bf16[3,64,128]{2,1,0:T(8,128)(2,1)S(1)} collective-permute-done((bf16[3,64,128]{2,1,0:T(8,128)(2,1)S(1)}, bf16[3,64,128]{2,1,0:T(8,128)(2,1)S(1)}, u32[]{:S(2)}, u32[]{:S(2)}) %collective-permute-start.1) | collective-permute-done | bytes 49184 | tf_op jit(solution)/shard_map/ppermute | solution.py:490
  19.2 1.9 %collective-permute-start.6 = (bf16[64,4096]{1,0:T(8,128)(2,1)S(1)}, bf16[64,4096]{1,0:T(8,128)(2,1)S(1)}, u32[]{:S(2)}, u32[]{:S(2)}) collective-permute-start(bf16[64,4096]{1,0:T(8,128)(2,1)S(1)} %get-tuple-element.45.refs_2_), channel_id=1, source_target_pairs={{0,127},{1,2},{2,1},{3,4},{4,3},{5,6},{6,5},{7,8},{8,7},{9,10},{10... | collective-permute-start | bytes 1572872 | tf_op jit(solution)/shard_map/ppermute | solution.py:505
  21.2 2.2 %copy-done = bf16[8,64,4096]{2,1,0:T(8,128)(2,1)S(1)} copy-done((bf16[8,64,4096]{2,1,0:T(8,128)(2,1)S(1)}, bf16[8,64,4096]{2,1,0:T(8,128)(2,1)}, u32[]{:S(2)}) %copy-start) | copy-done | bytes 4194328
  23.3 3.7 %interact.4.refs_1_ = f32[64,4096]{1,0:T(8,128)S(1)} custom-call(s32[512]{0:T(512)S(1)} %reshape.64.refs_0_, bf16[64,4096]{1,0:T(8,128)(2,1)S(1)} %collective-permute-done.3.refs_1_, bf16[64,4096]{1,0:T(8,128)(2,1)S(1)} %get-tuple-element.40.refs_2_, bf16[64,4096]{1,0:T(8,128)(2,1)S(1)} %collective-permute-done.4.refs_3_, bf16[8,64,4096]{2,1,0:T(8,128)(2,1)S(1)} %copy-done), custom_call_target="tpu_custom_call" | custom-call | tf_op jit(solution)/shard_map/interact/pallas_call | solution.py:579
  27.2 1.4 %collective-permute-start.5 = (bf16[3,64,128]{2,1,0:T(8,128)(2,1)S(1)}, bf16[3,64,128]{2,1,0:T(8,128)(2,1)S(1)}, u32[]{:S(2)}, u32[]{:S(2)}) collective-permute-start(bf16[3,64,128]{2,1,0:T(8,128)(2,1)S(1)} %fusion.4), channel_id=1, source_target_pairs={{0,8},{1,121},{2,10},{3,123},{4,12},{5,125},{6,14},{7,127},{8,0},{... | collective-permute-start | bytes 147464 | tf_op jit(solution)/shard_map/ppermute | solution.py:499
  28.6 4.7 %collective-permute-done.6.refs_1_ = bf16[64,4096]{1,0:T(8,128)(2,1)S(1)} collective-permute-done((bf16[64,4096]{1,0:T(8,128)(2,1)S(1)}, bf16[64,4096]{1,0:T(8,128)(2,1)S(1)}, u32[]{:S(2)}, u32[]{:S(2)}) %collective-permute-start.6) | collective-permute-done | bytes 524320 | tf_op jit(solution)/shard_map/ppermute | solution.py:505
  33.3 3.7 %interact.5.refs_2_ = f32[64,4096]{1,0:T(8,128)S(1)} custom-call(s32[512]{0:T(512)S(1)} %reshape.65.refs_0_, bf16[64,4096]{1,0:T(8,128)(2,1)S(1)} %collective-permute-done.6.refs_1_, bf16[64,4096]{1,0:T(8,128)(2,1)S(1)} %get-tuple-element.45.refs_2_, bf16[64,4096]{1,0:T(8,128)(2,1)S(1)} %collective-permute-done.7.refs_3_, bf16[8,64,4096]{2,1,0:T(8,128)(2,1)S(1)} %copy-done.1), custom_call_target="tpu_custom_call" | custom-call | tf_op jit(solution)/shard_map/interact/pallas_call | solution.py:579
  37.2 1.2 %collective-permute-done.8.refs_8_ = bf16[3,64,128]{2,1,0:T(8,128)(2,1)S(1)} collective-permute-done((bf16[3,64,128]{2,1,0:T(8,128)(2,1)S(1)}, bf16[3,64,128]{2,1,0:T(8,128)(2,1)S(1)}, u32[]{:S(2)}, u32[]{:S(2)}) %collective-permute-start.8) | collective-permute-done | bytes 49184 | tf_op jit(solution)/shard_map/ppermute | solution.py:490
  38.4 2.0 %inner.1.rows_ref.refs_2_ = bf16[64,4096]{1,0:T(8,128)(2,1)S(1)} custom-call(s32[1]{0:T(128)} %bitcast.scal_ref.refs_0_, f32[64,4096]{1,0:T(8,128)S(1)} %interact.4.refs_1_, f32[64,4096]{1,0:T(8,128)S(1)} %interact.5.refs_2_, bf16[64,4096]{1,0:T(8,128)(2,1)S(1)} %get-tuple-element.47.refs_3_, bf16[64,4096]{1,0:T(8,128)(2,1)S(1)} %copy-done.6, ...), custom_call_target="tpu_custom_call" | custom-call | tf_op jit(solution)/shard_map/inner/pallas_call | solution.py:618
  40.6 1.8 %collective-permute-done.9.refs_3_ = bf16[64,4096]{1,0:T(8,128)(2,1)S(1)} collective-permute-done((bf16[64,4096]{1,0:T(8,128)(2,1)S(1)}, bf16[64,4096]{1,0:T(8,128)(2,1)S(1)}, u32[]{:S(2)}, u32[]{:S(2)}) %collective-permute-start.9) | collective-permute-done | bytes 524320 | tf_op jit(solution)/shard_map/ppermute | solution.py:490
  42.4 1.8 %next.1 = (bf16[64,4096]{1,0:T(8,128)(2,1)S(1)}, bf16[3,64,128]{2,1,0:T(8,128)(2,1)S(1)}) custom-call(s32[1]{0:T(128)} %bitcast.scal_ref.refs_0_, bf16[2,2,64,64]{3,2,1,0:T(8,128)(2,1)S(1)} %copy-done.9, bf16[64,4096]{1,0:T(8,128)(2,1)S(1)} %inner.1.rows_ref.refs_2_, bf16[64,4096]{1,0:T(8,128)(2,1)S(1)} %copy-done.4, bf16[64,4096]{1,0:T(8,128)(2,1)S(1)} %copy-done.5), custom_call_target="tpu_custom_call" | custom-call | tf_op jit(solution)/shard_map/next/pallas_call | solution.py:628
  44.5 1.8 %collective-permute-start.13 = (bf16[64,4096]{1,0:T(8,128)(2,1)S(1)}, bf16[64,4096]{1,0:T(8,128)(2,1)S(1)}, u32[]{:S(2)}, u32[]{:S(2)}) collective-permute-start(bf16[64,4096]{1,0:T(8,128)(2,1)S(1)} %inner.1.rows_ref.refs_2_), channel_id=1, source_target_pairs={{0,127},{1,2},{2,1},{3,4},{4,3},{5,6},{6,5},{7,8},{8,7},{9,10},{10... | collective-permute-start | bytes 1572872 | tf_op jit(solution)/shard_map/ppermute | solution.py:505
  46.6 8.1 %collective-permute-done.11 = bf16[3,64,128]{2,1,0:T(8,128)(2,1)S(1)} collective-permute-done((bf16[3,64,128]{2,1,0:T(8,128)(2,1)S(1)}, bf16[3,64,128]{2,1,0:T(8,128)(2,1)S(1)}, u32[]{:S(2)}, u32[]{:S(2)}) %collective-permute-start.11) | collective-permute-done | bytes 49184 | tf_op jit(solution)/shard_map/ppermute | solution.py:490
  54.8 1.1 %collective-permute-start.15 = (bf16[64,4096]{1,0:T(8,128)(2,1)S(1)}, bf16[64,4096]{1,0:T(8,128)(2,1)S(1)}, u32[]{:S(2)}, u32[]{:S(2)}) collective-permute-start(bf16[64,4096]{1,0:T(8,128)(2,1)S(1)} %copy-done.4), channel_id=1, source_target_pairs={{0,127},{1,2},{2,1},{3,4},{4,3},{5,6},{6,5},{7,8},{8,7},{9,10},{10... | collective-permute-start | bytes 1572872 | tf_op jit(solution)/shard_map/ppermute | solution.py:505
  55.9 2.9 %collective-permute-done.13.refs_1_ = bf16[64,4096]{1,0:T(8,128)(2,1)S(1)} collective-permute-done((bf16[64,4096]{1,0:T(8,128)(2,1)S(1)}, bf16[64,4096]{1,0:T(8,128)(2,1)S(1)}, u32[]{:S(2)}, u32[]{:S(2)}) %collective-permute-start.13) | collective-permute-done | bytes 524320 | tf_op jit(solution)/shard_map/ppermute | solution.py:505
  58.8 3.6 %interact.6.refs_1_ = f32[64,4096]{1,0:T(8,128)S(1)} custom-call(s32[512]{0:T(512)S(1)} %reshape.64.refs_0_, bf16[64,4096]{1,0:T(8,128)(2,1)S(1)} %collective-permute-done.13.refs_1_, bf16[64,4096]{1,0:T(8,128)(2,1)S(1)} %inner.1.rows_ref.refs_2_, bf16[64,4096]{1,0:T(8,128)(2,1)S(1)} %collective-permute-done.9.refs_3_, bf16[8,64,4096]{2,1,0:T(8,128)(2,1)S(1)} %copy-done.2), custom_call_target="tpu_custom_call" | custom-call | tf_op jit(solution)/shard_map/interact/pallas_call | solution.py:579
  62.8 6.2 %collective-permute-done.15.refs_4_ = bf16[64,4096]{1,0:T(8,128)(2,1)S(1)} collective-permute-done((bf16[64,4096]{1,0:T(8,128)(2,1)S(1)}, bf16[64,4096]{1,0:T(8,128)(2,1)S(1)}, u32[]{:S(2)}, u32[]{:S(2)}) %collective-permute-start.15) | collective-permute-done | bytes 524320 | tf_op jit(solution)/shard_map/ppermute | solution.py:505
  69.0 5.1 %interact.7.refs_2_ = f32[64,4096]{1,0:T(8,128)S(1)} custom-call(s32[512]{0:T(512)S(1)} %reshape.65.refs_0_, bf16[64,4096]{1,0:T(8,128)(2,1)S(1)} %collective-permute-done.13.refs_1_, bf16[64,4096]{1,0:T(8,128)(2,1)S(1)} %get-tuple-element.55.refs_2_, bf16[64,4096]{1,0:T(8,128)(2,1)S(1)} %collective-permute-done.9.refs_3_, ...), custom_call_target="tpu_custom_call" | custom-call | tf_op jit(solution)/shard_map/interact/pallas_call | solution.py:579
  74.2 1.2 %collective-permute-done.17.refs_8_ = bf16[3,64,128]{2,1,0:T(8,128)(2,1)S(1)} collective-permute-done((bf16[3,64,128]{2,1,0:T(8,128)(2,1)S(1)}, bf16[3,64,128]{2,1,0:T(8,128)(2,1)S(1)}, u32[]{:S(2)}, u32[]{:S(2)}) %collective-permute-start.17) | collective-permute-done | bytes 49184 | tf_op jit(solution)/shard_map/ppermute | solution.py:490
  75.5 3.0 %outer.1 = (f32[64,4096]{1,0:T(8,128)S(1)}, f32[16,64,128]{2,1,0:T(8,128)S(1)}, f32[64,128]{1,0:T(8,128)S(1)}) custom-call(s32[1]{0:T(128)} %bitcast.scal_ref.refs_0_, f32[64,4096]{1,0:T(8,128)S(1)} %interact.6.refs_1_, f32[64,4096]{1,0:T(8,128)S(1)} %interact.7.refs_2_, bf16[64,4096]{1,0:T(8,128)(2,1)S(1)} %copy-done.4, bf16[64,4096]{1,0:T(8,128)(2,1)S(1)} %copy-done.5, ...), custom_call_target="tpu_custom_call" | custom-call | tf_op jit(solution)/shard_map/outer/pallas_call | solution.py:644
  78.6 1.9 %pairs.4.refs_0_ = f32[16,64,128]{2,1,0:T(8,128)S(1)} custom-call(f32[16,64,128]{2,1,0:T(8,128)S(1)} %get-tuple-element.60.refs_0_), custom_call_target="tpu_custom_call", output_to_operand_aliasing={{}: (0, {})} | custom-call | tf_op jit(solution)/shard_map/pairs/pallas_call | solution.py:659
  80.6 1.7 %pairs.5.refs_0_ = f32[16,64,128]{2,1,0:T(8,128)S(1)} custom-call(f32[16,64,128]{2,1,0:T(8,128)S(1)} %pairs.4.refs_0_), custom_call_target="tpu_custom_call", output_to_operand_aliasing={{}: (0, {})} | custom-call | tf_op jit(solution)/shard_map/pairs/pallas_call | solution.py:659
  82.4 2.2 %collective-permute-done.19 = f32[64,128]{1,0:T(8,128)S(1)} collective-permute-done((f32[64,128]{1,0:T(8,128)S(1)}, f32[64,128]{1,0:T(8,128)S(1)}, u32[]{:S(2)}, u32[]{:S(2)}) %collective-permute-start.19) | collective-permute-done | bytes 32800 | tf_op jit(solution)/shard_map/ppermute | solution.py:490
  84.5 1.8 %pairs.6.refs_0_ = f32[16,64,128]{2,1,0:T(8,128)S(1)} custom-call(f32[16,64,128]{2,1,0:T(8,128)S(1)} %pairs.5.refs_0_), custom_call_target="tpu_custom_call", output_to_operand_aliasing={{}: (0, {})} | custom-call | tf_op jit(solution)/shard_map/pairs/pallas_call | solution.py:659
  86.3 3.3 %collective-permute-done.20 = f32[64,128]{1,0:T(8,128)S(1)} collective-permute-done((f32[64,128]{1,0:T(8,128)S(1)}, f32[64,128]{1,0:T(8,128)S(1)}, u32[]{:S(2)}, u32[]{:S(2)}) %collective-permute-start.20) | collective-permute-done | bytes 32800 | tf_op jit(solution)/shard_map/ppermute | solution.py:490
  89.7 1.4 %pairs.7.work_ref.refs_1_ = f32[16,64,128]{2,1,0:T(8,128)S(1)} custom-call(f32[16,64,128]{2,1,0:T(8,128)S(1)} %pairs.6.refs_0_), custom_call_target="tpu_custom_call", output_to_operand_aliasing={{}: (0, {})} | custom-call | tf_op jit(solution)/shard_map/pairs/pallas_call | solution.py:659
  91.1 2.5 %collective-permute-done.21 = f32[64,128]{1,0:T(8,128)S(1)} collective-permute-done((f32[64,128]{1,0:T(8,128)S(1)}, f32[64,128]{1,0:T(8,128)S(1)}, u32[]{:S(2)}, u32[]{:S(2)}) %collective-permute-start.21) | collective-permute-done | bytes 32800 | tf_op jit(solution)/shard_map/ppermute | solution.py:490
  93.6 1.7 %solve.1 = f32[64,4096]{1,0:T(8,128)} custom-call(f32[16,64,128]{2,1,0:T(8,128)S(1)} %pairs.7.work_ref.refs_1_, f32[64,4096]{1,0:T(8,128)S(1)} %get-tuple-element.68.samples_ref), custom_call_target="tpu_custom_call" | custom-call | tf_op jit(solution)/shard_map/solve/pallas_call | solution.py:676
  95.3 3.4 %collective-permute-done.22 = f32[64,128]{1,0:T(8,128)S(1)} collective-permute-done((f32[64,128]{1,0:T(8,128)S(1)}, f32[64,128]{1,0:T(8,128)S(1)}, u32[]{:S(2)}, u32[]{:S(2)}) %collective-permute-start.22) | collective-permute-done | bytes 32800 | tf_op jit(solution)/shard_map/ppermute | solution.py:490
  98.7 4.3 %group.1 = f32[64,2048]{1,0:T(8,128)} custom-call(f32[64,128]{1,0:T(8,128)S(1)} %add.138.refs_0_, f32[16,64,128]{2,1,0:T(8,128)S(1)} %pairs.7.work_ref.refs_1_), custom_call_target="tpu_custom_call" | custom-call | tf_op jit(solution)/shard_map/group/pallas_call | solution.py:686
  (83 shorter events, 4.6 us)
Async XLA Ops:
  0.6 20.5 %collective-permute-start.3 = (bf16[64,4096]{1,0:T(8,128)(2,1)}, bf16[64,4096]{1,0:T(8,128)(2,1)S(1)}, u32[]{:S(2)}, u32[]{:S(2)}) collective-permute-start(bf16[64,4096]{1,0:T(8,128)(2,1)} %probes_hbm.1), channel_id=1, source_target_pairs={{0,127},{1,2},{2,1},{3,4},{4,3},{5,6},{6,5},{7,8},{8,7},{9,10},{10... | collective-permute-start | bytes 1572872 | tf_op jit(solution)/shard_map/ppermute | solution.py:505
  8.9 12.2 %collective-permute-start.4 = (bf16[64,4096]{1,0:T(8,128)(2,1)}, bf16[64,4096]{1,0:T(8,128)(2,1)S(1)}, u32[]{:S(2)}, u32[]{:S(2)}) collective-permute-start(bf16[64,4096]{1,0:T(8,128)(2,1)} %probes_hbm.1), channel_id=1, source_target_pairs={{0,1},{1,0},{2,3},{3,2},{4,5},{5,4},{6,7},{7,6},{8,9},{9,8},{10,11... | collective-permute-start | bytes 1572872 | tf_op jit(solution)/shard_map/ppermute | solution.py:490
  13.4 1.5 %collective-permute-start = (bf16[3,64,128]{2,1,0:T(8,128)(2,1)S(1)}, bf16[3,64,128]{2,1,0:T(8,128)(2,1)S(1)}, u32[]{:S(2)}, u32[]{:S(2)}) collective-permute-start(bf16[3,64,128]{2,1,0:T(8,128)(2,1)S(1)} %get-tuple-element.36), channel_id=1, source_target_pairs={{0,1},{1,0},{2,3},{3,2},{4,5},{5,4},{6,7},{7,6},{8,9},{9,8},{10,11... | collective-permute-start | bytes 147464 | tf_op jit(solution)/shard_map/ppermute | solution.py:490
  14.9 4.2 %collective-permute-start.1 = (bf16[3,64,128]{2,1,0:T(8,128)(2,1)S(1)}, bf16[3,64,128]{2,1,0:T(8,128)(2,1)S(1)}, u32[]{:S(2)}, u32[]{:S(2)}) collective-permute-start(bf16[3,64,128]{2,1,0:T(8,128)(2,1)S(1)} %pad_maximum_fusion.6), channel_id=1, source_target_pairs={{0,2},{1,3},{2,0},{3,1},{4,6},{5,7},{6,4},{7,5},{8,10},{9,11},{10,... | collective-permute-start | bytes 147464 | tf_op jit(solution)/shard_map/ppermute | solution.py:490
  19.1 8.0 %collective-permute-start.2 = (bf16[4,64,128]{2,1,0:T(8,128)(2,1)S(1)}, bf16[4,64,128]{2,1,0:T(8,128)(2,1)S(1)}, u32[]{:S(2)}, u32[]{:S(2)}) collective-permute-start(bf16[4,64,128]{2,1,0:T(8,128)(2,1)S(1)} %pad_maximum_fusion.refs_5_), channel_id=1, source_target_pairs={{0,6},{1,7},{2,4},{3,5},{4,2},{5,3},{6,0},{7,1},{8,14},{9,15},{10,... | collective-permute-start | bytes 196616 | tf_op jit(solution)/shard_map/ppermute | solution.py:490
  19.2 14.1 %collective-permute-start.6 = (bf16[64,4096]{1,0:T(8,128)(2,1)S(1)}, bf16[64,4096]{1,0:T(8,128)(2,1)S(1)}, u32[]{:S(2)}, u32[]{:S(2)}) collective-permute-start(bf16[64,4096]{1,0:T(8,128)(2,1)S(1)} %get-tuple-element.45.refs_2_), channel_id=1, source_target_pairs={{0,127},{1,2},{2,1},{3,4},{4,3},{5,6},{6,5},{7,8},{8,7},{9,10},{10... | collective-permute-start | bytes 1572872 | tf_op jit(solution)/shard_map/ppermute | solution.py:505
  21.1 12.2 %collective-permute-start.7 = (bf16[64,4096]{1,0:T(8,128)(2,1)S(1)}, bf16[64,4096]{1,0:T(8,128)(2,1)S(1)}, u32[]{:S(2)}, u32[]{:S(2)}) collective-permute-start(bf16[64,4096]{1,0:T(8,128)(2,1)S(1)} %get-tuple-element.45.refs_2_), channel_id=1, source_target_pairs={{0,1},{1,0},{2,3},{3,2},{4,5},{5,4},{6,7},{7,6},{8,9},{9,8},{10,11... | collective-permute-start | bytes 1572872 | tf_op jit(solution)/shard_map/ppermute | solution.py:490
  27.1 11.3 %copy-start.6 = (bf16[64,4096]{1,0:T(8,128)(2,1)S(1)}, bf16[64,4096]{1,0:T(8,128)(2,1)}, u32[]{:S(2)}) copy-start(bf16[64,4096]{1,0:T(8,128)(2,1)} %get-tuple-element.48.refs_4_) | copy-start | bytes 1572868
  27.1 11.3 %copy-start.8 = (bf16[2,2,64,64]{3,2,1,0:T(8,128)(2,1)S(1)}, bf16[2,2,64,64]{3,2,1,0:T(8,128)(2,1)}, u32[]{:S(2)}) copy-start(bf16[2,2,64,64]{3,2,1,0:T(8,128)(2,1)} %refs_9_.2) | copy-start | bytes 98308
  27.1 11.3 %copy-start.10 = (bf16[3,3,64,64]{3,2,1,0:T(8,128)(2,1)S(1)}, bf16[3,3,64,64]{3,2,1,0:T(8,128)(2,1)}, u32[]{:S(2)}) copy-start(bf16[3,3,64,64]{3,2,1,0:T(8,128)(2,1)} %refs_10_.2) | copy-start | bytes 221188
  27.2 15.2 %copy-start.4 = (bf16[64,4096]{1,0:T(8,128)(2,1)S(1)}, bf16[64,4096]{1,0:T(8,128)(2,1)}, u32[]{:S(2)}) copy-start(bf16[64,4096]{1,0:T(8,128)(2,1)} %refs_3_.1) | copy-start | bytes 1572868
  27.2 15.2 %copy-start.5 = (bf16[64,4096]{1,0:T(8,128)(2,1)S(1)}, bf16[64,4096]{1,0:T(8,128)(2,1)}, u32[]{:S(2)}) copy-start(bf16[64,4096]{1,0:T(8,128)(2,1)} %refs_4_.7) | copy-start | bytes 1572868
  27.2 15.2 %copy-start.9 = (bf16[2,2,64,64]{3,2,1,0:T(8,128)(2,1)S(1)}, bf16[2,2,64,64]{3,2,1,0:T(8,128)(2,1)}, u32[]{:S(2)}) copy-start(bf16[2,2,64,64]{3,2,1,0:T(8,128)(2,1)} %refs_9_.3) | copy-start | bytes 98308
  27.2 9.8 %collective-permute-start.5 = (bf16[3,64,128]{2,1,0:T(8,128)(2,1)S(1)}, bf16[3,64,128]{2,1,0:T(8,128)(2,1)S(1)}, u32[]{:S(2)}, u32[]{:S(2)}) collective-permute-start(bf16[3,64,128]{2,1,0:T(8,128)(2,1)S(1)} %fusion.4), channel_id=1, source_target_pairs={{0,8},{1,121},{2,10},{3,123},{4,12},{5,125},{6,14},{7,127},{8,0},{... | collective-permute-start | bytes 147464 | tf_op jit(solution)/shard_map/ppermute | solution.py:499
  37.0 21.8 %copy-start.2 = (bf16[8,64,4096]{2,1,0:T(8,128)(2,1)S(1)}, bf16[8,64,4096]{2,1,0:T(8,128)(2,1)}, u32[]{:S(2)}) copy-start(bf16[8,64,4096]{2,1,0:T(8,128)(2,1)} %refs_4_.6) | copy-start | bytes 12582916
  37.1 1.3 %collective-permute-start.8 = (bf16[3,64,128]{2,1,0:T(8,128)(2,1)S(1)}, bf16[3,64,128]{2,1,0:T(8,128)(2,1)S(1)}, u32[]{:S(2)}, u32[]{:S(2)}) collective-permute-start(bf16[3,64,128]{2,1,0:T(8,128)(2,1)S(1)} %collective-permute-done.5.refs_7_), channel_id=1, source_target_pairs={{0,1},{1,0},{2,3},{3,2},{4,5},{5,4},{6,7},{7,6},{8,9},{9,8},{10,11... | collective-permute-start | bytes 147464 | tf_op jit(solution)/shard_map/ppermute | solution.py:490
  40.4 2.0 %collective-permute-start.9 = (bf16[64,4096]{1,0:T(8,128)(2,1)S(1)}, bf16[64,4096]{1,0:T(8,128)(2,1)S(1)}, u32[]{:S(2)}, u32[]{:S(2)}) collective-permute-start(bf16[64,4096]{1,0:T(8,128)(2,1)S(1)} %inner.1.rows_ref.refs_2_), channel_id=1, source_target_pairs={{0,1},{1,0},{2,3},{3,2},{4,5},{5,4},{6,7},{7,6},{8,9},{9,8},{10,11... | collective-permute-start | bytes 1572872 | tf_op jit(solution)/shard_map/ppermute | solution.py:490
  44.2 24.8 %copy-start.3 = (bf16[8,64,4096]{2,1,0:T(8,128)(2,1)S(1)}, bf16[8,64,4096]{2,1,0:T(8,128)(2,1)}, u32[]{:S(2)}) copy-start(bf16[8,64,4096]{2,1,0:T(8,128)(2,1)} %refs_6_.1) | copy-start | bytes 12582916
  44.3 2.1 %collective-permute-start.10 = (bf16[3,64,128]{2,1,0:T(8,128)(2,1)S(1)}, bf16[3,64,128]{2,1,0:T(8,128)(2,1)S(1)}, u32[]{:S(2)}, u32[]{:S(2)}) collective-permute-start(bf16[3,64,128]{2,1,0:T(8,128)(2,1)S(1)} %get-tuple-element.51), channel_id=1, source_target_pairs={{0,1},{1,0},{2,3},{3,2},{4,5},{5,4},{6,7},{7,6},{8,9},{9,8},{10,11... | collective-permute-start | bytes 147464 | tf_op jit(solution)/shard_map/ppermute | solution.py:490
  44.5 14.3 %collective-permute-start.13 = (bf16[64,4096]{1,0:T(8,128)(2,1)S(1)}, bf16[64,4096]{1,0:T(8,128)(2,1)S(1)}, u32[]{:S(2)}, u32[]{:S(2)}) collective-permute-start(bf16[64,4096]{1,0:T(8,128)(2,1)S(1)} %inner.1.rows_ref.refs_2_), channel_id=1, source_target_pairs={{0,127},{1,2},{2,1},{3,4},{4,3},{5,6},{6,5},{7,8},{8,7},{9,10},{10... | collective-permute-start | bytes 1572872 | tf_op jit(solution)/shard_map/ppermute | solution.py:505
  46.4 8.3 %collective-permute-start.11 = (bf16[3,64,128]{2,1,0:T(8,128)(2,1)S(1)}, bf16[3,64,128]{2,1,0:T(8,128)(2,1)S(1)}, u32[]{:S(2)}, u32[]{:S(2)}) collective-permute-start(bf16[3,64,128]{2,1,0:T(8,128)(2,1)S(1)} %pad_maximum_fusion.7), channel_id=1, source_target_pairs={{0,2},{1,3},{2,0},{3,1},{4,6},{5,7},{6,4},{7,5},{8,10},{9,11},{10,... | collective-permute-start | bytes 147464 | tf_op jit(solution)/shard_map/ppermute | solution.py:490
  54.7 7.7 %collective-permute-start.12 = (bf16[4,64,128]{2,1,0:T(8,128)(2,1)S(1)}, bf16[4,64,128]{2,1,0:T(8,128)(2,1)S(1)}, u32[]{:S(2)}, u32[]{:S(2)}) collective-permute-start(bf16[4,64,128]{2,1,0:T(8,128)(2,1)S(1)} %pad_maximum_fusion.1.refs_5_), channel_id=1, source_target_pairs={{0,6},{1,7},{2,4},{3,5},{4,2},{5,3},{6,0},{7,1},{8,14},{9,15},{10,... | collective-permute-start | bytes 196616 | tf_op jit(solution)/shard_map/ppermute | solution.py:490
  54.8 14.2 %collective-permute-start.15 = (bf16[64,4096]{1,0:T(8,128)(2,1)S(1)}, bf16[64,4096]{1,0:T(8,128)(2,1)S(1)}, u32[]{:S(2)}, u32[]{:S(2)}) collective-permute-start(bf16[64,4096]{1,0:T(8,128)(2,1)S(1)} %copy-done.4), channel_id=1, source_target_pairs={{0,127},{1,2},{2,1},{3,4},{4,3},{5,6},{6,5},{7,8},{8,7},{9,10},{10... | collective-permute-start | bytes 1572872 | tf_op jit(solution)/shard_map/ppermute | solution.py:505
  55.9 13.2 %collective-permute-start.16 = (bf16[64,4096]{1,0:T(8,128)(2,1)S(1)}, bf16[64,4096]{1,0:T(8,128)(2,1)S(1)}, u32[]{:S(2)}, u32[]{:S(2)}) collective-permute-start(bf16[64,4096]{1,0:T(8,128)(2,1)S(1)} %copy-done.4), channel_id=1, source_target_pairs={{0,1},{1,0},{2,3},{3,2},{4,5},{5,4},{6,7},{7,6},{8,9},{9,8},{10,11... | collective-permute-start | bytes 1572872 | tf_op jit(solution)/shard_map/ppermute | solution.py:490
  62.5 13.0 %copy-start.11 = (bf16[3,3,64,64]{3,2,1,0:T(8,128)(2,1)S(1)}, bf16[3,3,64,64]{3,2,1,0:T(8,128)(2,1)}, u32[]{:S(2)}) copy-start(bf16[3,3,64,64]{3,2,1,0:T(8,128)(2,1)} %refs_10_.3) | copy-start | bytes 221188
  62.6 11.6 %collective-permute-start.14 = (bf16[3,64,128]{2,1,0:T(8,128)(2,1)S(1)}, bf16[3,64,128]{2,1,0:T(8,128)(2,1)S(1)}, u32[]{:S(2)}, u32[]{:S(2)}) collective-permute-start(bf16[3,64,128]{2,1,0:T(8,128)(2,1)S(1)} %fusion.1), channel_id=1, source_target_pairs={{0,8},{1,121},{2,10},{3,123},{4,12},{5,125},{6,14},{7,127},{8,0},{... | collective-permute-start | bytes 147464 | tf_op jit(solution)/shard_map/ppermute | solution.py:499
  74.1 1.3 %collective-permute-start.17 = (bf16[3,64,128]{2,1,0:T(8,128)(2,1)S(1)}, bf16[3,64,128]{2,1,0:T(8,128)(2,1)S(1)}, u32[]{:S(2)}, u32[]{:S(2)}) collective-permute-start(bf16[3,64,128]{2,1,0:T(8,128)(2,1)S(1)} %collective-permute-done.14.refs_7_), channel_id=1, source_target_pairs={{0,1},{1,0},{2,3},{3,2},{4,5},{5,4},{6,7},{7,6},{8,9},{9,8},{10,11... | collective-permute-start | bytes 147464 | tf_op jit(solution)/shard_map/ppermute | solution.py:490
  78.4 2.0 %collective-permute-start.18 = (f32[64,128]{1,0:T(8,128)S(1)}, f32[64,128]{1,0:T(8,128)S(1)}, u32[]{:S(2)}, u32[]{:S(2)}) collective-permute-start(f32[64,128]{1,0:T(8,128)S(1)} %get-tuple-element.59), channel_id=1, source_target_pairs={{0,1},{1,0},{2,3},{3,2},{4,5},{5,4},{6,7},{7,6},{8,9},{9,8},{10,11... | collective-permute-start | bytes 98312 | tf_op jit(solution)/shard_map/ppermute | solution.py:490
  80.5 4.0 %collective-permute-start.19 = (f32[64,128]{1,0:T(8,128)S(1)}, f32[64,128]{1,0:T(8,128)S(1)}, u32[]{:S(2)}, u32[]{:S(2)}) collective-permute-start(f32[64,128]{1,0:T(8,128)S(1)} %add.134), channel_id=1, source_target_pairs={{0,2},{1,3},{2,0},{3,1},{4,6},{5,7},{6,4},{7,5},{8,10},{9,11},{10,... | collective-permute-start | bytes 98312 | tf_op jit(solution)/shard_map/ppermute | solution.py:490
  84.5 5.1 %collective-permute-start.20 = (f32[64,128]{1,0:T(8,128)S(1)}, f32[64,128]{1,0:T(8,128)S(1)}, u32[]{:S(2)}, u32[]{:S(2)}) collective-permute-start(f32[64,128]{1,0:T(8,128)S(1)} %add.135), channel_id=1, source_target_pairs={{0,6},{1,7},{2,4},{3,5},{4,2},{5,3},{6,0},{7,1},{8,14},{9,15},{10,... | collective-permute-start | bytes 98312 | tf_op jit(solution)/shard_map/ppermute | solution.py:490
  89.6 3.9 %collective-permute-start.21 = (f32[64,128]{1,0:T(8,128)S(1)}, f32[64,128]{1,0:T(8,128)S(1)}, u32[]{:S(2)}, u32[]{:S(2)}) collective-permute-start(f32[64,128]{1,0:T(8,128)S(1)} %add.136), channel_id=1, source_target_pairs={{0,8},{1,9},{2,10},{3,11},{4,12},{5,13},{6,14},{7,15},{8,0},{9,1},... | collective-permute-start | bytes 98312 | tf_op jit(solution)/shard_map/ppermute | solution.py:490
  93.6 5.1 %collective-permute-start.22 = (f32[64,128]{1,0:T(8,128)S(1)}, f32[64,128]{1,0:T(8,128)S(1)}, u32[]{:S(2)}, u32[]{:S(2)}) collective-permute-start(f32[64,128]{1,0:T(8,128)S(1)} %add.137), channel_id=1, source_target_pairs={{0,24},{1,25},{2,26},{3,27},{4,28},{5,29},{6,30},{7,31},{8,16},{9,... | collective-permute-start | bytes 98312 | tf_op jit(solution)/shard_map/ppermute | solution.py:490
  (3 other events, 13.0 us)

commit v5 on v4

--- a/solution.py
+++ b/solution.py
@@ -281,7 +281,9 @@
         return total
 
     total = lax.fori_loop(0, work_ref.shape[0] // 8, step, jnp.zeros((LEAF, TILE), f32))
-    gram_ref[...] = total + swap_halves(total)
+    total = total + swap_halves(total)
+    half = LEAF // 2
+    gram_ref[...] = jnp.where(low_half((half, TILE)), total[:half], total[half:])
 
 
 def lane_take(tile, index):
@@ -445,7 +447,10 @@
 
 
 def group_kernel(gram_ref, work_ref, out_ref, own_ref, *, scale):
-    own_ref[0] = gram_ref[...] / scale
+    packed = gram_ref[...] / scale
+    other = swap_halves(packed)
+    low = low_half(packed.shape)
+    own_ref[0] = jnp.concatenate([jnp.where(low, packed, other), jnp.where(low, other, packed)], axis=0)
 
     def load(b):
         return own_ref[:, b * 8 : b * 8 + 8, :]
@@ -585,6 +590,9 @@
             compiler_params=params(56 if streamed else 6),
             name="interact",
         )(index, *rows, *bases, blocks)
+
+    def next_step(*args, **kwargs):
+        return pl.pallas_call(*args, **kwargs)
 
     row = struct((LEAF, width), bf16)
     payload = struct((3, LEAF, TILE), bf16)
@@ -625,14 +633,14 @@
         name="inner",
     )(scal, near_part, far_part, basis, transfer, mine, other, one, two, inner_tree, inner_links)
     middle_b, middle_a = node_halo(middle)
-    coords, pay = pl.pallas_call(
+    coords, pay = next_step(
         next_kernel,
         in_specs=[SMEM] + [VMEM] * 4,
         out_specs=(VMEM, VMEM),
         out_shape=(row, payload),
         compiler_params=params(6),
         name="next",
-    )(scal, outer_tree, after(middle, middle_a), outer_basis, outer_transfer)
+    )(scal, outer_tree, middle, outer_basis, outer_transfer)
     mine = coarse_near(pay, node)
     other = swap(mine, 6)
     near_part = interact(near_table, (middle_b, after(middle, mine), middle_a), outer_near)
@@ -648,7 +656,7 @@
         out_shape=(
             struct((LEAF, width), f32),
             struct((pairs // 2, LEAF, TILE), f32),
-            struct((LEAF, TILE), f32),
+            struct((LEAF // 2, TILE), f32),
         ),
         scratch_shapes=[pltpu.VMEM((LEAF, width), bf16)],
         compiler_params=params(6),

time: 103 us -> 101 us (0.981)
  waiting for transfers between devices: 41.3 us -> 39.3 us
    ppermute x17, waiting for transfers between devices: 27.4 us -> 25 us  [swap(): return lax.ppermute(x, AXES, [(i, i ^ mask) for i in range(count)])]
  transfers between devices with their start and end apart: 23 -> 23, of which waited for: 13 -> 12; matrix products, arithmetic and copies ran while one was open for 1% -> 1% of each run, Pallas kernels for 27% -> 28%
where the time goes in v5:
time: 101 us; the launch traced here: 100 us
  Pallas kernels  39.5 us (39%)
  waiting for transfers between devices  39.3 us (39%)
  starting transfers between devices  16 us (16%)
  local copies, waits for them, and re-layouts  3.46 us (3%)
  between operations  1.18 us (1%)
    ppermute x17, waiting for transfers between devices, swap(): return lax.ppermute(x, AXES, [(i, i ^ mask) for i in range(count)])  25 us
    pallas_call x4, Pallas kernels, interact(): pl.pallas_call(lambda *refs: interact_kernel(*refs, streamed=streamed), i...  16.2 us
    ppermute x4, waiting for transfers between devices, node_halo(): far = lax.ppermute(x, AXES, route)  14.3 us
    ppermute x4, starting transfers between devices, node_halo(): far = lax.ppermute(x, AXES, route)  12.6 us
    pallas_call x4, Pallas kernels, piece(): pl.pallas_call(lambda *refs: pair_kernel(*refs, first=2 * n, last=2 * n +...  6.79 us
    pallas_call x1, Pallas kernels, local(): pl.pallas_call(lambda *refs: group_kernel(*refs, scale=scale), in_specs=[...  4.36 us
    pallas_call x1, Pallas kernels, local(): pl.pallas_call(coords_kernel, in_specs=[SMEM, HBM, HBM, HBM, HBM], out_sp...  3.61 us
    unnamed x24, local copies, waits for them, and re-layouts  3.09 us
  transfers between devices with their start and end apart: 23, of which 12 were waited for; matrix products, arithmetic and copies ran while one was open for 1% of the time, Pallas kernels for 28%

profile of v5, /device:TPU:0, one launch (start us, length us, event | category | flops | bytes accessed | tf_op | source)
XLA Modules:
  0.0 100.4 jit_solution(13137971466568428828)
XLA Ops:
  0.6 8.3 %collective-permute-start.3 = (bf16[64,4096]{1,0:T(8,128)(2,1)}, bf16[64,4096]{1,0:T(8,128)(2,1)S(1)}, u32[]{:S(2)}, u32[]{:S(2)}) collective-permute-start(bf16[64,4096]{1,0:T(8,128)(2,1)} %probes_hbm.1), channel_id=1, source_target_pairs={{0,127},{1,2},{2,1},{3,4},{4,3},{5,6},{6,5},{7,8},{8,7},{9,10},{10... | collective-permute-start | bytes 1572872 | tf_op jit(solution)/shard_map/ppermute | solution.py:510
  8.9 0.8 copy-done.7
  9.8 3.6 %coords.1 = (bf16[64,4096]{1,0:T(8,128)(2,1)S(1)}, bf16[3,64,128]{2,1,0:T(8,128)(2,1)S(1)}, bf16[64,4096]{1,0:T(8,128)(2,1)S(1)}, bf16[64,4096]{1,0:T(8,128)(2,1)S(1)}, bf16[64,4096]{1,0:T(8,128)(2,1)}) custom-call(s32[1]{0:T(128)} %bitcast.scal_ref.refs_0_, bf16[2,2,64,64]{3,2,1,0:T(8,128)(2,1)S(1)} %copy-done.7, bf16[64,4096]{1,0:T(8,128)(2,1)} %probes_hbm.1, ...), custom_call_target="tpu_custom_call" | custom-call | tf_op jit(solution)/shard_map/coords/pallas_call | solution.py:602
  14.0 0.7 fusion.10
  15.4 3.6 %collective-permute-done.1 = bf16[3,64,128]{2,1,0:T(8,128)(2,1)S(1)} collective-permute-done((bf16[3,64,128]{2,1,0:T(8,128)(2,1)S(1)}, bf16[3,64,128]{2,1,0:T(8,128)(2,1)S(1)}, u32[]{:S(2)}, u32[]{:S(2)}) %collective-permute-start.1) | collective-permute-done | bytes 49184 | tf_op jit(solution)/shard_map/ppermute | solution.py:495
  19.2 1.9 %collective-permute-start.6 = (bf16[64,4096]{1,0:T(8,128)(2,1)S(1)}, bf16[64,4096]{1,0:T(8,128)(2,1)S(1)}, u32[]{:S(2)}, u32[]{:S(2)}) collective-permute-start(bf16[64,4096]{1,0:T(8,128)(2,1)S(1)} %get-tuple-element.44.refs_2_), channel_id=1, source_target_pairs={{0,127},{1,2},{2,1},{3,4},{4,3},{5,6},{6,5},{7,8},{8,7},{9,10},{10... | collective-permute-start | bytes 1572872 | tf_op jit(solution)/shard_map/ppermute | solution.py:510
  21.2 2.2 %copy-done = bf16[8,64,4096]{2,1,0:T(8,128)(2,1)S(1)} copy-done((bf16[8,64,4096]{2,1,0:T(8,128)(2,1)S(1)}, bf16[8,64,4096]{2,1,0:T(8,128)(2,1)}, u32[]{:S(2)}) %copy-start) | copy-done | bytes 4194328
  23.3 3.7 %interact.4.refs_1_ = f32[64,4096]{1,0:T(8,128)S(1)} custom-call(s32[512]{0:T(512)S(1)} %reshape.64.refs_0_, bf16[64,4096]{1,0:T(8,128)(2,1)S(1)} %collective-permute-done.3.refs_1_, bf16[64,4096]{1,0:T(8,128)(2,1)S(1)} %get-tuple-element.39.refs_2_, bf16[64,4096]{1,0:T(8,128)(2,1)S(1)} %collective-permute-done.4.refs_3_, bf16[8,64,4096]{2,1,0:T(8,128)(2,1)S(1)} %copy-done), custom_call_target="tpu_custom_call" | custom-call | tf_op jit(solution)/shard_map/interact/pallas_call | solution.py:584
  27.2 1.4 %collective-permute-start.5 = (bf16[3,64,128]{2,1,0:T(8,128)(2,1)S(1)}, bf16[3,64,128]{2,1,0:T(8,128)(2,1)S(1)}, u32[]{:S(2)}, u32[]{:S(2)}) collective-permute-start(bf16[3,64,128]{2,1,0:T(8,128)(2,1)S(1)} %fusion.4), channel_id=1, source_target_pairs={{0,8},{1,121},{2,10},{3,123},{4,12},{5,125},{6,14},{7,127},{8,0},{... | collective-permute-start | bytes 147464 | tf_op jit(solution)/shard_map/ppermute | solution.py:504
  28.6 4.7 %collective-permute-done.6.refs_1_ = bf16[64,4096]{1,0:T(8,128)(2,1)S(1)} collective-permute-done((bf16[64,4096]{1,0:T(8,128)(2,1)S(1)}, bf16[64,4096]{1,0:T(8,128)(2,1)S(1)}, u32[]{:S(2)}, u32[]{:S(2)}) %collective-permute-start.6) | collective-permute-done | bytes 524320 | tf_op jit(solution)/shard_map/ppermute | solution.py:510
  33.3 3.7 %interact.5.refs_2_ = f32[64,4096]{1,0:T(8,128)S(1)} custom-call(s32[512]{0:T(512)S(1)} %reshape.65.refs_0_, bf16[64,4096]{1,0:T(8,128)(2,1)S(1)} %collective-permute-done.6.refs_1_, bf16[64,4096]{1,0:T(8,128)(2,1)S(1)} %get-tuple-element.44.refs_2_, bf16[64,4096]{1,0:T(8,128)(2,1)S(1)} %collective-permute-done.7.refs_3_, bf16[8,64,4096]{2,1,0:T(8,128)(2,1)S(1)} %copy-done.1), custom_call_target="tpu_custom_call" | custom-call | tf_op jit(solution)/shard_map/interact/pallas_call | solution.py:584
  37.2 1.2 %collective-permute-done.8.refs_8_ = bf16[3,64,128]{2,1,0:T(8,128)(2,1)S(1)} collective-permute-done((bf16[3,64,128]{2,1,0:T(8,128)(2,1)S(1)}, bf16[3,64,128]{2,1,0:T(8,128)(2,1)S(1)}, u32[]{:S(2)}, u32[]{:S(2)}) %collective-permute-start.8) | collective-permute-done | bytes 49184 | tf_op jit(solution)/shard_map/ppermute | solution.py:495
  38.4 2.0 %inner.1.rows_ref.refs_2_ = bf16[64,4096]{1,0:T(8,128)(2,1)S(1)} custom-call(s32[1]{0:T(128)} %bitcast.scal_ref.refs_0_, f32[64,4096]{1,0:T(8,128)S(1)} %interact.4.refs_1_, f32[64,4096]{1,0:T(8,128)S(1)} %interact.5.refs_2_, bf16[64,4096]{1,0:T(8,128)(2,1)S(1)} %get-tuple-element.46.refs_3_, bf16[64,4096]{1,0:T(8,128)(2,1)S(1)} %copy-done.6, ...), custom_call_target="tpu_custom_call" | custom-call | tf_op jit(solution)/shard_map/inner/pallas_call | solution.py:626
  40.4 1.8 %next.1 = (bf16[64,4096]{1,0:T(8,128)(2,1)S(1)}, bf16[3,64,128]{2,1,0:T(8,128)(2,1)S(1)}) custom-call(s32[1]{0:T(128)} %bitcast.scal_ref.refs_0_, bf16[2,2,64,64]{3,2,1,0:T(8,128)(2,1)S(1)} %copy-done.9, bf16[64,4096]{1,0:T(8,128)(2,1)S(1)} %inner.1.rows_ref.refs_2_, bf16[64,4096]{1,0:T(8,128)(2,1)S(1)} %copy-done.4, bf16[64,4096]{1,0:T(8,128)(2,1)S(1)} %copy-done.5), custom_call_target="tpu_custom_call" | custom-call | tf_op jit(solution)/shard_map/next/pallas_call | solution.py:636
  42.5 1.8 %collective-permute-start.12 = (bf16[64,4096]{1,0:T(8,128)(2,1)S(1)}, bf16[64,4096]{1,0:T(8,128)(2,1)S(1)}, u32[]{:S(2)}, u32[]{:S(2)}) collective-permute-start(bf16[64,4096]{1,0:T(8,128)(2,1)S(1)} %inner.1.rows_ref.refs_2_), channel_id=1, source_target_pairs={{0,127},{1,2},{2,1},{3,4},{4,3},{5,6},{6,5},{7,8},{8,7},{9,10},{10... | collective-permute-start | bytes 1572872 | tf_op jit(solution)/shard_map/ppermute | solution.py:510
  44.6 8.1 %collective-permute-done.10 = bf16[3,64,128]{2,1,0:T(8,128)(2,1)S(1)} collective-permute-done((bf16[3,64,128]{2,1,0:T(8,128)(2,1)S(1)}, bf16[3,64,128]{2,1,0:T(8,128)(2,1)S(1)}, u32[]{:S(2)}, u32[]{:S(2)}) %collective-permute-start.10) | collective-permute-done | bytes 49184 | tf_op jit(solution)/shard_map/ppermute | solution.py:495
  53.4 3.5 %collective-permute-done.12.refs_1_ = bf16[64,4096]{1,0:T(8,128)(2,1)S(1)} collective-permute-done((bf16[64,4096]{1,0:T(8,128)(2,1)S(1)}, bf16[64,4096]{1,0:T(8,128)(2,1)S(1)}, u32[]{:S(2)}, u32[]{:S(2)}) %collective-permute-start.12) | collective-permute-done | bytes 524320 | tf_op jit(solution)/shard_map/ppermute | solution.py:510
  56.8 3.7 %interact.6.refs_1_ = f32[64,4096]{1,0:T(8,128)S(1)} custom-call(s32[512]{0:T(512)S(1)} %reshape.64.refs_0_, bf16[64,4096]{1,0:T(8,128)(2,1)S(1)} %collective-permute-done.12.refs_1_, bf16[64,4096]{1,0:T(8,128)(2,1)S(1)} %inner.1.rows_ref.refs_2_, bf16[64,4096]{1,0:T(8,128)(2,1)S(1)} %collective-permute-done.13.refs_3_, bf16[8,64,4096]{2,1,0:T(8,128)(2,1)S(1)} %copy-done.2), custom_call_target="tpu_custom_call" | custom-call | tf_op jit(solution)/shard_map/interact/pallas_call | solution.py:584
  61.0 6.1 %collective-permute-done.15.refs_4_ = bf16[64,4096]{1,0:T(8,128)(2,1)S(1)} collective-permute-done((bf16[64,4096]{1,0:T(8,128)(2,1)S(1)}, bf16[64,4096]{1,0:T(8,128)(2,1)S(1)}, u32[]{:S(2)}, u32[]{:S(2)}) %collective-permute-start.15) | collective-permute-done | bytes 524320 | tf_op jit(solution)/shard_map/ppermute | solution.py:510
  67.1 5.1 %interact.7.refs_2_ = f32[64,4096]{1,0:T(8,128)S(1)} custom-call(s32[512]{0:T(512)S(1)} %reshape.65.refs_0_, bf16[64,4096]{1,0:T(8,128)(2,1)S(1)} %collective-permute-done.12.refs_1_, bf16[64,4096]{1,0:T(8,128)(2,1)S(1)} %get-tuple-element.53.refs_2_, bf16[64,4096]{1,0:T(8,128)(2,1)S(1)} %collective-permute-done.13.refs_3_, ...), custom_call_target="tpu_custom_call" | custom-call | tf_op jit(solution)/shard_map/interact/pallas_call | solution.py:584
  72.3 1.2 %collective-permute-done.17.refs_8_ = bf16[3,64,128]{2,1,0:T(8,128)(2,1)S(1)} collective-permute-done((bf16[3,64,128]{2,1,0:T(8,128)(2,1)S(1)}, bf16[3,64,128]{2,1,0:T(8,128)(2,1)S(1)}, u32[]{:S(2)}, u32[]{:S(2)}) %collective-permute-start.17) | collective-permute-done | bytes 49184 | tf_op jit(solution)/shard_map/ppermute | solution.py:495
  73.5 3.0 %outer.1 = (f32[64,4096]{1,0:T(8,128)S(1)}, f32[16,64,128]{2,1,0:T(8,128)S(1)}, f32[32,128]{1,0:T(8,128)S(1)}) custom-call(s32[1]{0:T(128)} %bitcast.scal_ref.refs_0_, f32[64,4096]{1,0:T(8,128)S(1)} %interact.6.refs_1_, f32[64,4096]{1,0:T(8,128)S(1)} %interact.7.refs_2_, bf16[64,4096]{1,0:T(8,128)(2,1)S(1)} %copy-done.4, bf16[64,4096]{1,0:T(8,128)(2,1)S(1)} %copy-done.5, ...), custom_call_target="tpu_custom_call" | custom-call | tf_op jit(solution)/shard_map/outer/pallas_call | solution.py:652
  76.7 1.9 %pairs.4.refs_0_ = f32[16,64,128]{2,1,0:T(8,128)S(1)} custom-call(f32[16,64,128]{2,1,0:T(8,128)S(1)} %get-tuple-element.58.refs_0_), custom_call_target="tpu_custom_call", output_to_operand_aliasing={{}: (0, {})} | custom-call | tf_op jit(solution)/shard_map/pairs/pallas_call | solution.py:667
  78.6 1.8 %pairs.5.refs_0_ = f32[16,64,128]{2,1,0:T(8,128)S(1)} custom-call(f32[16,64,128]{2,1,0:T(8,128)S(1)} %pairs.4.refs_0_), custom_call_target="tpu_custom_call", output_to_operand_aliasing={{}: (0, {})} | custom-call | tf_op jit(solution)/shard_map/pairs/pallas_call | solution.py:667
  80.4 2.0 %collective-permute-done.19 = f32[32,128]{1,0:T(8,128)S(1)} collective-permute-done((f32[32,128]{1,0:T(8,128)S(1)}, f32[32,128]{1,0:T(8,128)S(1)}, u32[]{:S(2)}, u32[]{:S(2)}) %collective-permute-start.19) | collective-permute-done | bytes 16416 | tf_op jit(solution)/shard_map/ppermute | solution.py:495
  82.4 1.8 %pairs.6.refs_0_ = f32[16,64,128]{2,1,0:T(8,128)S(1)} custom-call(f32[16,64,128]{2,1,0:T(8,128)S(1)} %pairs.5.refs_0_), custom_call_target="tpu_custom_call", output_to_operand_aliasing={{}: (0, {})} | custom-call | tf_op jit(solution)/shard_map/pairs/pallas_call | solution.py:667
  84.1 3.2 %collective-permute-done.20 = f32[32,128]{1,0:T(8,128)S(1)} collective-permute-done((f32[32,128]{1,0:T(8,128)S(1)}, f32[32,128]{1,0:T(8,128)S(1)}, u32[]{:S(2)}, u32[]{:S(2)}) %collective-permute-start.20) | collective-permute-done | bytes 16416 | tf_op jit(solution)/shard_map/ppermute | solution.py:495
  87.3 1.4 %pairs.7.work_ref.refs_1_ = f32[16,64,128]{2,1,0:T(8,128)S(1)} custom-call(f32[16,64,128]{2,1,0:T(8,128)S(1)} %pairs.6.refs_0_), custom_call_target="tpu_custom_call", output_to_operand_aliasing={{}: (0, {})} | custom-call | tf_op jit(solution)/shard_map/pairs/pallas_call | solution.py:667
  88.7 2.3 %collective-permute-done.21 = f32[32,128]{1,0:T(8,128)S(1)} collective-permute-done((f32[32,128]{1,0:T(8,128)S(1)}, f32[32,128]{1,0:T(8,128)S(1)}, u32[]{:S(2)}, u32[]{:S(2)}) %collective-permute-start.21) | collective-permute-done | bytes 16416 | tf_op jit(solution)/shard_map/ppermute | solution.py:495
  91.1 1.7 %solve.1 = f32[64,4096]{1,0:T(8,128)} custom-call(f32[16,64,128]{2,1,0:T(8,128)S(1)} %pairs.7.work_ref.refs_1_, f32[64,4096]{1,0:T(8,128)S(1)} %get-tuple-element.66.samples_ref), custom_call_target="tpu_custom_call" | custom-call | tf_op jit(solution)/shard_map/solve/pallas_call | solution.py:684
  92.8 3.2 %collective-permute-done.22 = f32[32,128]{1,0:T(8,128)S(1)} collective-permute-done((f32[32,128]{1,0:T(8,128)S(1)}, f32[32,128]{1,0:T(8,128)S(1)}, u32[]{:S(2)}, u32[]{:S(2)}) %collective-permute-start.22) | collective-permute-done | bytes 16416 | tf_op jit(solution)/shard_map/ppermute | solution.py:495
  96.0 4.4 %group.1 = f32[64,2048]{1,0:T(8,128)} custom-call(f32[32,128]{1,0:T(8,128)S(1)} %add.138.refs_0_, f32[16,64,128]{2,1,0:T(8,128)S(1)} %pairs.7.work_ref.refs_1_), custom_call_target="tpu_custom_call" | custom-call | tf_op jit(solution)/shard_map/group/pallas_call | solution.py:694
  (83 shorter events, 3.3 us)
Async XLA Ops:
  0.6 20.5 %collective-permute-start.3 = (bf16[64,4096]{1,0:T(8,128)(2,1)}, bf16[64,4096]{1,0:T(8,128)(2,1)S(1)}, u32[]{:S(2)}, u32[]{:S(2)}) collective-permute-start(bf16[64,4096]{1,0:T(8,128)(2,1)} %probes_hbm.1), channel_id=1, source_target_pairs={{0,127},{1,2},{2,1},{3,4},{4,3},{5,6},{6,5},{7,8},{8,7},{9,10},{10... | collective-permute-start | bytes 1572872 | tf_op jit(solution)/shard_map/ppermute | solution.py:510
  8.9 12.2 %collective-permute-start.4 = (bf16[64,4096]{1,0:T(8,128)(2,1)}, bf16[64,4096]{1,0:T(8,128)(2,1)S(1)}, u32[]{:S(2)}, u32[]{:S(2)}) collective-permute-start(bf16[64,4096]{1,0:T(8,128)(2,1)} %probes_hbm.1), channel_id=1, source_target_pairs={{0,1},{1,0},{2,3},{3,2},{4,5},{5,4},{6,7},{7,6},{8,9},{9,8},{10,11... | collective-permute-start | bytes 1572872 | tf_op jit(solution)/shard_map/ppermute | solution.py:495
  13.4 1.5 %collective-permute-start = (bf16[3,64,128]{2,1,0:T(8,128)(2,1)S(1)}, bf16[3,64,128]{2,1,0:T(8,128)(2,1)S(1)}, u32[]{:S(2)}, u32[]{:S(2)}) collective-permute-start(bf16[3,64,128]{2,1,0:T(8,128)(2,1)S(1)} %get-tuple-element.35), channel_id=1, source_target_pairs={{0,1},{1,0},{2,3},{3,2},{4,5},{5,4},{6,7},{7,6},{8,9},{9,8},{10,11... | collective-permute-start | bytes 147464 | tf_op jit(solution)/shard_map/ppermute | solution.py:495
  14.9 4.2 %collective-permute-start.1 = (bf16[3,64,128]{2,1,0:T(8,128)(2,1)S(1)}, bf16[3,64,128]{2,1,0:T(8,128)(2,1)S(1)}, u32[]{:S(2)}, u32[]{:S(2)}) collective-permute-start(bf16[3,64,128]{2,1,0:T(8,128)(2,1)S(1)} %pad_maximum_fusion.6), channel_id=1, source_target_pairs={{0,2},{1,3},{2,0},{3,1},{4,6},{5,7},{6,4},{7,5},{8,10},{9,11},{10,... | collective-permute-start | bytes 147464 | tf_op jit(solution)/shard_map/ppermute | solution.py:495
  19.1 8.0 %collective-permute-start.2 = (bf16[4,64,128]{2,1,0:T(8,128)(2,1)S(1)}, bf16[4,64,128]{2,1,0:T(8,128)(2,1)S(1)}, u32[]{:S(2)}, u32[]{:S(2)}) collective-permute-start(bf16[4,64,128]{2,1,0:T(8,128)(2,1)S(1)} %pad_maximum_fusion.refs_5_), channel_id=1, source_target_pairs={{0,6},{1,7},{2,4},{3,5},{4,2},{5,3},{6,0},{7,1},{8,14},{9,15},{10,... | collective-permute-start | bytes 196616 | tf_op jit(solution)/shard_map/ppermute | solution.py:495
  19.2 14.1 %collective-permute-start.6 = (bf16[64,4096]{1,0:T(8,128)(2,1)S(1)}, bf16[64,4096]{1,0:T(8,128)(2,1)S(1)}, u32[]{:S(2)}, u32[]{:S(2)}) collective-permute-start(bf16[64,4096]{1,0:T(8,128)(2,1)S(1)} %get-tuple-element.44.refs_2_), channel_id=1, source_target_pairs={{0,127},{1,2},{2,1},{3,4},{4,3},{5,6},{6,5},{7,8},{8,7},{9,10},{10... | collective-permute-start | bytes 1572872 | tf_op jit(solution)/shard_map/ppermute | solution.py:510
  21.1 12.2 %collective-permute-start.7 = (bf16[64,4096]{1,0:T(8,128)(2,1)S(1)}, bf16[64,4096]{1,0:T(8,128)(2,1)S(1)}, u32[]{:S(2)}, u32[]{:S(2)}) collective-permute-start(bf16[64,4096]{1,0:T(8,128)(2,1)S(1)} %get-tuple-element.44.refs_2_), channel_id=1, source_target_pairs={{0,1},{1,0},{2,3},{3,2},{4,5},{5,4},{6,7},{7,6},{8,9},{9,8},{10,11... | collective-permute-start | bytes 1572872 | tf_op jit(solution)/shard_map/ppermute | solution.py:495
  27.1 11.3 %copy-start.6 = (bf16[64,4096]{1,0:T(8,128)(2,1)S(1)}, bf16[64,4096]{1,0:T(8,128)(2,1)}, u32[]{:S(2)}) copy-start(bf16[64,4096]{1,0:T(8,128)(2,1)} %get-tuple-element.47.refs_4_) | copy-start | bytes 1572868
  27.1 11.3 %copy-start.8 = (bf16[2,2,64,64]{3,2,1,0:T(8,128)(2,1)S(1)}, bf16[2,2,64,64]{3,2,1,0:T(8,128)(2,1)}, u32[]{:S(2)}) copy-start(bf16[2,2,64,64]{3,2,1,0:T(8,128)(2,1)} %refs_9_.2) | copy-start | bytes 98308
  27.1 11.3 %copy-start.10 = (bf16[3,3,64,64]{3,2,1,0:T(8,128)(2,1)S(1)}, bf16[3,3,64,64]{3,2,1,0:T(8,128)(2,1)}, u32[]{:S(2)}) copy-start(bf16[3,3,64,64]{3,2,1,0:T(8,128)(2,1)} %refs_10_.2) | copy-start | bytes 221188
  27.2 13.2 %copy-start.4 = (bf16[64,4096]{1,0:T(8,128)(2,1)S(1)}, bf16[64,4096]{1,0:T(8,128)(2,1)}, u32[]{:S(2)}) copy-start(bf16[64,4096]{1,0:T(8,128)(2,1)} %refs_3_.1) | copy-start | bytes 1572868
  27.2 13.2 %copy-start.5 = (bf16[64,4096]{1,0:T(8,128)(2,1)S(1)}, bf16[64,4096]{1,0:T(8,128)(2,1)}, u32[]{:S(2)}) copy-start(bf16[64,4096]{1,0:T(8,128)(2,1)} %refs_4_.7) | copy-start | bytes 1572868
  27.2 13.2 %copy-start.9 = (bf16[2,2,64,64]{3,2,1,0:T(8,128)(2,1)S(1)}, bf16[2,2,64,64]{3,2,1,0:T(8,128)(2,1)}, u32[]{:S(2)}) copy-start(bf16[2,2,64,64]{3,2,1,0:T(8,128)(2,1)} %refs_9_.3) | copy-start | bytes 98308
  27.2 9.8 %collective-permute-start.5 = (bf16[3,64,128]{2,1,0:T(8,128)(2,1)S(1)}, bf16[3,64,128]{2,1,0:T(8,128)(2,1)S(1)}, u32[]{:S(2)}, u32[]{:S(2)}) collective-permute-start(bf16[3,64,128]{2,1,0:T(8,128)(2,1)S(1)} %fusion.4), channel_id=1, source_target_pairs={{0,8},{1,121},{2,10},{3,123},{4,12},{5,125},{6,14},{7,127},{8,0},{... | collective-permute-start | bytes 147464 | tf_op jit(solution)/shard_map/ppermute | solution.py:504
  37.0 19.8 %copy-start.2 = (bf16[8,64,4096]{2,1,0:T(8,128)(2,1)S(1)}, bf16[8,64,4096]{2,1,0:T(8,128)(2,1)}, u32[]{:S(2)}) copy-start(bf16[8,64,4096]{2,1,0:T(8,128)(2,1)} %refs_4_.6) | copy-start | bytes 12582916
  37.1 1.3 %collective-permute-start.8 = (bf16[3,64,128]{2,1,0:T(8,128)(2,1)S(1)}, bf16[3,64,128]{2,1,0:T(8,128)(2,1)S(1)}, u32[]{:S(2)}, u32[]{:S(2)}) collective-permute-start(bf16[3,64,128]{2,1,0:T(8,128)(2,1)S(1)} %collective-permute-done.5.refs_7_), channel_id=1, source_target_pairs={{0,1},{1,0},{2,3},{3,2},{4,5},{5,4},{6,7},{7,6},{8,9},{9,8},{10,11... | collective-permute-start | bytes 147464 | tf_op jit(solution)/shard_map/ppermute | solution.py:495
  42.3 24.8 %copy-start.3 = (bf16[8,64,4096]{2,1,0:T(8,128)(2,1)S(1)}, bf16[8,64,4096]{2,1,0:T(8,128)(2,1)}, u32[]{:S(2)}) copy-start(bf16[8,64,4096]{2,1,0:T(8,128)(2,1)} %refs_6_.1) | copy-start | bytes 12582916
  42.3 2.1 %collective-permute-start.9 = (bf16[3,64,128]{2,1,0:T(8,128)(2,1)S(1)}, bf16[3,64,128]{2,1,0:T(8,128)(2,1)S(1)}, u32[]{:S(2)}, u32[]{:S(2)}) collective-permute-start(bf16[3,64,128]{2,1,0:T(8,128)(2,1)S(1)} %get-tuple-element.49), channel_id=1, source_target_pairs={{0,1},{1,0},{2,3},{3,2},{4,5},{5,4},{6,7},{7,6},{8,9},{9,8},{10,11... | collective-permute-start | bytes 147464 | tf_op jit(solution)/shard_map/ppermute | solution.py:495
  42.5 14.3 %collective-permute-start.12 = (bf16[64,4096]{1,0:T(8,128)(2,1)S(1)}, bf16[64,4096]{1,0:T(8,128)(2,1)S(1)}, u32[]{:S(2)}, u32[]{:S(2)}) collective-permute-start(bf16[64,4096]{1,0:T(8,128)(2,1)S(1)} %inner.1.rows_ref.refs_2_), channel_id=1, source_target_pairs={{0,127},{1,2},{2,1},{3,4},{4,3},{5,6},{6,5},{7,8},{8,7},{9,10},{10... | collective-permute-start | bytes 1572872 | tf_op jit(solution)/shard_map/ppermute | solution.py:510
  44.4 12.5 %collective-permute-start.13 = (bf16[64,4096]{1,0:T(8,128)(2,1)S(1)}, bf16[64,4096]{1,0:T(8,128)(2,1)S(1)}, u32[]{:S(2)}, u32[]{:S(2)}) collective-permute-start(bf16[64,4096]{1,0:T(8,128)(2,1)S(1)} %inner.1.rows_ref.refs_2_), channel_id=1, source_target_pairs={{0,1},{1,0},{2,3},{3,2},{4,5},{5,4},{6,7},{7,6},{8,9},{9,8},{10,11... | collective-permute-start | bytes 1572872 | tf_op jit(solution)/shard_map/ppermute | solution.py:495
  44.4 8.3 %collective-permute-start.10 = (bf16[3,64,128]{2,1,0:T(8,128)(2,1)S(1)}, bf16[3,64,128]{2,1,0:T(8,128)(2,1)S(1)}, u32[]{:S(2)}, u32[]{:S(2)}) collective-permute-start(bf16[3,64,128]{2,1,0:T(8,128)(2,1)S(1)} %pad_maximum_fusion.7), channel_id=1, source_target_pairs={{0,2},{1,3},{2,0},{3,1},{4,6},{5,7},{6,4},{7,5},{8,10},{9,11},{10,... | collective-permute-start | bytes 147464 | tf_op jit(solution)/shard_map/ppermute | solution.py:495
  52.7 7.8 %collective-permute-start.11 = (bf16[4,64,128]{2,1,0:T(8,128)(2,1)S(1)}, bf16[4,64,128]{2,1,0:T(8,128)(2,1)S(1)}, u32[]{:S(2)}, u32[]{:S(2)}) collective-permute-start(bf16[4,64,128]{2,1,0:T(8,128)(2,1)S(1)} %pad_maximum_fusion.1.refs_5_), channel_id=1, source_target_pairs={{0,6},{1,7},{2,4},{3,5},{4,2},{5,3},{6,0},{7,1},{8,14},{9,15},{10,... | collective-permute-start | bytes 196616 | tf_op jit(solution)/shard_map/ppermute | solution.py:495
  52.8 14.2 %collective-permute-start.15 = (bf16[64,4096]{1,0:T(8,128)(2,1)S(1)}, bf16[64,4096]{1,0:T(8,128)(2,1)S(1)}, u32[]{:S(2)}, u32[]{:S(2)}) collective-permute-start(bf16[64,4096]{1,0:T(8,128)(2,1)S(1)} %copy-done.4), channel_id=1, source_target_pairs={{0,127},{1,2},{2,1},{3,4},{4,3},{5,6},{6,5},{7,8},{8,7},{9,10},{10... | collective-permute-start | bytes 1572872 | tf_op jit(solution)/shard_map/ppermute | solution.py:510
  53.4 13.7 %collective-permute-start.16 = (bf16[64,4096]{1,0:T(8,128)(2,1)S(1)}, bf16[64,4096]{1,0:T(8,128)(2,1)S(1)}, u32[]{:S(2)}, u32[]{:S(2)}) collective-permute-start(bf16[64,4096]{1,0:T(8,128)(2,1)S(1)} %copy-done.4), channel_id=1, source_target_pairs={{0,1},{1,0},{2,3},{3,2},{4,5},{5,4},{6,7},{7,6},{8,9},{9,8},{10,11... | collective-permute-start | bytes 1572872 | tf_op jit(solution)/shard_map/ppermute | solution.py:495
  60.6 12.9 %copy-start.11 = (bf16[3,3,64,64]{3,2,1,0:T(8,128)(2,1)S(1)}, bf16[3,3,64,64]{3,2,1,0:T(8,128)(2,1)}, u32[]{:S(2)}) copy-start(bf16[3,3,64,64]{3,2,1,0:T(8,128)(2,1)} %refs_10_.3) | copy-start | bytes 221188
  60.7 11.5 %collective-permute-start.14 = (bf16[3,64,128]{2,1,0:T(8,128)(2,1)S(1)}, bf16[3,64,128]{2,1,0:T(8,128)(2,1)S(1)}, u32[]{:S(2)}, u32[]{:S(2)}) collective-permute-start(bf16[3,64,128]{2,1,0:T(8,128)(2,1)S(1)} %fusion.1), channel_id=1, source_target_pairs={{0,8},{1,121},{2,10},{3,123},{4,12},{5,125},{6,14},{7,127},{8,0},{... | collective-permute-start | bytes 147464 | tf_op jit(solution)/shard_map/ppermute | solution.py:504
  72.2 1.3 %collective-permute-start.17 = (bf16[3,64,128]{2,1,0:T(8,128)(2,1)S(1)}, bf16[3,64,128]{2,1,0:T(8,128)(2,1)S(1)}, u32[]{:S(2)}, u32[]{:S(2)}) collective-permute-start(bf16[3,64,128]{2,1,0:T(8,128)(2,1)S(1)} %collective-permute-done.14.refs_7_), channel_id=1, source_target_pairs={{0,1},{1,0},{2,3},{3,2},{4,5},{5,4},{6,7},{7,6},{8,9},{9,8},{10,11... | collective-permute-start | bytes 147464 | tf_op jit(solution)/shard_map/ppermute | solution.py:495
  76.5 2.0 %collective-permute-start.18 = (f32[32,128]{1,0:T(8,128)S(1)}, f32[32,128]{1,0:T(8,128)S(1)}, u32[]{:S(2)}, u32[]{:S(2)}) collective-permute-start(f32[32,128]{1,0:T(8,128)S(1)} %get-tuple-element.57), channel_id=1, source_target_pairs={{0,1},{1,0},{2,3},{3,2},{4,5},{5,4},{6,7},{7,6},{8,9},{9,8},{10,11... | collective-permute-start | bytes 49160 | tf_op jit(solution)/shard_map/ppermute | solution.py:495
  78.5 3.8 %collective-permute-start.19 = (f32[32,128]{1,0:T(8,128)S(1)}, f32[32,128]{1,0:T(8,128)S(1)}, u32[]{:S(2)}, u32[]{:S(2)}) collective-permute-start(f32[32,128]{1,0:T(8,128)S(1)} %add.134), channel_id=1, source_target_pairs={{0,2},{1,3},{2,0},{3,1},{4,6},{5,7},{6,4},{7,5},{8,10},{9,11},{10,... | collective-permute-start | bytes 49160 | tf_op jit(solution)/shard_map/ppermute | solution.py:495
  82.4 4.9 %collective-permute-start.20 = (f32[32,128]{1,0:T(8,128)S(1)}, f32[32,128]{1,0:T(8,128)S(1)}, u32[]{:S(2)}, u32[]{:S(2)}) collective-permute-start(f32[32,128]{1,0:T(8,128)S(1)} %add.135), channel_id=1, source_target_pairs={{0,6},{1,7},{2,4},{3,5},{4,2},{5,3},{6,0},{7,1},{8,14},{9,15},{10,... | collective-permute-start | bytes 49160 | tf_op jit(solution)/shard_map/ppermute | solution.py:495
  87.3 3.7 %collective-permute-start.21 = (f32[32,128]{1,0:T(8,128)S(1)}, f32[32,128]{1,0:T(8,128)S(1)}, u32[]{:S(2)}, u32[]{:S(2)}) collective-permute-start(f32[32,128]{1,0:T(8,128)S(1)} %add.136), channel_id=1, source_target_pairs={{0,8},{1,9},{2,10},{3,11},{4,12},{5,13},{6,14},{7,15},{8,0},{9,1},... | collective-permute-start | bytes 49160 | tf_op jit(solution)/shard_map/ppermute | solution.py:495
  91.1 4.9 %collective-permute-start.22 = (f32[32,128]{1,0:T(8,128)S(1)}, f32[32,128]{1,0:T(8,128)S(1)}, u32[]{:S(2)}, u32[]{:S(2)}) collective-permute-start(f32[32,128]{1,0:T(8,128)S(1)} %add.137), channel_id=1, source_target_pairs={{0,24},{1,25},{2,26},{3,27},{4,28},{5,29},{6,30},{7,31},{8,16},{9,... | collective-permute-start | bytes 49160 | tf_op jit(solution)/shard_map/ppermute | solution.py:495
  (3 other events, 13.0 us)
